TPU v7x, 512 devices: a whole 4x4x16 slice. The times are simulated.
512 devices in a mesh: front: 4 (over x), wide: 16 (over z), narrow: 8 (over y, core).
Axes of the slice: x: 4, y: 4, z: 16, core: 2. Of those that a mesh axis runs over, the one named last changes fastest.
Arguments:
- boundary: int32 [8, 32], P('front'), may hold values from 0 to 63, as said below
- owner: int32 [64], replicated, may hold values from 0 to 7, as said below
- ancestor_cov: bfloat16 [64, 128, 8192], P('narrow', None, 'wide'), may hold values from -1 to 3, as said below
- gain: bfloat16 [8, 4096, 2048], P('front', 'narrow', 'wide'), may hold values from -0.59765625 to 0.59765625
- pivot_inverse: float32 [8, 2048, 256], P('front', 'narrow', 'wide'), may hold values from -6 to 6
Outputs:
- boundary_cov: float32 [8, 2048, 4096], P('front', 'narrow', 'wide')
- diag_cov: float32 [8, 2048, 256], P('front', 'narrow', 'wide')
Inputs may be any that keep to these rules, and one draw needn't show every extreme that they name: `boundary`: each row lists 32 distinct ancestor blocks; for every w below 16, positions w * 2 to (w + 1) * 2 - 1 hold blocks from w * 4 to (w + 1) * 4 - 1; for every n below 8, positions n * 4 to (n + 1) * 4 - 1 hold at most 1 block of one owner. In every aligned group of 8 block rows each narrow index owns exactly one; every narrow index owns 8 block rows, and block row r sits in that owner's slot r // 8. `ancestor_cov`: the ancestors' covariance that it holds is symmetric.
All inputs are finite; a program needn't handle non-finite values.
Results may differ from a plain program's by a relative error of at most 0.014.
Values may be sent and summed in bfloat16 or wider, within the bound.
No kernel may reach another device: no remote copies, remote signals or barrier semaphores. Data moves between devices by JAX's collectives and lax.ppermute only.
A program may use at most 64 MiB of HBM per device.

v0:
```python
import jax
import jax.numpy as jnp
from jax import lax
from jax.experimental import pallas as pl
from jax.experimental.pallas import tpu as pltpu
from jax.sharding import Mesh
from jax.sharding import PartitionSpec as P

BLK = 128
NARROW = ("y", "core")
WHOLE = pl.BlockSpec(memory_space=pltpu.VMEM)


def pick_columns(bnd, pos, ancestor):
    def body(bnd_ref, pos_ref, a_ref, o_ref):
        o_ref[...] = a_ref[...]

    slots, rows, _ = ancestor.shape
    fronts = bnd.shape[0]
    return pl.pallas_call(
        body,
        out_shape=jax.ShapeDtypeStruct((slots, fronts, rows, 2 * BLK), ancestor.dtype),
        grid_spec=pltpu.PrefetchScalarGridSpec(
            num_scalar_prefetch=2,
            grid=(fronts, 2),
            in_specs=[
                pl.BlockSpec(
                    (slots, rows, BLK),
                    lambda m, j, b, p: (0, 0, b[m, 2 * p[0] + j] - 4 * p[0]),
                )
            ],
            out_specs=pl.BlockSpec((slots, None, rows, BLK), lambda m, j, b, p: (0, m, 0, j)),
        ),
        name="pick_columns",
    )(bnd, pos, ancestor)


def turned(bnd, owner, pos, own, other):
    _, fronts, rows, width = own.shape
    blocks = bnd.shape[1] // 8

    def body(bnd_ref, owner_ref, pos_ref, own_ref, other_ref, o_ref):
        n = pos_ref[1]
        for m in range(fronts):
            for c, (ref, at) in enumerate(((own_ref, n), (other_ref, n ^ 1))):
                for j in range(blocks):
                    source = owner_ref[bnd_ref[m, blocks * at + j]]
                    first = (c * blocks + j) * rows
                    o_ref[m, :, first : first + rows] = ref[source, m].T

    smem = pl.BlockSpec(memory_space=pltpu.SMEM)
    return pl.pallas_call(
        body,
        out_shape=jax.ShapeDtypeStruct((fronts, width, 2 * blocks * rows), own.dtype),
        in_specs=[smem, smem, smem, WHOLE, WHOLE],
        out_specs=WHOLE,
        name="turned",
    )(bnd, owner, pos, own, other)


def products(left, owns, others):
    fronts, rows, cols = owns[0].shape
    width = left.shape[1]
    count = len(owns)

    def body(left_ref, *refs):
        own, other, out = refs[:count], refs[count : 2 * count], refs[2 * count]
        for m in range(fronts):
            for first in range(0, count, 2):
                group = range(first, min(first + 2, count))
                near = jnp.concatenate([own[s][m] for s in group], axis=1)
                far = jnp.concatenate([other[s][m] for s in group], axis=1)
                value = jnp.dot(left_ref[m, :, :rows], near, preferred_element_type=jnp.float32)
                value += jnp.dot(left_ref[m, :, rows:], far, preferred_element_type=jnp.float32)
                for at, s in enumerate(group):
                    out[s, m] = value[:, at * cols : (at + 1) * cols].astype(jnp.bfloat16)

    flops = 4 * count * fronts * rows * cols * width
    return pl.pallas_call(
        body,
        out_shape=jax.ShapeDtypeStruct((count, fronts, width, cols), jnp.bfloat16),
        in_specs=[WHOLE] * (1 + 2 * count),
        out_specs=WHOLE,
        cost_estimate=pl.CostEstimate(
            flops=flops, transcendentals=0, bytes_accessed=4 * count * fronts * rows * cols * 2
        ),
        name="products",
    )(left, *owns, *others)


def assemble(pos, mine, theirs):
    shape = mine[0].shape[1:]

    def body(pos_ref, *refs):
        out = refs[-1]
        w, core = pos_ref[0], pos_ref[2]
        for from_core, parts in ((core, refs[: len(mine)]), (1 - core, refs[len(mine) : -1])):
            step = 0
            for ref in parts:
                for s in range(ref.shape[0]):
                    to = (w + (2 * from_core - 1) * step) & 15
                    wanted = ((to >> 1) & 1) == core
                    if step == 0:
                        wanted = jnp.logical_and(wanted, from_core == 0)
                    if step == 8:
                        wanted = jnp.logical_and(wanted, from_core == 1)

                    @pl.when(wanted)
                    def _():
                        out[2 * (to >> 2) + (to & 1)] = ref[s]

                    step += 1

    return pl.pallas_call(
        body,
        out_shape=jax.ShapeDtypeStruct((8, *shape), jnp.bfloat16),
        in_specs=[pl.BlockSpec(memory_space=pltpu.SMEM)] + [WHOLE] * (len(mine) + len(theirs)),
        out_specs=WHOLE,
        name="assemble",
    )(pos, *mine, *theirs)


def finish(pos, arrived, pieces):
    peers, halves, fronts, rows, cols = arrived.shape
    count = len(pieces)

    def body(pos_ref, a_ref, *refs):
        gs, (x_ref, d_ref, low_ref) = refs[:count], refs[count:]
        w, n = pos_ref[0], pos_ref[1]
        for m in range(fronts):
            for h in range(halves):
                total = a_ref[0, h, m].astype(jnp.float32)
                for s in range(1, peers):
                    total = total + a_ref[s, h, m].astype(jnp.float32)
                cross = -total
                x_ref[m, h * cols : (h + 1) * cols, :] = cross.T
                low_ref[m, :, h * cols : (h + 1) * cols] = cross.astype(jnp.bfloat16)
        for at, g_ref in enumerate(gs):
            step = at + 1
            down = (w - step % 8) & 15
            up = (w + step) & 15
            first = (down >> 1) == n
            half = jnp.where(first, down & 1, up & 1)

            @pl.when(jnp.logical_or(first, (up >> 1) == n))
            def _():
                for m in range(fronts):
                    site = jnp.dot(g_ref[m].T, low_ref[m], preferred_element_type=jnp.float32)
                    d_ref[pl.ds(half * 8, 8), m] = site.astype(jnp.bfloat16).reshape(8, 16, halves * cols)

    return pl.pallas_call(
        body,
        out_shape=(
            jax.ShapeDtypeStruct((fronts, halves * cols, rows), jnp.float32),
            jax.ShapeDtypeStruct((16, fronts, 16, halves * cols), jnp.bfloat16),
        ),
        in_specs=[pl.BlockSpec(memory_space=pltpu.SMEM)] + [WHOLE] * (1 + count),
        out_specs=(WHOLE, WHOLE),
        scratch_shapes=[pltpu.VMEM((fronts, rows, halves * cols), jnp.bfloat16)],
        name="finish",
    )(pos, arrived, *pieces)


def ring_pairs(cores):
    pairs = []
    for i in range(16):
        if 0 in cores:
            pairs.append((2 * i, 2 * ((i + 1) % 16)))
        if 1 in cores:
            pairs.append((2 * i + 1, 2 * ((i - 1) % 16) + 1))
    return pairs


def piece_pairs(step):
    pairs = []
    for i in range(16):
        down, up = (i - step % 8) % 16, (i + step) % 16
        pairs.append((8 * i + 2 * (i // 4), 8 * i + down // 2))
        pairs.append((8 * i + 2 * (i // 4) + 1, 8 * i + up // 2))
    return pairs


def level(boundary, owner, ancestor_cov, gain, pivot_inverse):
    w = lax.axis_index("wide")
    core = lax.axis_index("core")
    narrow = lax.axis_index("y") * 2 + core
    pos = jnp.stack([w, narrow, core]).astype(jnp.int32)
    swap = [(0, 1), (1, 0)]
    early = 6

    owns = [gain]
    others = [lax.ppermute(gain, "core", swap)]
    rows = gain.shape[1] // 2
    near = (w >> 1) & 1 == core
    pieces = []
    for step in range(1, 9):
        pairs = ring_pairs((0, 1) if step < 8 else (1,))
        owns.append(lax.ppermute(owns[-1], ("wide", "core"), pairs))
        others.append(lax.ppermute(others[-1], ("wide", "core"), pairs))
        a, b = owns[step], others[step]
        if step == 8:
            a = jnp.where(core == 0, owns[0], a)
            b = jnp.where(core == 0, others[0], b)
        held = jnp.where(near, a, b)
        piece = lax.dynamic_slice_in_dim(held, (w & 1) * rows, rows, 1)
        pieces.append(lax.ppermute(piece, ("wide", "y", "core"), piece_pairs(step)))
        if step == 1:
            picked = pick_columns(boundary, pos, ancestor_cov)
            arrived = lax.all_to_all(picked, NARROW, split_axis=0, concat_axis=0, tiled=True)
            paired = lax.ppermute(arrived, "core", swap)
            left = turned(boundary, owner, pos, arrived, paired)

    mine = [products(left, owns[:early], others[:early])]
    theirs = [lax.ppermute(mine[0], "core", swap)]
    mine.append(products(left, owns[early:], others[early:]))
    theirs.append(lax.ppermute(mine[1], "core", swap))
    ready = assemble(pos, mine, theirs)
    ready = ready.reshape(4, 2, *ready.shape[1:])
    parts = lax.all_to_all(ready, "y", split_axis=0, concat_axis=0, tiled=True)

    boundary_cov, site = finish(pos, parts, pieces)
    sums = lax.all_to_all(site, "wide", split_axis=0, concat_axis=0, tiled=True)
    reduced = jnp.sum(sums.astype(jnp.float32), axis=0)
    diag_cov = pivot_inverse - jnp.swapaxes(reduced, 1, 2)
    return boundary_cov, diag_cov


def solution(mesh):
    fine = Mesh(mesh.devices.reshape(4, 16, 4, 2), ("front", "wide", "y", "core"))
    placed = (
        P("front", None),
        P(),
        P(NARROW, None, "wide"),
        P("front", NARROW, "wide"),
        P("front", NARROW, "wide"),
    )
    return jax.shard_map(
        level,
        mesh=fine,
        in_specs=placed,
        out_specs=(P("front", NARROW, "wide"), P("front", NARROW, "wide")),
        check_vma=False,
    )
```

profile of v0, /device:TPU:4, one launch (start us, length us, event | category | flops | bytes accessed | tf_op | source)
XLA Modules:
  0.0 179.8 jit_solution(1084218137780409888)
XLA Ops:
  1.3 4.2 %pick_columns.1 = bf16[8,2,128,256]{3,2,1,0:T(8,128)(2,1)} custom-call(s32[2,32]{1,0:T(2,128)} %bnd_ref.3, s32[3]{0:T(128)} %pad_add_fusion.pos_ref, bf16[8,128,512]{2,1,0:T(8,128)(2,1)} %a_ref.1), custom_call_target="tpu_custom_call" | custom-call | tf_op jit(solution)/shard_map/pick_columns/pallas_call | solution.py:20
  5.5 4.6 %all-to-all-start = ((bf16[8,2,128,256]{3,2,1,0:T(8,128)(2,1)}), bf16[8,2,128,256]{3,2,1,0:T(8,128)(2,1)S(1)}, u32[]{:S(2)}, u32[]{:S(2)}) async-start(bf16[8,2,128,256]{3,2,1,0:T(8,128)(2,1)} %pick_columns.1), calls=%async_computation | async-start | bytes 2097152 | tf_op jit(solution)/shard_map/all_to_all | solution.py:209
  10.1 2.4 %collective-permute-start.6 = (bf16[2,512,128]{2,1,0:T(8,128)(2,1)S(1)}, bf16[2,512,128]{2,1,0:T(8,128)(2,1)S(1)}, u32[]{:S(2)}, u32[]{:S(2)}) collective-permute-start(bf16[2,512,128]{2,1,0:T(8,128)(2,1)S(1)} %copy-done.22), channel_id=1, source_target_pairs={{0,1},{1,0},{2,3},{3,2},{4,5},{5,4},{6,7},{7,6},{8,9},{9,8},{10,11... | collective-permute-start | bytes 786440 | tf_op jit(solution)/shard_map/ppermute | solution.py:192
  12.5 3.8 %collective-permute-start.1 = (bf16[2,512,128]{2,1,0:T(8,128)(2,1)S(1)}, bf16[2,512,128]{2,1,0:T(8,128)(2,1)S(1)}, u32[]{:S(2)}, u32[]{:S(2)}) collective-permute-start(bf16[2,512,128]{2,1,0:T(8,128)(2,1)S(1)} %copy-done.22), channel_id=1, source_target_pairs={{0,8},{1,121},{8,16},{9,1},{16,24},{17,9},{24,32},{25,17},{32,40},... | collective-permute-start | bytes 786440 | tf_op jit(solution)/shard_map/ppermute | solution.py:198
  16.2 3.8 %collective-permute-start.7 = (bf16[2,512,128]{2,1,0:T(8,128)(2,1)S(1)}, bf16[2,512,128]{2,1,0:T(8,128)(2,1)S(1)}, u32[]{:S(2)}, u32[]{:S(2)}) collective-permute-start(bf16[2,512,128]{2,1,0:T(8,128)(2,1)S(1)} %collective-permute-done.6.refs_6_), channel_id=1, source_target_pairs={{0,8},{1,121},{8,16},{9,1},{16,24},{17,9},{24,32},{25,17},{32,40},... | collective-permute-start | bytes 786440 | tf_op jit(solution)/shard_map/ppermute | solution.py:199
  20.1 8.1 %collective-permute-done.1.refs_1_ = bf16[2,512,128]{2,1,0:T(8,128)(2,1)S(1)} collective-permute-done((bf16[2,512,128]{2,1,0:T(8,128)(2,1)S(1)}, bf16[2,512,128]{2,1,0:T(8,128)(2,1)S(1)}, u32[]{:S(2)}, u32[]{:S(2)}) %collective-permute-start.1) | collective-permute-done | bytes 262176 | tf_op jit(solution)/shard_map/ppermute | solution.py:198
  28.1 1.9 %collective-permute-start.2 = (bf16[2,512,128]{2,1,0:T(8,128)(2,1)S(1)}, bf16[2,512,128]{2,1,0:T(8,128)(2,1)S(1)}, u32[]{:S(2)}, u32[]{:S(2)}) collective-permute-start(bf16[2,512,128]{2,1,0:T(8,128)(2,1)S(1)} %collective-permute-done.1.refs_1_), channel_id=1, source_target_pairs={{0,8},{1,121},{8,16},{9,1},{16,24},{17,9},{24,32},{25,17},{32,40},... | collective-permute-start | bytes 786440 | tf_op jit(solution)/shard_map/ppermute | solution.py:198
  31.0 1.9 %collective-permute-start.8 = (bf16[2,512,128]{2,1,0:T(8,128)(2,1)S(1)}, bf16[2,512,128]{2,1,0:T(8,128)(2,1)}, u32[]{:S(2)}, u32[]{:S(2)}) collective-permute-start(bf16[2,512,128]{2,1,0:T(8,128)(2,1)S(1)} %collective-permute-done.7.refs_7_), channel_id=1, source_target_pairs={{0,8},{1,121},{8,16},{9,1},{16,24},{17,9},{24,32},{25,17},{32,40},... | collective-permute-start | bytes 786440 | tf_op jit(solution)/shard_map/ppermute | solution.py:199
  32.9 4.7 %collective-permute-done.2.refs_2_ = bf16[2,512,128]{2,1,0:T(8,128)(2,1)S(1)} collective-permute-done((bf16[2,512,128]{2,1,0:T(8,128)(2,1)S(1)}, bf16[2,512,128]{2,1,0:T(8,128)(2,1)S(1)}, u32[]{:S(2)}, u32[]{:S(2)}) %collective-permute-start.2) | collective-permute-done | bytes 262176 | tf_op jit(solution)/shard_map/ppermute | solution.py:198
  42.5 2.9 %collective-permute-start = (bf16[8,2,128,256]{3,2,1,0:T(8,128)(2,1)S(1)}, bf16[8,2,128,256]{3,2,1,0:T(8,128)(2,1)S(1)}, u32[]{:S(2)}, u32[]{:S(2)}) collective-permute-start(bf16[8,2,128,256]{3,2,1,0:T(8,128)(2,1)S(1)} %all-to-all-done.own_ref), channel_id=1, source_target_pairs={{0,1},{1,0},{2,3},{3,2},{4,5},{5,4},{6,7},{7,6},{8,9},{9,8},{10,11... | collective-permute-start | bytes 3145736 | tf_op jit(solution)/shard_map/ppermute | solution.py:210
  47.1 1.9 %collective-permute-start.4 = (bf16[2,512,128]{2,1,0:T(8,128)(2,1)S(1)}, bf16[2,512,128]{2,1,0:T(8,128)(2,1)S(1)}, u32[]{:S(2)}, u32[]{:S(2)}) collective-permute-start(bf16[2,512,128]{2,1,0:T(8,128)(2,1)S(1)} %collective-permute-done.3.refs_3_), channel_id=1, source_target_pairs={{0,8},{1,121},{8,16},{9,1},{16,24},{17,9},{24,32},{25,17},{32,40},... | collective-permute-start | bytes 786440 | tf_op jit(solution)/shard_map/ppermute | solution.py:198
  50.2 1.9 %collective-permute-start.10 = (bf16[2,512,128]{2,1,0:T(8,128)(2,1)S(1)}, bf16[2,512,128]{2,1,0:T(8,128)(2,1)S(1)}, u32[]{:S(2)}, u32[]{:S(2)}) collective-permute-start(bf16[2,512,128]{2,1,0:T(8,128)(2,1)S(1)} %collective-permute-done.9.refs_9_), channel_id=1, source_target_pairs={{0,8},{1,121},{8,16},{9,1},{16,24},{17,9},{24,32},{25,17},{32,40},... | collective-permute-start | bytes 786440 | tf_op jit(solution)/shard_map/ppermute | solution.py:199
  52.1 4.4 %collective-permute-done.4.refs_4_ = bf16[2,512,128]{2,1,0:T(8,128)(2,1)S(1)} collective-permute-done((bf16[2,512,128]{2,1,0:T(8,128)(2,1)S(1)}, bf16[2,512,128]{2,1,0:T(8,128)(2,1)S(1)}, u32[]{:S(2)}, u32[]{:S(2)}) %collective-permute-start.4) | collective-permute-done | bytes 262176 | tf_op jit(solution)/shard_map/ppermute | solution.py:198
  61.6 4.4 %collective-permute-done.5.refs_5_ = bf16[2,512,128]{2,1,0:T(8,128)(2,1)S(1)} collective-permute-done((bf16[2,512,128]{2,1,0:T(8,128)(2,1)S(1)}, bf16[2,512,128]{2,1,0:T(8,128)(2,1)S(1)}, u32[]{:S(2)}, u32[]{:S(2)}) %collective-permute-start.5) | collective-permute-done | bytes 262176 | tf_op jit(solution)/shard_map/ppermute | solution.py:198
  66.0 1.9 %collective-permute-start.12 = (bf16[2,512,128]{2,1,0:T(8,128)(2,1)S(1)}, bf16[2,512,128]{2,1,0:T(8,128)(2,1)}, u32[]{:S(2)}, u32[]{:S(2)}) collective-permute-start(bf16[2,512,128]{2,1,0:T(8,128)(2,1)S(1)} %collective-permute-done.5.refs_5_), channel_id=1, source_target_pairs={{0,8},{1,121},{8,16},{9,1},{16,24},{17,9},{24,32},{25,17},{32,40},... | collective-permute-start | bytes 786440 | tf_op jit(solution)/shard_map/ppermute | solution.py:198
  69.1 1.9 %collective-permute-start.15 = (bf16[2,512,128]{2,1,0:T(8,128)(2,1)S(1)}, bf16[2,512,128]{2,1,0:T(8,128)(2,1)}, u32[]{:S(2)}, u32[]{:S(2)}) collective-permute-start(bf16[2,512,128]{2,1,0:T(8,128)(2,1)S(1)} %collective-permute-done.11.refs_11_), channel_id=1, source_target_pairs={{0,8},{1,121},{8,16},{9,1},{16,24},{17,9},{24,32},{25,17},{32,40},... | collective-permute-start | bytes 786440 | tf_op jit(solution)/shard_map/ppermute | solution.py:199
  71.1 4.5 %collective-permute-done.12.refs_0_ = bf16[2,512,128]{2,1,0:T(8,128)(2,1)} collective-permute-done((bf16[2,512,128]{2,1,0:T(8,128)(2,1)S(1)}, bf16[2,512,128]{2,1,0:T(8,128)(2,1)}, u32[]{:S(2)}, u32[]{:S(2)}) %collective-permute-start.12) | collective-permute-done | bytes 262176 | tf_op jit(solution)/shard_map/ppermute | solution.py:198
  75.6 1.9 %collective-permute-start.13 = (bf16[2,512,128]{2,1,0:T(8,128)(2,1)}, bf16[2,512,128]{2,1,0:T(8,128)(2,1)}, u32[]{:S(2)}, u32[]{:S(2)}) collective-permute-start(bf16[2,512,128]{2,1,0:T(8,128)(2,1)} %collective-permute-done.12.refs_0_), channel_id=1, source_target_pairs={{0,8},{1,121},{8,16},{9,1},{16,24},{17,9},{24,32},{25,17},{32,40},... | collective-permute-start | bytes 786440 | tf_op jit(solution)/shard_map/ppermute | solution.py:198
  78.7 1.9 %collective-permute-start.16 = (bf16[2,512,128]{2,1,0:T(8,128)(2,1)}, bf16[2,512,128]{2,1,0:T(8,128)(2,1)}, u32[]{:S(2)}, u32[]{:S(2)}) collective-permute-start(bf16[2,512,128]{2,1,0:T(8,128)(2,1)} %collective-permute-done.15.refs_3_), channel_id=1, source_target_pairs={{0,8},{1,121},{8,16},{9,1},{16,24},{17,9},{24,32},{25,17},{32,40},... | collective-permute-start | bytes 786440 | tf_op jit(solution)/shard_map/ppermute | solution.py:199
  81.7 2.9 %turned.1.left_ref = bf16[2,256,1024]{2,1,0:T(8,128)(2,1)} custom-call(s32[2,32]{1,0:T(2,128)} %bnd_ref.3, s32[64]{0:T(128)} %owner_ref.1, s32[3]{0:T(128)} %pad_add_fusion.pos_ref, bf16[8,2,128,256]{3,2,1,0:T(8,128)(2,1)} %copy-done.1, bf16[8,2,128,256]{3,2,1,0:T(8,128)(2,1)} %copy-done.2), custom_call_target="tpu_custom_call" | custom-call | tf_op jit(solution)/shard_map/turned/pallas_call | solution.py:52
  84.7 4.0 %products.2.refs_0_ = bf16[6,2,256,128]{3,2,1,0:T(8,128)(2,1)} custom-call(bf16[2,256,1024]{2,1,0:T(8,128)(2,1)} %turned.1.left_ref, bf16[2,512,128]{2,1,0:T(8,128)(2,1)} %refs_0_.1, bf16[2,512,128]{2,1,0:T(8,128)(2,1)} %copy-done.6, bf16[2,512,128]{2,1,0:T(8,128)(2,1)} %copy-done.12, bf16[2,512,128]{2,1,0:T(8,128)(2,1)} %copy-done.4, ...), custom_call_target="tpu_custom_call" | custom-call | flops 805306368 | bytes 6291456 | tf_op jit(solution)/shard_map/products/pallas_call | solution.py:79
  88.7 2.0 %collective-permute-start.18 = (bf16[6,2,256,128]{3,2,1,0:T(8,128)(2,1)}, bf16[6,2,256,128]{3,2,1,0:T(8,128)(2,1)S(1)}, u32[]{:S(2)}, u32[]{:S(2)}) collective-permute-start(bf16[6,2,256,128]{3,2,1,0:T(8,128)(2,1)} %products.2.refs_0_), channel_id=1, source_target_pairs={{0,1},{1,0},{2,3},{3,2},{4,5},{5,4},{6,7},{7,6},{8,9},{9,8},{10,11... | collective-permute-start | bytes 2359304 | tf_op jit(solution)/shard_map/ppermute | solution.py:214
  93.5 3.1 %products.3.refs_1_ = bf16[3,2,256,128]{3,2,1,0:T(8,128)(2,1)} custom-call(bf16[2,256,1024]{2,1,0:T(8,128)(2,1)} %turned.1.left_ref, bf16[2,512,128]{2,1,0:T(8,128)(2,1)} %collective-permute-done.12.refs_0_, bf16[2,512,128]{2,1,0:T(8,128)(2,1)} %collective-permute-done.13.refs_1_, bf16[2,512,128]{2,1,0:T(8,128)(2,1)} %copy-done.26, ...), custom_call_target="tpu_custom_call" | custom-call | flops 402653184 | bytes 3145728 | tf_op jit(solution)/shard_map/products/pallas_call | solution.py:79
  96.7 12.6 %collective-permute-start.19 = (bf16[3,2,256,128]{3,2,1,0:T(8,128)(2,1)}, bf16[3,2,256,128]{3,2,1,0:T(8,128)(2,1)S(1)}, u32[]{:S(2)}, u32[]{:S(2)}) collective-permute-start(bf16[3,2,256,128]{3,2,1,0:T(8,128)(2,1)} %products.3.refs_1_), channel_id=1, source_target_pairs={{0,1},{1,0},{2,3},{3,2},{4,5},{5,4},{6,7},{7,6},{8,9},{9,8},{10,11... | collective-permute-start | bytes 1179656 | tf_op jit(solution)/shard_map/ppermute | solution.py:216
  109.4 4.4 %collective-permute-start.20 = (bf16[2,256,128]{2,1,0:T(8,128)(2,1)S(1)}, bf16[2,256,128]{2,1,0:T(8,128)(2,1)S(1)}, u32[]{:S(2)}, u32[]{:S(2)}) collective-permute-start(bf16[2,256,128]{2,1,0:T(8,128)(2,1)S(1)} %dynamic-slice_select_fusion.8), channel_id=1, source_target_pairs={{0,7},{1,0},{8,8},{9,9},{16,16},{17,17},{24,25},{25,26},{34,33},{3... | collective-permute-start | bytes 393224 | tf_op jit(solution)/shard_map/ppermute | solution.py:206
  117.7 2.8 %assemble.1 = bf16[8,2,256,128]{3,2,1,0:T(8,128)(2,1)} custom-call(s32[3]{0:T(128)} %pad_add_fusion.pos_ref, bf16[6,2,256,128]{3,2,1,0:T(8,128)(2,1)} %products.2.refs_0_, bf16[3,2,256,128]{3,2,1,0:T(8,128)(2,1)} %products.3.refs_1_, bf16[6,2,256,128]{3,2,1,0:T(8,128)(2,1)} %copy-done.3, bf16[3,2,256,128]{3,2,1,0:T(8,128)(2,1)} %copy-done.30), custom_call_target="tpu_custom_call" | custom-call | tf_op jit(solution)/shard_map/assemble/pallas_call | solution.py:114
  120.5 3.7 %all-to-all-start.1 = ((bf16[4,2,2,256,128]{4,3,2,1,0:T(8,128)(2,1)}), bf16[4,2,2,256,128]{4,3,2,1,0:T(8,128)(2,1)S(1)}, u32[]{:S(2)}, u32[]{:S(2)}) async-start(bf16[4,2,2,256,128]{4,3,2,1,0:T(8,128)(2,1)} %bitcast.6), calls=%async_computation.1 | async-start | bytes 2097152 | tf_op jit(solution)/shard_map/all_to_all | solution.py:219
  124.3 5.2 %collective-permute-start.22 = (bf16[2,256,128]{2,1,0:T(8,128)(2,1)S(1)}, bf16[2,256,128]{2,1,0:T(8,128)(2,1)S(1)}, u32[]{:S(2)}, u32[]{:S(2)}) collective-permute-start(bf16[2,256,128]{2,1,0:T(8,128)(2,1)S(1)} %dynamic-slice_select_fusion.6), channel_id=1, source_target_pairs={{0,6},{1,1},{8,15},{9,10},{16,23},{17,18},{24,24},{25,27},{34,32},... | collective-permute-start | bytes 393224 | tf_op jit(solution)/shard_map/ppermute | solution.py:206
  139.5 2.8 %collective-permute-done.25.refs_5_ = bf16[2,256,128]{2,1,0:T(8,128)(2,1)S(1)} collective-permute-done((bf16[2,256,128]{2,1,0:T(8,128)(2,1)S(1)}, bf16[2,256,128]{2,1,0:T(8,128)(2,1)S(1)}, u32[]{:S(2)}, u32[]{:S(2)}) %collective-permute-start.25) | collective-permute-done | bytes 131104 | tf_op jit(solution)/shard_map/ppermute | solution.py:206
  142.3 2.4 %collective-permute-done.26.refs_6_ = bf16[2,256,128]{2,1,0:T(8,128)(2,1)S(1)} collective-permute-done((bf16[2,256,128]{2,1,0:T(8,128)(2,1)S(1)}, bf16[2,256,128]{2,1,0:T(8,128)(2,1)S(1)}, u32[]{:S(2)}, u32[]{:S(2)}) %collective-permute-start.26) | collective-permute-done | bytes 131104 | tf_op jit(solution)/shard_map/ppermute | solution.py:206
  146.3 3.2 %finish.1 = (f32[2,256,256]{2,1,0:T(8,128)}, bf16[16,2,16,256]{3,2,1,0:T(8,128)(2,1)}) custom-call(s32[3]{0:T(128)} %pad_add_fusion.pos_ref, bf16[4,2,2,256,128]{4,3,2,1,0:T(8,128)(2,1)} %copy-done, bf16[2,256,128]{2,1,0:T(8,128)(2,1)} %copy-done.31, bf16[2,256,128]{2,1,0:T(8,128)(2,1)} %copy-done.32, bf16[2,256,128]{2,1,0:T(8,128)(2,1)} %copy-done.33, ...), custom_call_target="tpu_custom_call" | custom-call | tf_op jit(solution)/shard_map/finish/pallas_call | solution.py:151
  149.5 28.9 %all_to_all.15 = bf16[16,2,16,256]{3,2,1,0:T(8,128)(2,1)S(1)} all-to-all(bf16[16,2,16,256]{3,2,1,0:T(8,128)(2,1)} %get-tuple-element.5), channel_id=1, replica_groups=mesh['front'=4,'wide'=16,'y'=4,'core'=2] {'wide'}, dimensions={0} | all-to-all | bytes 524288 | tf_op jit(solution)/shard_map/all_to_all | solution.py:222
  (126 shorter events, 37.3 us)
Async XLA Ops:
  5.5 37.0 %all-to-all-start = ((bf16[8,2,128,256]{3,2,1,0:T(8,128)(2,1)}), bf16[8,2,128,256]{3,2,1,0:T(8,128)(2,1)S(1)}, u32[]{:S(2)}, u32[]{:S(2)}) async-start(bf16[8,2,128,256]{3,2,1,0:T(8,128)(2,1)} %pick_columns.1), calls=%async_computation | async-start | bytes 2097152 | tf_op jit(solution)/shard_map/all_to_all | solution.py:209
  10.1 6.2 %collective-permute-start.6 = (bf16[2,512,128]{2,1,0:T(8,128)(2,1)S(1)}, bf16[2,512,128]{2,1,0:T(8,128)(2,1)S(1)}, u32[]{:S(2)}, u32[]{:S(2)}) collective-permute-start(bf16[2,512,128]{2,1,0:T(8,128)(2,1)S(1)} %copy-done.22), channel_id=1, source_target_pairs={{0,1},{1,0},{2,3},{3,2},{4,5},{5,4},{6,7},{7,6},{8,9},{9,8},{10,11... | collective-permute-start | bytes 786440 | tf_op jit(solution)/shard_map/ppermute | solution.py:192
  12.5 15.7 %collective-permute-start.1 = (bf16[2,512,128]{2,1,0:T(8,128)(2,1)S(1)}, bf16[2,512,128]{2,1,0:T(8,128)(2,1)S(1)}, u32[]{:S(2)}, u32[]{:S(2)}) collective-permute-start(bf16[2,512,128]{2,1,0:T(8,128)(2,1)S(1)} %copy-done.22), channel_id=1, source_target_pairs={{0,8},{1,121},{8,16},{9,1},{16,24},{17,9},{24,32},{25,17},{32,40},... | collective-permute-start | bytes 786440 | tf_op jit(solution)/shard_map/ppermute | solution.py:198
  16.2 14.7 %collective-permute-start.7 = (bf16[2,512,128]{2,1,0:T(8,128)(2,1)S(1)}, bf16[2,512,128]{2,1,0:T(8,128)(2,1)S(1)}, u32[]{:S(2)}, u32[]{:S(2)}) collective-permute-start(bf16[2,512,128]{2,1,0:T(8,128)(2,1)S(1)} %collective-permute-done.6.refs_6_), channel_id=1, source_target_pairs={{0,8},{1,121},{8,16},{9,1},{16,24},{17,9},{24,32},{25,17},{32,40},... | collective-permute-start | bytes 786440 | tf_op jit(solution)/shard_map/ppermute | solution.py:199
  28.1 56.5 %copy-start.6 = (bf16[2,512,128]{2,1,0:T(8,128)(2,1)}, bf16[2,512,128]{2,1,0:T(8,128)(2,1)S(1)}, u32[]{:S(2)}) copy-start(bf16[2,512,128]{2,1,0:T(8,128)(2,1)S(1)} %collective-permute-done.1.refs_1_) | copy-start | bytes 786436
  28.1 9.5 %collective-permute-start.2 = (bf16[2,512,128]{2,1,0:T(8,128)(2,1)S(1)}, bf16[2,512,128]{2,1,0:T(8,128)(2,1)S(1)}, u32[]{:S(2)}, u32[]{:S(2)}) collective-permute-start(bf16[2,512,128]{2,1,0:T(8,128)(2,1)S(1)} %collective-permute-done.1.refs_1_), channel_id=1, source_target_pairs={{0,8},{1,121},{8,16},{9,1},{16,24},{17,9},{24,32},{25,17},{32,40},... | collective-permute-start | bytes 786440 | tf_op jit(solution)/shard_map/ppermute | solution.py:198
  31.0 53.7 %copy-start.10 = (bf16[2,512,128]{2,1,0:T(8,128)(2,1)}, bf16[2,512,128]{2,1,0:T(8,128)(2,1)S(1)}, u32[]{:S(2)}) copy-start(bf16[2,512,128]{2,1,0:T(8,128)(2,1)S(1)} %collective-permute-done.7.refs_7_) | copy-start | bytes 786436
  31.0 9.6 %collective-permute-start.8 = (bf16[2,512,128]{2,1,0:T(8,128)(2,1)S(1)}, bf16[2,512,128]{2,1,0:T(8,128)(2,1)}, u32[]{:S(2)}, u32[]{:S(2)}) collective-permute-start(bf16[2,512,128]{2,1,0:T(8,128)(2,1)S(1)} %collective-permute-done.7.refs_7_), channel_id=1, source_target_pairs={{0,8},{1,121},{8,16},{9,1},{16,24},{17,9},{24,32},{25,17},{32,40},... | collective-permute-start | bytes 786440 | tf_op jit(solution)/shard_map/ppermute | solution.py:199
  37.6 9.5 %collective-permute-start.3 = (bf16[2,512,128]{2,1,0:T(8,128)(2,1)S(1)}, bf16[2,512,128]{2,1,0:T(8,128)(2,1)S(1)}, u32[]{:S(2)}, u32[]{:S(2)}) collective-permute-start(bf16[2,512,128]{2,1,0:T(8,128)(2,1)S(1)} %collective-permute-done.2.refs_2_), channel_id=1, source_target_pairs={{0,8},{1,121},{8,16},{9,1},{16,24},{17,9},{24,32},{25,17},{32,40},... | collective-permute-start | bytes 786440 | tf_op jit(solution)/shard_map/ppermute | solution.py:198
  40.5 9.7 %collective-permute-start.9 = (bf16[2,512,128]{2,1,0:T(8,128)(2,1)}, bf16[2,512,128]{2,1,0:T(8,128)(2,1)S(1)}, u32[]{:S(2)}, u32[]{:S(2)}) collective-permute-start(bf16[2,512,128]{2,1,0:T(8,128)(2,1)} %collective-permute-done.8.refs_8_), channel_id=1, source_target_pairs={{0,8},{1,121},{8,16},{9,1},{16,24},{17,9},{24,32},{25,17},{32,40},... | collective-permute-start | bytes 786440 | tf_op jit(solution)/shard_map/ppermute | solution.py:199
  42.5 38.2 %collective-permute-start = (bf16[8,2,128,256]{3,2,1,0:T(8,128)(2,1)S(1)}, bf16[8,2,128,256]{3,2,1,0:T(8,128)(2,1)S(1)}, u32[]{:S(2)}, u32[]{:S(2)}) collective-permute-start(bf16[8,2,128,256]{3,2,1,0:T(8,128)(2,1)S(1)} %all-to-all-done.own_ref), channel_id=1, source_target_pairs={{0,1},{1,0},{2,3},{3,2},{4,5},{5,4},{6,7},{7,6},{8,9},{9,8},{10,11... | collective-permute-start | bytes 3145736 | tf_op jit(solution)/shard_map/ppermute | solution.py:210
  47.1 9.5 %collective-permute-start.4 = (bf16[2,512,128]{2,1,0:T(8,128)(2,1)S(1)}, bf16[2,512,128]{2,1,0:T(8,128)(2,1)S(1)}, u32[]{:S(2)}, u32[]{:S(2)}) collective-permute-start(bf16[2,512,128]{2,1,0:T(8,128)(2,1)S(1)} %collective-permute-done.3.refs_3_), channel_id=1, source_target_pairs={{0,8},{1,121},{8,16},{9,1},{16,24},{17,9},{24,32},{25,17},{32,40},... | collective-permute-start | bytes 786440 | tf_op jit(solution)/shard_map/ppermute | solution.py:198
  50.2 9.5 %collective-permute-start.10 = (bf16[2,512,128]{2,1,0:T(8,128)(2,1)S(1)}, bf16[2,512,128]{2,1,0:T(8,128)(2,1)S(1)}, u32[]{:S(2)}, u32[]{:S(2)}) collective-permute-start(bf16[2,512,128]{2,1,0:T(8,128)(2,1)S(1)} %collective-permute-done.9.refs_9_), channel_id=1, source_target_pairs={{0,8},{1,121},{8,16},{9,1},{16,24},{17,9},{24,32},{25,17},{32,40},... | collective-permute-start | bytes 786440 | tf_op jit(solution)/shard_map/ppermute | solution.py:199
  56.5 9.5 %collective-permute-start.5 = (bf16[2,512,128]{2,1,0:T(8,128)(2,1)S(1)}, bf16[2,512,128]{2,1,0:T(8,128)(2,1)S(1)}, u32[]{:S(2)}, u32[]{:S(2)}) collective-permute-start(bf16[2,512,128]{2,1,0:T(8,128)(2,1)S(1)} %collective-permute-done.4.refs_4_), channel_id=1, source_target_pairs={{0,8},{1,121},{8,16},{9,1},{16,24},{17,9},{24,32},{25,17},{32,40},... | collective-permute-start | bytes 786440 | tf_op jit(solution)/shard_map/ppermute | solution.py:198
  59.7 9.5 %collective-permute-start.11 = (bf16[2,512,128]{2,1,0:T(8,128)(2,1)S(1)}, bf16[2,512,128]{2,1,0:T(8,128)(2,1)S(1)}, u32[]{:S(2)}, u32[]{:S(2)}) collective-permute-start(bf16[2,512,128]{2,1,0:T(8,128)(2,1)S(1)} %collective-permute-done.10.refs_10_), channel_id=1, source_target_pairs={{0,8},{1,121},{8,16},{9,1},{16,24},{17,9},{24,32},{25,17},{32,40},... | collective-permute-start | bytes 786440 | tf_op jit(solution)/shard_map/ppermute | solution.py:199
  66.0 9.6 %collective-permute-start.12 = (bf16[2,512,128]{2,1,0:T(8,128)(2,1)S(1)}, bf16[2,512,128]{2,1,0:T(8,128)(2,1)}, u32[]{:S(2)}, u32[]{:S(2)}) collective-permute-start(bf16[2,512,128]{2,1,0:T(8,128)(2,1)S(1)} %collective-permute-done.5.refs_5_), channel_id=1, source_target_pairs={{0,8},{1,121},{8,16},{9,1},{16,24},{17,9},{24,32},{25,17},{32,40},... | collective-permute-start | bytes 786440 | tf_op jit(solution)/shard_map/ppermute | solution.py:198
  69.1 9.6 %collective-permute-start.15 = (bf16[2,512,128]{2,1,0:T(8,128)(2,1)S(1)}, bf16[2,512,128]{2,1,0:T(8,128)(2,1)}, u32[]{:S(2)}, u32[]{:S(2)}) collective-permute-start(bf16[2,512,128]{2,1,0:T(8,128)(2,1)S(1)} %collective-permute-done.11.refs_11_), channel_id=1, source_target_pairs={{0,8},{1,121},{8,16},{9,1},{16,24},{17,9},{24,32},{25,17},{32,40},... | collective-permute-start | bytes 786440 | tf_op jit(solution)/shard_map/ppermute | solution.py:199
  75.6 15.2 %collective-permute-start.13 = (bf16[2,512,128]{2,1,0:T(8,128)(2,1)}, bf16[2,512,128]{2,1,0:T(8,128)(2,1)}, u32[]{:S(2)}, u32[]{:S(2)}) collective-permute-start(bf16[2,512,128]{2,1,0:T(8,128)(2,1)} %collective-permute-done.12.refs_0_), channel_id=1, source_target_pairs={{0,8},{1,121},{8,16},{9,1},{16,24},{17,9},{24,32},{25,17},{32,40},... | collective-permute-start | bytes 786440 | tf_op jit(solution)/shard_map/ppermute | solution.py:198
  78.7 12.7 %collective-permute-start.16 = (bf16[2,512,128]{2,1,0:T(8,128)(2,1)}, bf16[2,512,128]{2,1,0:T(8,128)(2,1)}, u32[]{:S(2)}, u32[]{:S(2)}) collective-permute-start(bf16[2,512,128]{2,1,0:T(8,128)(2,1)} %collective-permute-done.15.refs_3_), channel_id=1, source_target_pairs={{0,8},{1,121},{8,16},{9,1},{16,24},{17,9},{24,32},{25,17},{32,40},... | collective-permute-start | bytes 786440 | tf_op jit(solution)/shard_map/ppermute | solution.py:199
  88.7 27.4 %collective-permute-start.18 = (bf16[6,2,256,128]{3,2,1,0:T(8,128)(2,1)}, bf16[6,2,256,128]{3,2,1,0:T(8,128)(2,1)S(1)}, u32[]{:S(2)}, u32[]{:S(2)}) collective-permute-start(bf16[6,2,256,128]{3,2,1,0:T(8,128)(2,1)} %products.2.refs_0_), channel_id=1, source_target_pairs={{0,1},{1,0},{2,3},{3,2},{4,5},{5,4},{6,7},{7,6},{8,9},{9,8},{10,11... | collective-permute-start | bytes 2359304 | tf_op jit(solution)/shard_map/ppermute | solution.py:214
  90.7 1.4 collective-permute-start.14
  91.4 0.7 collective-permute-start.17
  96.7 19.4 %collective-permute-start.19 = (bf16[3,2,256,128]{3,2,1,0:T(8,128)(2,1)}, bf16[3,2,256,128]{3,2,1,0:T(8,128)(2,1)S(1)}, u32[]{:S(2)}, u32[]{:S(2)}) collective-permute-start(bf16[3,2,256,128]{3,2,1,0:T(8,128)(2,1)} %products.3.refs_1_), channel_id=1, source_target_pairs={{0,1},{1,0},{2,3},{3,2},{4,5},{5,4},{6,7},{7,6},{8,9},{9,8},{10,11... | collective-permute-start | bytes 1179656 | tf_op jit(solution)/shard_map/ppermute | solution.py:216
  109.4 25.3 %collective-permute-start.20 = (bf16[2,256,128]{2,1,0:T(8,128)(2,1)S(1)}, bf16[2,256,128]{2,1,0:T(8,128)(2,1)S(1)}, u32[]{:S(2)}, u32[]{:S(2)}) collective-permute-start(bf16[2,256,128]{2,1,0:T(8,128)(2,1)S(1)} %dynamic-slice_select_fusion.8), channel_id=1, source_target_pairs={{0,7},{1,0},{8,8},{9,9},{16,16},{17,17},{24,25},{25,26},{34,33},{3... | collective-permute-start | bytes 393224 | tf_op jit(solution)/shard_map/ppermute | solution.py:206
  114.7 21.3 %collective-permute-start.21 = (bf16[2,256,128]{2,1,0:T(8,128)(2,1)S(1)}, bf16[2,256,128]{2,1,0:T(8,128)(2,1)S(1)}, u32[]{:S(2)}, u32[]{:S(2)}) collective-permute-start(bf16[2,256,128]{2,1,0:T(8,128)(2,1)S(1)} %dynamic-slice_select_fusion.7), channel_id=1, source_target_pairs={{0,7},{1,1},{8,15},{9,9},{16,16},{17,18},{24,24},{25,26},{34,33},{... | collective-permute-start | bytes 393224 | tf_op jit(solution)/shard_map/ppermute | solution.py:206
  120.5 24.2 %all-to-all-start.1 = ((bf16[4,2,2,256,128]{4,3,2,1,0:T(8,128)(2,1)}), bf16[4,2,2,256,128]{4,3,2,1,0:T(8,128)(2,1)S(1)}, u32[]{:S(2)}, u32[]{:S(2)}) async-start(bf16[4,2,2,256,128]{4,3,2,1,0:T(8,128)(2,1)} %bitcast.6), calls=%async_computation.1 | async-start | bytes 2097152 | tf_op jit(solution)/shard_map/all_to_all | solution.py:219
  124.3 13.1 %collective-permute-start.22 = (bf16[2,256,128]{2,1,0:T(8,128)(2,1)S(1)}, bf16[2,256,128]{2,1,0:T(8,128)(2,1)S(1)}, u32[]{:S(2)}, u32[]{:S(2)}) collective-permute-start(bf16[2,256,128]{2,1,0:T(8,128)(2,1)S(1)} %dynamic-slice_select_fusion.6), channel_id=1, source_target_pairs={{0,6},{1,1},{8,15},{9,10},{16,23},{17,18},{24,24},{25,27},{34,32},... | collective-permute-start | bytes 393224 | tf_op jit(solution)/shard_map/ppermute | solution.py:206
  129.6 8.5 %collective-permute-start.23 = (bf16[2,256,128]{2,1,0:T(8,128)(2,1)S(1)}, bf16[2,256,128]{2,1,0:T(8,128)(2,1)S(1)}, u32[]{:S(2)}, u32[]{:S(2)}) collective-permute-start(bf16[2,256,128]{2,1,0:T(8,128)(2,1)S(1)} %dynamic-slice_select_fusion.5), channel_id=1, source_target_pairs={{0,6},{1,2},{8,14},{9,10},{16,23},{17,19},{24,31},{25,27},{34,32},... | collective-permute-start | bytes 393224 | tf_op jit(solution)/shard_map/ppermute | solution.py:206
  131.0 8.5 %collective-permute-start.24 = (bf16[2,256,128]{2,1,0:T(8,128)(2,1)S(1)}, bf16[2,256,128]{2,1,0:T(8,128)(2,1)S(1)}, u32[]{:S(2)}, u32[]{:S(2)}) collective-permute-start(bf16[2,256,128]{2,1,0:T(8,128)(2,1)S(1)} %dynamic-slice_select_fusion.4), channel_id=1, source_target_pairs={{0,5},{1,2},{8,14},{9,11},{16,22},{17,19},{24,31},{25,28},{34,39},... | collective-permute-start | bytes 393224 | tf_op jit(solution)/shard_map/ppermute | solution.py:206
  134.7 7.6 %collective-permute-start.25 = (bf16[2,256,128]{2,1,0:T(8,128)(2,1)S(1)}, bf16[2,256,128]{2,1,0:T(8,128)(2,1)S(1)}, u32[]{:S(2)}, u32[]{:S(2)}) collective-permute-start(bf16[2,256,128]{2,1,0:T(8,128)(2,1)S(1)} %dynamic-slice_select_fusion.3), channel_id=1, source_target_pairs={{0,5},{1,3},{8,13},{9,11},{16,22},{17,20},{24,30},{25,28},{34,39},... | collective-permute-start | bytes 393224 | tf_op jit(solution)/shard_map/ppermute | solution.py:206
  136.1 8.6 %collective-permute-start.26 = (bf16[2,256,128]{2,1,0:T(8,128)(2,1)S(1)}, bf16[2,256,128]{2,1,0:T(8,128)(2,1)S(1)}, u32[]{:S(2)}, u32[]{:S(2)}) collective-permute-start(bf16[2,256,128]{2,1,0:T(8,128)(2,1)S(1)} %dynamic-slice_select_fusion.2), channel_id=1, source_target_pairs={{0,4},{1,3},{8,13},{9,12},{16,21},{17,20},{24,30},{25,29},{34,38},... | collective-permute-start | bytes 393224 | tf_op jit(solution)/shard_map/ppermute | solution.py:206
  137.4 7.3 %collective-permute-start.27 = (bf16[2,256,128]{2,1,0:T(8,128)(2,1)S(1)}, bf16[2,256,128]{2,1,0:T(8,128)(2,1)S(1)}, u32[]{:S(2)}, u32[]{:S(2)}) collective-permute-start(bf16[2,256,128]{2,1,0:T(8,128)(2,1)S(1)} %fusion), channel_id=1, source_target_pairs={{0,0},{1,4},{8,8},{9,12},{16,17},{17,21},{24,25},{25,29},{34,34},{... | collective-permute-start | bytes 393224 | tf_op jit(solution)/shard_map/ppermute | solution.py:206
  (38 other events, 407.3 us)
where the time goes:
time: 181 us; the launch traced here: 180 us
  starting transfers between devices  76.9 us (42%)
  waiting for transfers between devices  41.2 us (23%)
  blocking collectives  28.9 us (16%)
  Pallas kernels  20.2 us (11%)
  local copies, waits for them, and re-layouts  6.51 us (4%)
  other arithmetic  4.62 us (3%)
    all_to_all x1, blocking collectives, level(): sums = lax.all_to_all(site, 'wide', split_axis=0, concat_axis=0, tiled=True)  28.9 us
    ppermute x8, waiting for transfers between devices, level(): owns.append(lax.ppermute(owns[-1], ('wide', 'core'), pairs))  27.9 us
    ppermute x8, starting transfers between devices, level(): pieces.append(lax.ppermute(piece, ('wide', 'y', 'core'), piece_pairs(step)))  16.9 us
    ppermute x8, starting transfers between devices, level(): others.append(lax.ppermute(others[-1], ('wide', 'core'), pairs))  16 us
    ppermute x8, starting transfers between devices, level(): owns.append(lax.ppermute(owns[-1], ('wide', 'core'), pairs))  15.9 us
    ppermute x1, starting transfers between devices, level(): theirs.append(lax.ppermute(mine[1], 'core', swap))  12.6 us
    pallas_call x2, Pallas kernels, products(): pl.pallas_call(body, out_shape=jax.ShapeDtypeStruct((count, fronts, width...  7.12 us
    ppermute x8, waiting for transfers between devices, level(): others.append(lax.ppermute(others[-1], ('wide', 'core'), pairs))  6.71 us
  transfers between devices with their start and end apart: 30, of which 15 were waited for; matrix products, arithmetic and copies ran while one was open for 2% of the time, Pallas kernels for 7%

commit v1 on v0

--- a/solution.py
+++ b/solution.py
@@ -11,42 +11,23 @@
 WHOLE = pl.BlockSpec(memory_space=pltpu.VMEM)
 
 
-def pick_columns(bnd, pos, ancestor):
-    def body(bnd_ref, pos_ref, a_ref, o_ref):
-        o_ref[...] = a_ref[...]
-
-    slots, rows, _ = ancestor.shape
-    fronts = bnd.shape[0]
-    return pl.pallas_call(
-        body,
-        out_shape=jax.ShapeDtypeStruct((slots, fronts, rows, 2 * BLK), ancestor.dtype),
-        grid_spec=pltpu.PrefetchScalarGridSpec(
-            num_scalar_prefetch=2,
-            grid=(fronts, 2),
-            in_specs=[
-                pl.BlockSpec(
-                    (slots, rows, BLK),
-                    lambda m, j, b, p: (0, 0, b[m, 2 * p[0] + j] - 4 * p[0]),
-                )
-            ],
-            out_specs=pl.BlockSpec((slots, None, rows, BLK), lambda m, j, b, p: (0, m, 0, j)),
-        ),
-        name="pick_columns",
-    )(bnd, pos, ancestor)
-
-
 def turned(bnd, owner, pos, own, other):
-    _, fronts, rows, width = own.shape
-    blocks = bnd.shape[1] // 8
+    fronts, rows = bnd.shape[0], own.shape[1]
+    blocks, width = bnd.shape[1] // 8, 2 * BLK
 
     def body(bnd_ref, owner_ref, pos_ref, own_ref, other_ref, o_ref):
-        n = pos_ref[1]
+        w, n = pos_ref[0], pos_ref[1]
         for m in range(fronts):
+            columns = [
+                pl.ds(pl.multiple_of((bnd_ref[m, 2 * w + b] - 4 * w) * BLK, BLK), BLK) for b in range(2)
+            ]
             for c, (ref, at) in enumerate(((own_ref, n), (other_ref, n ^ 1))):
                 for j in range(blocks):
                     source = owner_ref[bnd_ref[m, blocks * at + j]]
                     first = (c * blocks + j) * rows
-                    o_ref[m, :, first : first + rows] = ref[source, m].T
+                    for b in range(2):
+                        block = ref[source, :, columns[b]]
+                        o_ref[m, b * BLK : (b + 1) * BLK, first : first + rows] = block.T
 
     smem = pl.BlockSpec(memory_space=pltpu.SMEM)
     return pl.pallas_call(
@@ -186,7 +167,7 @@
     narrow = lax.axis_index("y") * 2 + core
     pos = jnp.stack([w, narrow, core]).astype(jnp.int32)
     swap = [(0, 1), (1, 0)]
-    early = 6
+    early = 7
 
     owns = [gain]
     others = [lax.ppermute(gain, "core", swap)]
@@ -205,8 +186,7 @@
         piece = lax.dynamic_slice_in_dim(held, (w & 1) * rows, rows, 1)
         pieces.append(lax.ppermute(piece, ("wide", "y", "core"), piece_pairs(step)))
         if step == 1:
-            picked = pick_columns(boundary, pos, ancestor_cov)
-            arrived = lax.all_to_all(picked, NARROW, split_axis=0, concat_axis=0, tiled=True)
+            arrived = lax.all_to_all(ancestor_cov, NARROW, split_axis=0, concat_axis=0, tiled=True)
             paired = lax.ppermute(arrived, "core", swap)
             left = turned(boundary, owner, pos, arrived, paired)
 

time: 181 us -> 177 us (0.978)
  waiting for transfers between devices: 41.2 us -> 47.6 us
  starting transfers between devices: 76.9 us -> 70.8 us
  Pallas kernels: 20.2 us -> 16 us
    ppermute x8, waiting for transfers between devices: 6.71 us -> 15.6 us  [level(): others.append(lax.ppermute(others[-1], ('wide', 'core'), pairs))]
    ppermute x1, starting transfers between devices: 12.6 us -> 6.22 us  [level(): theirs.append(lax.ppermute(mine[1], 'core', swap))]
    pallas_call x1 -> x0, Pallas kernels: 4.2 us -> none  [pick_columns(): pl.pallas_call(body, out_shape=jax.ShapeDtypeStruct((slots, fronts, rows,...]
  transfers between devices with their start and end apart: 30 -> 30, of which waited for: 15 -> 15; matrix products, arithmetic and copies ran while one was open for 2% -> 2% of each run, Pallas kernels for 7% -> 5%
where the time goes in v1:
time: 177 us; the launch traced here: 176 us
  starting transfers between devices  70.8 us (40%)
  waiting for transfers between devices  47.6 us (27%)
  blocking collectives  28.1 us (16%)
  Pallas kernels  16 us (9%)
  local copies, waits for them, and re-layouts  7.38 us (4%)
  other arithmetic  4.64 us (3%)
    all_to_all x1, blocking collectives, level(): sums = lax.all_to_all(site, 'wide', split_axis=0, concat_axis=0, tiled=True)  28.1 us
    ppermute x8, waiting for transfers between devices, level(): owns.append(lax.ppermute(owns[-1], ('wide', 'core'), pairs))  26.5 us
    ppermute x8, starting transfers between devices, level(): pieces.append(lax.ppermute(piece, ('wide', 'y', 'core'), piece_pairs(step)))  17.1 us
    ppermute x8, starting transfers between devices, level(): others.append(lax.ppermute(others[-1], ('wide', 'core'), pairs))  16 us
    ppermute x8, starting transfers between devices, level(): owns.append(lax.ppermute(owns[-1], ('wide', 'core'), pairs))  16 us
    ppermute x8, waiting for transfers between devices, level(): others.append(lax.ppermute(others[-1], ('wide', 'core'), pairs))  15.6 us
    unnamed x80, local copies, waits for them, and re-layouts  7.38 us
    pallas_call x2, Pallas kernels, products(): pl.pallas_call(body, out_shape=jax.ShapeDtypeStruct((count, fronts, width...  7.14 us
  transfers between devices with their start and end apart: 30, of which 15 were waited for; matrix products, arithmetic and copies ran while one was open for 2% of the time, Pallas kernels for 5%

profile of v1, /device:TPU:4, one launch (start us, length us, event | category | flops | bytes accessed | tf_op | source)
XLA Modules:
  0.0 176.0 jit_solution(13775670383700230149)
XLA Ops:
  0.6 4.6 %all-to-all-start = ((bf16[8,128,512]{2,1,0:T(8,128)(2,1)}), bf16[8,128,512]{2,1,0:T(8,128)(2,1)S(1)}, u32[]{:S(2)}, u32[]{:S(2)}) async-start(bf16[8,128,512]{2,1,0:T(8,128)(2,1)} %param.7), calls=%async_computation | async-start | bytes 2097152 | tf_op jit(solution)/shard_map/all_to_all | solution.py:189
  5.3 2.4 %collective-permute-start.7 = (bf16[2,512,128]{2,1,0:T(8,128)(2,1)S(1)}, bf16[2,512,128]{2,1,0:T(8,128)(2,1)S(1)}, u32[]{:S(2)}, u32[]{:S(2)}) collective-permute-start(bf16[2,512,128]{2,1,0:T(8,128)(2,1)S(1)} %copy-done.22), channel_id=1, source_target_pairs={{0,1},{1,0},{2,3},{3,2},{4,5},{5,4},{6,7},{7,6},{8,9},{9,8},{10,11... | collective-permute-start | bytes 786440 | tf_op jit(solution)/shard_map/ppermute | solution.py:173
  7.7 3.8 %collective-permute-start.1 = (bf16[2,512,128]{2,1,0:T(8,128)(2,1)S(1)}, bf16[2,512,128]{2,1,0:T(8,128)(2,1)S(1)}, u32[]{:S(2)}, u32[]{:S(2)}) collective-permute-start(bf16[2,512,128]{2,1,0:T(8,128)(2,1)S(1)} %copy-done.22), channel_id=1, source_target_pairs={{0,8},{1,121},{8,16},{9,1},{16,24},{17,9},{24,32},{25,17},{32,40},... | collective-permute-start | bytes 786440 | tf_op jit(solution)/shard_map/ppermute | solution.py:179
  11.5 3.8 %collective-permute-start.8 = (bf16[2,512,128]{2,1,0:T(8,128)(2,1)S(1)}, bf16[2,512,128]{2,1,0:T(8,128)(2,1)S(1)}, u32[]{:S(2)}, u32[]{:S(2)}) collective-permute-start(bf16[2,512,128]{2,1,0:T(8,128)(2,1)S(1)} %collective-permute-done.7.refs_7_), channel_id=1, source_target_pairs={{0,8},{1,121},{8,16},{9,1},{16,24},{17,9},{24,32},{25,17},{32,40},... | collective-permute-start | bytes 786440 | tf_op jit(solution)/shard_map/ppermute | solution.py:180
  15.4 8.1 %collective-permute-done.1.refs_1_ = bf16[2,512,128]{2,1,0:T(8,128)(2,1)S(1)} collective-permute-done((bf16[2,512,128]{2,1,0:T(8,128)(2,1)S(1)}, bf16[2,512,128]{2,1,0:T(8,128)(2,1)S(1)}, u32[]{:S(2)}, u32[]{:S(2)}) %collective-permute-start.1) | collective-permute-done | bytes 262176 | tf_op jit(solution)/shard_map/ppermute | solution.py:179
  28.1 4.7 %collective-permute-done.2.refs_2_ = bf16[2,512,128]{2,1,0:T(8,128)(2,1)S(1)} collective-permute-done((bf16[2,512,128]{2,1,0:T(8,128)(2,1)S(1)}, bf16[2,512,128]{2,1,0:T(8,128)(2,1)S(1)}, u32[]{:S(2)}, u32[]{:S(2)}) %collective-permute-start.2) | collective-permute-done | bytes 262176 | tf_op jit(solution)/shard_map/ppermute | solution.py:179
  34.8 2.9 %collective-permute-start = (bf16[8,128,512]{2,1,0:T(8,128)(2,1)S(1)}, bf16[8,128,512]{2,1,0:T(8,128)(2,1)S(1)}, u32[]{:S(2)}, u32[]{:S(2)}) collective-permute-start(bf16[8,128,512]{2,1,0:T(8,128)(2,1)S(1)} %all-to-all-done.own_ref), channel_id=1, source_target_pairs={{0,1},{1,0},{2,3},{3,2},{4,5},{5,4},{6,7},{7,6},{8,9},{9,8},{10,11... | collective-permute-start | bytes 3145736 | tf_op jit(solution)/shard_map/ppermute | solution.py:190
  37.7 1.9 %collective-permute-start.10 = (bf16[2,512,128]{2,1,0:T(8,128)(2,1)}, bf16[2,512,128]{2,1,0:T(8,128)(2,1)S(1)}, u32[]{:S(2)}, u32[]{:S(2)}) collective-permute-start(bf16[2,512,128]{2,1,0:T(8,128)(2,1)} %collective-permute-done.9.refs_9_), channel_id=1, source_target_pairs={{0,8},{1,121},{8,16},{9,1},{16,24},{17,9},{24,32},{25,17},{32,40},... | collective-permute-start | bytes 786440 | tf_op jit(solution)/shard_map/ppermute | solution.py:180
  39.6 2.7 %collective-permute-done.3.refs_3_ = bf16[2,512,128]{2,1,0:T(8,128)(2,1)S(1)} collective-permute-done((bf16[2,512,128]{2,1,0:T(8,128)(2,1)S(1)}, bf16[2,512,128]{2,1,0:T(8,128)(2,1)S(1)}, u32[]{:S(2)}, u32[]{:S(2)}) %collective-permute-start.3) | collective-permute-done | bytes 262176 | tf_op jit(solution)/shard_map/ppermute | solution.py:179
  44.3 3.1 %collective-permute-done.10.refs_10_ = bf16[2,512,128]{2,1,0:T(8,128)(2,1)S(1)} collective-permute-done((bf16[2,512,128]{2,1,0:T(8,128)(2,1)}, bf16[2,512,128]{2,1,0:T(8,128)(2,1)S(1)}, u32[]{:S(2)}, u32[]{:S(2)}) %collective-permute-start.10) | collective-permute-done | bytes 262176 | tf_op jit(solution)/shard_map/ppermute | solution.py:180
  49.3 2.5 %collective-permute-done.4.refs_4_ = bf16[2,512,128]{2,1,0:T(8,128)(2,1)S(1)} collective-permute-done((bf16[2,512,128]{2,1,0:T(8,128)(2,1)S(1)}, bf16[2,512,128]{2,1,0:T(8,128)(2,1)S(1)}, u32[]{:S(2)}, u32[]{:S(2)}) %collective-permute-start.4) | collective-permute-done | bytes 262176 | tf_op jit(solution)/shard_map/ppermute | solution.py:179
  53.7 3.1 %collective-permute-done.11.refs_11_ = bf16[2,512,128]{2,1,0:T(8,128)(2,1)S(1)} collective-permute-done((bf16[2,512,128]{2,1,0:T(8,128)(2,1)S(1)}, bf16[2,512,128]{2,1,0:T(8,128)(2,1)S(1)}, u32[]{:S(2)}, u32[]{:S(2)}) %collective-permute-start.11) | collective-permute-done | bytes 262176 | tf_op jit(solution)/shard_map/ppermute | solution.py:180
  58.8 2.6 %collective-permute-done.5.refs_5_ = bf16[2,512,128]{2,1,0:T(8,128)(2,1)} collective-permute-done((bf16[2,512,128]{2,1,0:T(8,128)(2,1)S(1)}, bf16[2,512,128]{2,1,0:T(8,128)(2,1)}, u32[]{:S(2)}, u32[]{:S(2)}) %collective-permute-start.5) | collective-permute-done | bytes 262176 | tf_op jit(solution)/shard_map/ppermute | solution.py:179
  63.3 3.1 %collective-permute-done.12.refs_12_ = bf16[2,512,128]{2,1,0:T(8,128)(2,1)} collective-permute-done((bf16[2,512,128]{2,1,0:T(8,128)(2,1)S(1)}, bf16[2,512,128]{2,1,0:T(8,128)(2,1)}, u32[]{:S(2)}, u32[]{:S(2)}) %collective-permute-start.12) | collective-permute-done | bytes 262176 | tf_op jit(solution)/shard_map/ppermute | solution.py:180
  70.1 2.9 %turned.1.left_ref = bf16[2,256,1024]{2,1,0:T(8,128)(2,1)} custom-call(s32[2,32]{1,0:T(2,128)} %bnd_ref.1, s32[64]{0:T(128)} %owner_ref.1, s32[3]{0:T(128)} %pad_add_fusion.pos_ref, bf16[8,128,512]{2,1,0:T(8,128)(2,1)} %copy-done.1, bf16[8,128,512]{2,1,0:T(8,128)(2,1)} %copy-done.2), custom_call_target="tpu_custom_call" | custom-call | tf_op jit(solution)/shard_map/turned/pallas_call | solution.py:33
  73.0 3.2 %collective-permute-done.13.refs_13_ = bf16[2,512,128]{2,1,0:T(8,128)(2,1)} collective-permute-done((bf16[2,512,128]{2,1,0:T(8,128)(2,1)}, bf16[2,512,128]{2,1,0:T(8,128)(2,1)}, u32[]{:S(2)}, u32[]{:S(2)}) %collective-permute-start.13) | collective-permute-done | bytes 262176 | tf_op jit(solution)/shard_map/ppermute | solution.py:180
  76.2 4.5 %products.2.refs_0_ = bf16[7,2,256,128]{3,2,1,0:T(8,128)(2,1)} custom-call(bf16[2,256,1024]{2,1,0:T(8,128)(2,1)} %turned.1.left_ref, bf16[2,512,128]{2,1,0:T(8,128)(2,1)} %refs_0_.1, bf16[2,512,128]{2,1,0:T(8,128)(2,1)} %copy-done.6, bf16[2,512,128]{2,1,0:T(8,128)(2,1)} %copy-done.10, bf16[2,512,128]{2,1,0:T(8,128)(2,1)} %copy-done.4, ...), custom_call_target="tpu_custom_call" | custom-call | flops 939524096 | bytes 7340032 | tf_op jit(solution)/shard_map/products/pallas_call | solution.py:60
  80.7 2.1 %collective-permute-start.18 = (bf16[7,2,256,128]{3,2,1,0:T(8,128)(2,1)}, bf16[7,2,256,128]{3,2,1,0:T(8,128)(2,1)S(1)}, u32[]{:S(2)}, u32[]{:S(2)}) collective-permute-start(bf16[7,2,256,128]{3,2,1,0:T(8,128)(2,1)} %products.2.refs_0_), channel_id=1, source_target_pairs={{0,1},{1,0},{2,3},{3,2},{4,5},{5,4},{6,7},{7,6},{8,9},{9,8},{10,11... | collective-permute-start | bytes 2752520 | tf_op jit(solution)/shard_map/ppermute | solution.py:194
  82.8 1.9 %collective-permute-start.14 = (bf16[2,512,128]{2,1,0:T(8,128)(2,1)}, bf16[2,512,128]{2,1,0:T(8,128)(2,1)S(1)}, u32[]{:S(2)}, u32[]{:S(2)}) collective-permute-start(bf16[2,512,128]{2,1,0:T(8,128)(2,1)} %collective-permute-done.6.refs_6_), channel_id=1, source_target_pairs={{0,8},{1,121},{8,16},{9,1},{16,24},{17,9},{24,32},{25,17},{32,40},... | collective-permute-start | bytes 786440 | tf_op jit(solution)/shard_map/ppermute | solution.py:179
  84.7 1.9 %collective-permute-start.16 = (bf16[2,512,128]{2,1,0:T(8,128)(2,1)}, bf16[2,512,128]{2,1,0:T(8,128)(2,1)S(1)}, u32[]{:S(2)}, u32[]{:S(2)}) collective-permute-start(bf16[2,512,128]{2,1,0:T(8,128)(2,1)} %collective-permute-done.13.refs_13_), channel_id=1, source_target_pairs={{0,8},{1,121},{8,16},{9,1},{16,24},{17,9},{24,32},{25,17},{32,40},... | collective-permute-start | bytes 786440 | tf_op jit(solution)/shard_map/ppermute | solution.py:180
  86.7 5.8 %collective-permute-done.14.refs_0_ = bf16[2,512,128]{2,1,0:T(8,128)(2,1)S(1)} collective-permute-done((bf16[2,512,128]{2,1,0:T(8,128)(2,1)}, bf16[2,512,128]{2,1,0:T(8,128)(2,1)S(1)}, u32[]{:S(2)}, u32[]{:S(2)}) %collective-permute-start.14) | collective-permute-done | bytes 262176 | tf_op jit(solution)/shard_map/ppermute | solution.py:179
  93.2 2.1 %collective-permute-done.16.refs_2_ = bf16[2,512,128]{2,1,0:T(8,128)(2,1)S(1)} collective-permute-done((bf16[2,512,128]{2,1,0:T(8,128)(2,1)}, bf16[2,512,128]{2,1,0:T(8,128)(2,1)S(1)}, u32[]{:S(2)}, u32[]{:S(2)}) %collective-permute-start.16) | collective-permute-done | bytes 262176 | tf_op jit(solution)/shard_map/ppermute | solution.py:180
  97.4 2.6 %products.3.refs_1_ = bf16[2,2,256,128]{3,2,1,0:T(8,128)(2,1)} custom-call(bf16[2,256,1024]{2,1,0:T(8,128)(2,1)} %turned.1.left_ref, bf16[2,512,128]{2,1,0:T(8,128)(2,1)} %copy-done.18, bf16[2,512,128]{2,1,0:T(8,128)(2,1)} %copy-done.26, bf16[2,512,128]{2,1,0:T(8,128)(2,1)} %copy-done.20, bf16[2,512,128]{2,1,0:T(8,128)(2,1)} %copy-done.28), custom_call_target="tpu_custom_call" | custom-call | flops 268435456 | bytes 2097152 | tf_op jit(solution)/shard_map/products/pallas_call | solution.py:60
  100.0 6.2 %collective-permute-start.19 = (bf16[2,2,256,128]{3,2,1,0:T(8,128)(2,1)}, bf16[2,2,256,128]{3,2,1,0:T(8,128)(2,1)S(1)}, u32[]{:S(2)}, u32[]{:S(2)}) collective-permute-start(bf16[2,2,256,128]{3,2,1,0:T(8,128)(2,1)} %products.3.refs_1_), channel_id=1, source_target_pairs={{0,1},{1,0},{2,3},{3,2},{4,5},{5,4},{6,7},{7,6},{8,9},{9,8},{10,11... | collective-permute-start | bytes 786440 | tf_op jit(solution)/shard_map/ppermute | solution.py:196
  106.4 4.5 %collective-permute-start.20 = (bf16[2,256,128]{2,1,0:T(8,128)(2,1)S(1)}, bf16[2,256,128]{2,1,0:T(8,128)(2,1)S(1)}, u32[]{:S(2)}, u32[]{:S(2)}) collective-permute-start(bf16[2,256,128]{2,1,0:T(8,128)(2,1)S(1)} %dynamic-slice_select_fusion.8), channel_id=1, source_target_pairs={{0,7},{1,0},{8,8},{9,9},{16,16},{17,17},{24,25},{25,26},{34,33},{3... | collective-permute-start | bytes 393224 | tf_op jit(solution)/shard_map/ppermute | solution.py:187
  114.8 2.8 %assemble.1 = bf16[8,2,256,128]{3,2,1,0:T(8,128)(2,1)} custom-call(s32[3]{0:T(128)} %pad_add_fusion.pos_ref, bf16[7,2,256,128]{3,2,1,0:T(8,128)(2,1)} %products.2.refs_0_, bf16[2,2,256,128]{3,2,1,0:T(8,128)(2,1)} %products.3.refs_1_, bf16[7,2,256,128]{3,2,1,0:T(8,128)(2,1)} %copy-done.3, bf16[2,2,256,128]{3,2,1,0:T(8,128)(2,1)} %copy-done.30), custom_call_target="tpu_custom_call" | custom-call | tf_op jit(solution)/shard_map/assemble/pallas_call | solution.py:95
  117.5 3.7 %all-to-all-start.1 = ((bf16[4,2,2,256,128]{4,3,2,1,0:T(8,128)(2,1)}), bf16[4,2,2,256,128]{4,3,2,1,0:T(8,128)(2,1)S(1)}, u32[]{:S(2)}, u32[]{:S(2)}) async-start(bf16[4,2,2,256,128]{4,3,2,1,0:T(8,128)(2,1)} %bitcast.6), calls=%async_computation.1 | async-start | bytes 2097152 | tf_op jit(solution)/shard_map/all_to_all | solution.py:199
  121.3 5.2 %collective-permute-start.22 = (bf16[2,256,128]{2,1,0:T(8,128)(2,1)S(1)}, bf16[2,256,128]{2,1,0:T(8,128)(2,1)S(1)}, u32[]{:S(2)}, u32[]{:S(2)}) collective-permute-start(bf16[2,256,128]{2,1,0:T(8,128)(2,1)S(1)} %dynamic-slice_select_fusion.6), channel_id=1, source_target_pairs={{0,6},{1,1},{8,15},{9,10},{16,23},{17,18},{24,24},{25,27},{34,32},... | collective-permute-start | bytes 393224 | tf_op jit(solution)/shard_map/ppermute | solution.py:187
  136.4 2.8 %collective-permute-done.25.refs_5_ = bf16[2,256,128]{2,1,0:T(8,128)(2,1)S(1)} collective-permute-done((bf16[2,256,128]{2,1,0:T(8,128)(2,1)S(1)}, bf16[2,256,128]{2,1,0:T(8,128)(2,1)S(1)}, u32[]{:S(2)}, u32[]{:S(2)}) %collective-permute-start.25) | collective-permute-done | bytes 131104 | tf_op jit(solution)/shard_map/ppermute | solution.py:187
  139.3 2.3 %collective-permute-done.26.refs_6_ = bf16[2,256,128]{2,1,0:T(8,128)(2,1)S(1)} collective-permute-done((bf16[2,256,128]{2,1,0:T(8,128)(2,1)S(1)}, bf16[2,256,128]{2,1,0:T(8,128)(2,1)S(1)}, u32[]{:S(2)}, u32[]{:S(2)}) %collective-permute-start.26) | collective-permute-done | bytes 131104 | tf_op jit(solution)/shard_map/ppermute | solution.py:187
  143.3 3.2 %finish.1 = (f32[2,256,256]{2,1,0:T(8,128)}, bf16[16,2,16,256]{3,2,1,0:T(8,128)(2,1)}) custom-call(s32[3]{0:T(128)} %pad_add_fusion.pos_ref, bf16[4,2,2,256,128]{4,3,2,1,0:T(8,128)(2,1)} %copy-done, bf16[2,256,128]{2,1,0:T(8,128)(2,1)} %copy-done.31, bf16[2,256,128]{2,1,0:T(8,128)(2,1)} %copy-done.32, bf16[2,256,128]{2,1,0:T(8,128)(2,1)} %copy-done.33, ...), custom_call_target="tpu_custom_call" | custom-call | tf_op jit(solution)/shard_map/finish/pallas_call | solution.py:132
  146.4 28.1 %all_to_all.15 = bf16[16,2,16,256]{3,2,1,0:T(8,128)(2,1)S(1)} all-to-all(bf16[16,2,16,256]{3,2,1,0:T(8,128)(2,1)} %get-tuple-element.5), channel_id=1, replica_groups=mesh['front'=4,'wide'=16,'y'=4,'core'=2] {'wide'}, dimensions={0} | all-to-all | bytes 524288 | tf_op jit(solution)/shard_map/all_to_all | solution.py:202
  (125 shorter events, 39.3 us)
Async XLA Ops:
  0.6 34.2 %all-to-all-start = ((bf16[8,128,512]{2,1,0:T(8,128)(2,1)}), bf16[8,128,512]{2,1,0:T(8,128)(2,1)S(1)}, u32[]{:S(2)}, u32[]{:S(2)}) async-start(bf16[8,128,512]{2,1,0:T(8,128)(2,1)} %param.7), calls=%async_computation | async-start | bytes 2097152 | tf_op jit(solution)/shard_map/all_to_all | solution.py:189
  5.3 6.2 %collective-permute-start.7 = (bf16[2,512,128]{2,1,0:T(8,128)(2,1)S(1)}, bf16[2,512,128]{2,1,0:T(8,128)(2,1)S(1)}, u32[]{:S(2)}, u32[]{:S(2)}) collective-permute-start(bf16[2,512,128]{2,1,0:T(8,128)(2,1)S(1)} %copy-done.22), channel_id=1, source_target_pairs={{0,1},{1,0},{2,3},{3,2},{4,5},{5,4},{6,7},{7,6},{8,9},{9,8},{10,11... | collective-permute-start | bytes 786440 | tf_op jit(solution)/shard_map/ppermute | solution.py:173
  7.7 15.7 %collective-permute-start.1 = (bf16[2,512,128]{2,1,0:T(8,128)(2,1)S(1)}, bf16[2,512,128]{2,1,0:T(8,128)(2,1)S(1)}, u32[]{:S(2)}, u32[]{:S(2)}) collective-permute-start(bf16[2,512,128]{2,1,0:T(8,128)(2,1)S(1)} %copy-done.22), channel_id=1, source_target_pairs={{0,8},{1,121},{8,16},{9,1},{16,24},{17,9},{24,32},{25,17},{32,40},... | collective-permute-start | bytes 786440 | tf_op jit(solution)/shard_map/ppermute | solution.py:179
  11.5 14.7 %collective-permute-start.8 = (bf16[2,512,128]{2,1,0:T(8,128)(2,1)S(1)}, bf16[2,512,128]{2,1,0:T(8,128)(2,1)S(1)}, u32[]{:S(2)}, u32[]{:S(2)}) collective-permute-start(bf16[2,512,128]{2,1,0:T(8,128)(2,1)S(1)} %collective-permute-done.7.refs_7_), channel_id=1, source_target_pairs={{0,8},{1,121},{8,16},{9,1},{16,24},{17,9},{24,32},{25,17},{32,40},... | collective-permute-start | bytes 786440 | tf_op jit(solution)/shard_map/ppermute | solution.py:180
  23.4 49.6 %copy-start.6 = (bf16[2,512,128]{2,1,0:T(8,128)(2,1)}, bf16[2,512,128]{2,1,0:T(8,128)(2,1)S(1)}, u32[]{:S(2)}) copy-start(bf16[2,512,128]{2,1,0:T(8,128)(2,1)S(1)} %collective-permute-done.1.refs_1_) | copy-start | bytes 786436
  23.4 9.5 %collective-permute-start.2 = (bf16[2,512,128]{2,1,0:T(8,128)(2,1)S(1)}, bf16[2,512,128]{2,1,0:T(8,128)(2,1)S(1)}, u32[]{:S(2)}, u32[]{:S(2)}) collective-permute-start(bf16[2,512,128]{2,1,0:T(8,128)(2,1)S(1)} %collective-permute-done.1.refs_1_), channel_id=1, source_target_pairs={{0,8},{1,121},{8,16},{9,1},{16,24},{17,9},{24,32},{25,17},{32,40},... | collective-permute-start | bytes 786440 | tf_op jit(solution)/shard_map/ppermute | solution.py:179
  26.2 46.8 %copy-start.8 = (bf16[2,512,128]{2,1,0:T(8,128)(2,1)}, bf16[2,512,128]{2,1,0:T(8,128)(2,1)S(1)}, u32[]{:S(2)}) copy-start(bf16[2,512,128]{2,1,0:T(8,128)(2,1)S(1)} %collective-permute-done.8.refs_8_) | copy-start | bytes 786436
  26.2 11.5 %collective-permute-start.9 = (bf16[2,512,128]{2,1,0:T(8,128)(2,1)S(1)}, bf16[2,512,128]{2,1,0:T(8,128)(2,1)}, u32[]{:S(2)}, u32[]{:S(2)}) collective-permute-start(bf16[2,512,128]{2,1,0:T(8,128)(2,1)S(1)} %collective-permute-done.8.refs_8_), channel_id=1, source_target_pairs={{0,8},{1,121},{8,16},{9,1},{16,24},{17,9},{24,32},{25,17},{32,40},... | collective-permute-start | bytes 786440 | tf_op jit(solution)/shard_map/ppermute | solution.py:180
  32.9 9.5 %collective-permute-start.3 = (bf16[2,512,128]{2,1,0:T(8,128)(2,1)S(1)}, bf16[2,512,128]{2,1,0:T(8,128)(2,1)S(1)}, u32[]{:S(2)}, u32[]{:S(2)}) collective-permute-start(bf16[2,512,128]{2,1,0:T(8,128)(2,1)S(1)} %collective-permute-done.2.refs_2_), channel_id=1, source_target_pairs={{0,8},{1,121},{8,16},{9,1},{16,24},{17,9},{24,32},{25,17},{32,40},... | collective-permute-start | bytes 786440 | tf_op jit(solution)/shard_map/ppermute | solution.py:179
  34.8 34.2 %collective-permute-start = (bf16[8,128,512]{2,1,0:T(8,128)(2,1)S(1)}, bf16[8,128,512]{2,1,0:T(8,128)(2,1)S(1)}, u32[]{:S(2)}, u32[]{:S(2)}) collective-permute-start(bf16[8,128,512]{2,1,0:T(8,128)(2,1)S(1)} %all-to-all-done.own_ref), channel_id=1, source_target_pairs={{0,1},{1,0},{2,3},{3,2},{4,5},{5,4},{6,7},{7,6},{8,9},{9,8},{10,11... | collective-permute-start | bytes 3145736 | tf_op jit(solution)/shard_map/ppermute | solution.py:190
  37.7 9.7 %collective-permute-start.10 = (bf16[2,512,128]{2,1,0:T(8,128)(2,1)}, bf16[2,512,128]{2,1,0:T(8,128)(2,1)S(1)}, u32[]{:S(2)}, u32[]{:S(2)}) collective-permute-start(bf16[2,512,128]{2,1,0:T(8,128)(2,1)} %collective-permute-done.9.refs_9_), channel_id=1, source_target_pairs={{0,8},{1,121},{8,16},{9,1},{16,24},{17,9},{24,32},{25,17},{32,40},... | collective-permute-start | bytes 786440 | tf_op jit(solution)/shard_map/ppermute | solution.py:180
  42.4 9.5 %collective-permute-start.4 = (bf16[2,512,128]{2,1,0:T(8,128)(2,1)S(1)}, bf16[2,512,128]{2,1,0:T(8,128)(2,1)S(1)}, u32[]{:S(2)}, u32[]{:S(2)}) collective-permute-start(bf16[2,512,128]{2,1,0:T(8,128)(2,1)S(1)} %collective-permute-done.3.refs_3_), channel_id=1, source_target_pairs={{0,8},{1,121},{8,16},{9,1},{16,24},{17,9},{24,32},{25,17},{32,40},... | collective-permute-start | bytes 786440 | tf_op jit(solution)/shard_map/ppermute | solution.py:179
  47.4 9.5 %collective-permute-start.11 = (bf16[2,512,128]{2,1,0:T(8,128)(2,1)S(1)}, bf16[2,512,128]{2,1,0:T(8,128)(2,1)S(1)}, u32[]{:S(2)}, u32[]{:S(2)}) collective-permute-start(bf16[2,512,128]{2,1,0:T(8,128)(2,1)S(1)} %collective-permute-done.10.refs_10_), channel_id=1, source_target_pairs={{0,8},{1,121},{8,16},{9,1},{16,24},{17,9},{24,32},{25,17},{32,40},... | collective-permute-start | bytes 786440 | tf_op jit(solution)/shard_map/ppermute | solution.py:180
  51.8 9.6 %collective-permute-start.5 = (bf16[2,512,128]{2,1,0:T(8,128)(2,1)S(1)}, bf16[2,512,128]{2,1,0:T(8,128)(2,1)}, u32[]{:S(2)}, u32[]{:S(2)}) collective-permute-start(bf16[2,512,128]{2,1,0:T(8,128)(2,1)S(1)} %collective-permute-done.4.refs_4_), channel_id=1, source_target_pairs={{0,8},{1,121},{8,16},{9,1},{16,24},{17,9},{24,32},{25,17},{32,40},... | collective-permute-start | bytes 786440 | tf_op jit(solution)/shard_map/ppermute | solution.py:179
  56.9 9.6 %collective-permute-start.12 = (bf16[2,512,128]{2,1,0:T(8,128)(2,1)S(1)}, bf16[2,512,128]{2,1,0:T(8,128)(2,1)}, u32[]{:S(2)}, u32[]{:S(2)}) collective-permute-start(bf16[2,512,128]{2,1,0:T(8,128)(2,1)S(1)} %collective-permute-done.11.refs_11_), channel_id=1, source_target_pairs={{0,8},{1,121},{8,16},{9,1},{16,24},{17,9},{24,32},{25,17},{32,40},... | collective-permute-start | bytes 786440 | tf_op jit(solution)/shard_map/ppermute | solution.py:180
  61.4 11.6 %collective-permute-start.6 = (bf16[2,512,128]{2,1,0:T(8,128)(2,1)}, bf16[2,512,128]{2,1,0:T(8,128)(2,1)}, u32[]{:S(2)}, u32[]{:S(2)}) collective-permute-start(bf16[2,512,128]{2,1,0:T(8,128)(2,1)} %collective-permute-done.5.refs_5_), channel_id=1, source_target_pairs={{0,8},{1,121},{8,16},{9,1},{16,24},{17,9},{24,32},{25,17},{32,40},... | collective-permute-start | bytes 786440 | tf_op jit(solution)/shard_map/ppermute | solution.py:179
  66.4 9.8 %collective-permute-start.13 = (bf16[2,512,128]{2,1,0:T(8,128)(2,1)}, bf16[2,512,128]{2,1,0:T(8,128)(2,1)}, u32[]{:S(2)}, u32[]{:S(2)}) collective-permute-start(bf16[2,512,128]{2,1,0:T(8,128)(2,1)} %collective-permute-done.12.refs_12_), channel_id=1, source_target_pairs={{0,8},{1,121},{8,16},{9,1},{16,24},{17,9},{24,32},{25,17},{32,40},... | collective-permute-start | bytes 786440 | tf_op jit(solution)/shard_map/ppermute | solution.py:180
  80.7 32.4 %collective-permute-start.18 = (bf16[7,2,256,128]{3,2,1,0:T(8,128)(2,1)}, bf16[7,2,256,128]{3,2,1,0:T(8,128)(2,1)S(1)}, u32[]{:S(2)}, u32[]{:S(2)}) collective-permute-start(bf16[7,2,256,128]{3,2,1,0:T(8,128)(2,1)} %products.2.refs_0_), channel_id=1, source_target_pairs={{0,1},{1,0},{2,3},{3,2},{4,5},{5,4},{6,7},{7,6},{8,9},{9,8},{10,11... | collective-permute-start | bytes 2752520 | tf_op jit(solution)/shard_map/ppermute | solution.py:194
  82.8 9.7 %collective-permute-start.14 = (bf16[2,512,128]{2,1,0:T(8,128)(2,1)}, bf16[2,512,128]{2,1,0:T(8,128)(2,1)S(1)}, u32[]{:S(2)}, u32[]{:S(2)}) collective-permute-start(bf16[2,512,128]{2,1,0:T(8,128)(2,1)} %collective-permute-done.6.refs_6_), channel_id=1, source_target_pairs={{0,8},{1,121},{8,16},{9,1},{16,24},{17,9},{24,32},{25,17},{32,40},... | collective-permute-start | bytes 786440 | tf_op jit(solution)/shard_map/ppermute | solution.py:179
  84.7 10.6 %collective-permute-start.16 = (bf16[2,512,128]{2,1,0:T(8,128)(2,1)}, bf16[2,512,128]{2,1,0:T(8,128)(2,1)S(1)}, u32[]{:S(2)}, u32[]{:S(2)}) collective-permute-start(bf16[2,512,128]{2,1,0:T(8,128)(2,1)} %collective-permute-done.13.refs_13_), channel_id=1, source_target_pairs={{0,8},{1,121},{8,16},{9,1},{16,24},{17,9},{24,32},{25,17},{32,40},... | collective-permute-start | bytes 786440 | tf_op jit(solution)/shard_map/ppermute | solution.py:180
  92.5 3.5 %collective-permute-start.15 = (bf16[2,512,128]{2,1,0:T(8,128)(2,1)S(1)}, bf16[2,512,128]{2,1,0:T(8,128)(2,1)S(1)}, u32[]{:S(2)}, u32[]{:S(2)}) collective-permute-start(bf16[2,512,128]{2,1,0:T(8,128)(2,1)S(1)} %collective-permute-done.14.refs_0_), channel_id=1, source_target_pairs={{1,121},{9,1},{17,9},{25,17},{33,25},{41,33},{49,41},{57,49},{65,5... | collective-permute-start | bytes 786440 | tf_op jit(solution)/shard_map/ppermute | solution.py:179
  95.3 0.7 collective-permute-start.17
  100.0 13.1 %collective-permute-start.19 = (bf16[2,2,256,128]{3,2,1,0:T(8,128)(2,1)}, bf16[2,2,256,128]{3,2,1,0:T(8,128)(2,1)S(1)}, u32[]{:S(2)}, u32[]{:S(2)}) collective-permute-start(bf16[2,2,256,128]{3,2,1,0:T(8,128)(2,1)} %products.3.refs_1_), channel_id=1, source_target_pairs={{0,1},{1,0},{2,3},{3,2},{4,5},{5,4},{6,7},{7,6},{8,9},{9,8},{10,11... | collective-permute-start | bytes 786440 | tf_op jit(solution)/shard_map/ppermute | solution.py:196
  106.4 26.3 %collective-permute-start.20 = (bf16[2,256,128]{2,1,0:T(8,128)(2,1)S(1)}, bf16[2,256,128]{2,1,0:T(8,128)(2,1)S(1)}, u32[]{:S(2)}, u32[]{:S(2)}) collective-permute-start(bf16[2,256,128]{2,1,0:T(8,128)(2,1)S(1)} %dynamic-slice_select_fusion.8), channel_id=1, source_target_pairs={{0,7},{1,0},{8,8},{9,9},{16,16},{17,17},{24,25},{25,26},{34,33},{3... | collective-permute-start | bytes 393224 | tf_op jit(solution)/shard_map/ppermute | solution.py:187
  111.8 22.2 %collective-permute-start.21 = (bf16[2,256,128]{2,1,0:T(8,128)(2,1)S(1)}, bf16[2,256,128]{2,1,0:T(8,128)(2,1)S(1)}, u32[]{:S(2)}, u32[]{:S(2)}) collective-permute-start(bf16[2,256,128]{2,1,0:T(8,128)(2,1)S(1)} %dynamic-slice_select_fusion.7), channel_id=1, source_target_pairs={{0,7},{1,1},{8,15},{9,9},{16,16},{17,18},{24,24},{25,26},{34,33},{... | collective-permute-start | bytes 393224 | tf_op jit(solution)/shard_map/ppermute | solution.py:187
  117.5 24.1 %all-to-all-start.1 = ((bf16[4,2,2,256,128]{4,3,2,1,0:T(8,128)(2,1)}), bf16[4,2,2,256,128]{4,3,2,1,0:T(8,128)(2,1)S(1)}, u32[]{:S(2)}, u32[]{:S(2)}) async-start(bf16[4,2,2,256,128]{4,3,2,1,0:T(8,128)(2,1)} %bitcast.6), calls=%async_computation.1 | async-start | bytes 2097152 | tf_op jit(solution)/shard_map/all_to_all | solution.py:199
  121.3 14.1 %collective-permute-start.22 = (bf16[2,256,128]{2,1,0:T(8,128)(2,1)S(1)}, bf16[2,256,128]{2,1,0:T(8,128)(2,1)S(1)}, u32[]{:S(2)}, u32[]{:S(2)}) collective-permute-start(bf16[2,256,128]{2,1,0:T(8,128)(2,1)S(1)} %dynamic-slice_select_fusion.6), channel_id=1, source_target_pairs={{0,6},{1,1},{8,15},{9,10},{16,23},{17,18},{24,24},{25,27},{34,32},... | collective-permute-start | bytes 393224 | tf_op jit(solution)/shard_map/ppermute | solution.py:187
  126.6 9.4 %collective-permute-start.23 = (bf16[2,256,128]{2,1,0:T(8,128)(2,1)S(1)}, bf16[2,256,128]{2,1,0:T(8,128)(2,1)S(1)}, u32[]{:S(2)}, u32[]{:S(2)}) collective-permute-start(bf16[2,256,128]{2,1,0:T(8,128)(2,1)S(1)} %dynamic-slice_select_fusion.5), channel_id=1, source_target_pairs={{0,6},{1,2},{8,14},{9,10},{16,23},{17,19},{24,31},{25,27},{34,32},... | collective-permute-start | bytes 393224 | tf_op jit(solution)/shard_map/ppermute | solution.py:187
  129.1 7.3 %collective-permute-start.24 = (bf16[2,256,128]{2,1,0:T(8,128)(2,1)S(1)}, bf16[2,256,128]{2,1,0:T(8,128)(2,1)S(1)}, u32[]{:S(2)}, u32[]{:S(2)}) collective-permute-start(bf16[2,256,128]{2,1,0:T(8,128)(2,1)S(1)} %dynamic-slice_select_fusion.4), channel_id=1, source_target_pairs={{0,5},{1,2},{8,14},{9,11},{16,22},{17,19},{24,31},{25,28},{34,39},... | collective-permute-start | bytes 393224 | tf_op jit(solution)/shard_map/ppermute | solution.py:187
  132.7 6.6 %collective-permute-start.25 = (bf16[2,256,128]{2,1,0:T(8,128)(2,1)S(1)}, bf16[2,256,128]{2,1,0:T(8,128)(2,1)S(1)}, u32[]{:S(2)}, u32[]{:S(2)}) collective-permute-start(bf16[2,256,128]{2,1,0:T(8,128)(2,1)S(1)} %dynamic-slice_select_fusion.3), channel_id=1, source_target_pairs={{0,5},{1,3},{8,13},{9,11},{16,22},{17,20},{24,30},{25,28},{34,39},... | collective-permute-start | bytes 393224 | tf_op jit(solution)/shard_map/ppermute | solution.py:187
  134.0 7.6 %collective-permute-start.26 = (bf16[2,256,128]{2,1,0:T(8,128)(2,1)S(1)}, bf16[2,256,128]{2,1,0:T(8,128)(2,1)S(1)}, u32[]{:S(2)}, u32[]{:S(2)}) collective-permute-start(bf16[2,256,128]{2,1,0:T(8,128)(2,1)S(1)} %dynamic-slice_select_fusion.2), channel_id=1, source_target_pairs={{0,4},{1,3},{8,13},{9,12},{16,21},{17,20},{24,30},{25,29},{34,38},... | collective-permute-start | bytes 393224 | tf_op jit(solution)/shard_map/ppermute | solution.py:187
  135.3 6.2 %collective-permute-start.27 = (bf16[2,256,128]{2,1,0:T(8,128)(2,1)S(1)}, bf16[2,256,128]{2,1,0:T(8,128)(2,1)S(1)}, u32[]{:S(2)}, u32[]{:S(2)}) collective-permute-start(bf16[2,256,128]{2,1,0:T(8,128)(2,1)S(1)} %fusion), channel_id=1, source_target_pairs={{0,0},{1,4},{8,8},{9,12},{16,17},{17,21},{24,25},{25,29},{34,34},{... | collective-permute-start | bytes 393224 | tf_op jit(solution)/shard_map/ppermute | solution.py:187
  (38 other events, 317.7 us)

commit v2 on v1

--- a/solution.py
+++ b/solution.py
@@ -103,31 +103,23 @@
 
 def finish(pos, arrived, pieces):
     peers, halves, fronts, rows, cols = arrived.shape
-    count = len(pieces)
-
-    def body(pos_ref, a_ref, *refs):
-        gs, (x_ref, d_ref, low_ref) = refs[:count], refs[count:]
-        w, n = pos_ref[0], pos_ref[1]
+
+    def body(pos_ref, a_ref, g_ref, x_ref, d_ref):
+        w = pos_ref[0]
         for m in range(fronts):
+            lows = []
             for h in range(halves):
                 total = a_ref[0, h, m].astype(jnp.float32)
                 for s in range(1, peers):
                     total = total + a_ref[s, h, m].astype(jnp.float32)
                 cross = -total
                 x_ref[m, h * cols : (h + 1) * cols, :] = cross.T
-                low_ref[m, :, h * cols : (h + 1) * cols] = cross.astype(jnp.bfloat16)
-        for at, g_ref in enumerate(gs):
-            step = at + 1
-            down = (w - step % 8) & 15
-            up = (w + step) & 15
-            first = (down >> 1) == n
-            half = jnp.where(first, down & 1, up & 1)
-
-            @pl.when(jnp.logical_or(first, (up >> 1) == n))
-            def _():
-                for m in range(fronts):
-                    site = jnp.dot(g_ref[m].T, low_ref[m], preferred_element_type=jnp.float32)
-                    d_ref[pl.ds(half * 8, 8), m] = site.astype(jnp.bfloat16).reshape(8, 16, halves * cols)
+                lows.append(cross.astype(jnp.bfloat16))
+            low = jnp.concatenate(lows, axis=1)
+            for t in range(2):
+                half = (w + t) & 1
+                site = jnp.dot(g_ref[t, m].T, low, preferred_element_type=jnp.float32)
+                d_ref[pl.ds(half * 8, 8), m] = site.astype(jnp.bfloat16).reshape(8, 16, halves * cols)
 
     return pl.pallas_call(
         body,
@@ -135,11 +127,10 @@
             jax.ShapeDtypeStruct((fronts, halves * cols, rows), jnp.float32),
             jax.ShapeDtypeStruct((16, fronts, 16, halves * cols), jnp.bfloat16),
         ),
-        in_specs=[pl.BlockSpec(memory_space=pltpu.SMEM)] + [WHOLE] * (1 + count),
+        in_specs=[pl.BlockSpec(memory_space=pltpu.SMEM)] + [WHOLE] * 2,
         out_specs=(WHOLE, WHOLE),
-        scratch_shapes=[pltpu.VMEM((fronts, rows, halves * cols), jnp.bfloat16)],
         name="finish",
-    )(pos, arrived, *pieces)
+    )(pos, arrived, pieces)
 
 
 def ring_pairs(cores):
@@ -152,12 +143,17 @@
     return pairs
 
 
-def piece_pairs(step):
+def turn_pairs(way):
+    return [(4 * i + y, 4 * i + (y + way * (i // 4)) % 4) for i in range(16) for y in range(4)]
+
+
+def block_pairs(t):
     pairs = []
     for i in range(16):
-        down, up = (i - step % 8) % 16, (i + step) % 16
-        pairs.append((8 * i + 2 * (i // 4), 8 * i + down // 2))
-        pairs.append((8 * i + 2 * (i // 4) + 1, 8 * i + up // 2))
+        for y in range(4):
+            for c in range(2):
+                to = 4 * ((y - i // 4) % 4) + 2 * c + (i + t) % 2
+                pairs.append((8 * i + 2 * y + c, 8 * to + 2 * y + (i // 2) % 2))
     return pairs
 
 
@@ -172,19 +168,17 @@
     owns = [gain]
     others = [lax.ppermute(gain, "core", swap)]
     rows = gain.shape[1] // 2
-    near = (w >> 1) & 1 == core
-    pieces = []
+    turned_gain = lax.ppermute(gain, ("wide", "y"), turn_pairs(1))
+    blocks = []
+    for t in range(2):
+        half = lax.dynamic_slice_in_dim(turned_gain, ((w + t) & 1) * rows, rows, 1)
+        blocks.append(lax.ppermute(half, ("wide", "y", "core"), block_pairs(t)))
+    blocks = jnp.stack(blocks)
+    pieces = lax.ppermute(blocks, ("wide", "y"), turn_pairs(-1))
     for step in range(1, 9):
         pairs = ring_pairs((0, 1) if step < 8 else (1,))
         owns.append(lax.ppermute(owns[-1], ("wide", "core"), pairs))
         others.append(lax.ppermute(others[-1], ("wide", "core"), pairs))
-        a, b = owns[step], others[step]
-        if step == 8:
-            a = jnp.where(core == 0, owns[0], a)
-            b = jnp.where(core == 0, others[0], b)
-        held = jnp.where(near, a, b)
-        piece = lax.dynamic_slice_in_dim(held, (w & 1) * rows, rows, 1)
-        pieces.append(lax.ppermute(piece, ("wide", "y", "core"), piece_pairs(step)))
         if step == 1:
             arrived = lax.all_to_all(ancestor_cov, NARROW, split_axis=0, concat_axis=0, tiled=True)
             paired = lax.ppermute(arrived, "core", swap)

time: 177 us -> 191 us (1.079)
  the two profiles are of different devices: /device:TPU:4 before, /device:TPU:44 now
where the time goes in v2:
time: 191 us; the launch traced here: 190 us
  starting transfers between devices  72.7 us (38%)
  waiting for transfers between devices  53.9 us (28%)
  blocking collectives  38.1 us (20%)
  Pallas kernels  15.3 us (8%)
  local copies, waits for them, and re-layouts  7.18 us (4%)
    all_to_all x1, blocking collectives, level(): sums = lax.all_to_all(site, 'wide', split_axis=0, concat_axis=0, tiled=True)  38.1 us
    ppermute x2, waiting for transfers between devices, level(): blocks.append(lax.ppermute(half, ('wide', 'y', 'core'), block_pairs(t)))  19.2 us
    ppermute x8, waiting for transfers between devices, level(): owns.append(lax.ppermute(owns[-1], ('wide', 'core'), pairs))  19 us
    ppermute x8, starting transfers between devices, level(): owns.append(lax.ppermute(owns[-1], ('wide', 'core'), pairs))  18.6 us
    ppermute x8, starting transfers between devices, level(): others.append(lax.ppermute(others[-1], ('wide', 'core'), pairs))  18.3 us
    ppermute x8, waiting for transfers between devices, level(): others.append(lax.ppermute(others[-1], ('wide', 'core'), pairs))  15.1 us
    ppermute x2, starting transfers between devices, level(): blocks.append(lax.ppermute(half, ('wide', 'y', 'core'), block_pairs(t)))  9.5 us
    ppermute x1, starting transfers between devices, level(): theirs.append(lax.ppermute(mine[1], 'core', swap))  8.13 us
  transfers between devices with their start and end apart: 26, of which 14 were waited for; matrix products, arithmetic and copies ran while one was open for 0% of the time, Pallas kernels for 4%

profile of v2, /device:TPU:44, one launch (start us, length us, event | category | flops | bytes accessed | tf_op | source)
XLA Modules:
  0.0 189.6 jit_solution(7585623378246588642)
XLA Ops:
  0.6 5.1 %all-to-all-start = ((bf16[8,128,512]{2,1,0:T(8,128)(2,1)}), bf16[8,128,512]{2,1,0:T(8,128)(2,1)S(1)}, u32[]{:S(2)}, u32[]{:S(2)}) async-start(bf16[8,128,512]{2,1,0:T(8,128)(2,1)} %param.7), calls=%async_computation | async-start | bytes 2097152 | tf_op jit(solution)/shard_map/all_to_all | solution.py:183
  5.7 2.0 %collective-permute-start.7 = (bf16[2,512,128]{2,1,0:T(8,128)(2,1)S(1)}, bf16[2,512,128]{2,1,0:T(8,128)(2,1)S(1)}, u32[]{:S(2)}, u32[]{:S(2)}) collective-permute-start(bf16[2,512,128]{2,1,0:T(8,128)(2,1)S(1)} %copy-done.4), channel_id=1, source_target_pairs={{0,1},{1,0},{2,3},{3,2},{4,5},{5,4},{6,7},{7,6},{8,9},{9,8},{10,11... | collective-permute-start | bytes 786440 | tf_op jit(solution)/shard_map/ppermute | solution.py:169
  7.7 3.8 %collective-permute-start.1 = (bf16[2,512,128]{2,1,0:T(8,128)(2,1)S(1)}, bf16[2,512,128]{2,1,0:T(8,128)(2,1)S(1)}, u32[]{:S(2)}, u32[]{:S(2)}) collective-permute-start(bf16[2,512,128]{2,1,0:T(8,128)(2,1)S(1)} %copy-done.4), channel_id=1, source_target_pairs={{0,8},{1,121},{8,16},{9,1},{16,24},{17,9},{24,32},{25,17},{32,40},... | collective-permute-start | bytes 786440 | tf_op jit(solution)/shard_map/ppermute | solution.py:180
  11.6 3.8 %collective-permute-start.8 = (bf16[2,512,128]{2,1,0:T(8,128)(2,1)S(1)}, bf16[2,512,128]{2,1,0:T(8,128)(2,1)S(1)}, u32[]{:S(2)}, u32[]{:S(2)}) collective-permute-start(bf16[2,512,128]{2,1,0:T(8,128)(2,1)S(1)} %collective-permute-done.7.refs_7_), channel_id=1, source_target_pairs={{0,8},{1,121},{8,16},{9,1},{16,24},{17,9},{24,32},{25,17},{32,40},... | collective-permute-start | bytes 786440 | tf_op jit(solution)/shard_map/ppermute | solution.py:181
  16.0 4.5 %collective-permute-start.2 = (bf16[2,512,128]{2,1,0:T(8,128)(2,1)S(1)}, bf16[2,512,128]{2,1,0:T(8,128)(2,1)S(1)}, u32[]{:S(2)}, u32[]{:S(2)}) collective-permute-start(bf16[2,512,128]{2,1,0:T(8,128)(2,1)S(1)} %collective-permute-done.1.refs_1_), channel_id=1, source_target_pairs={{0,8},{1,121},{8,16},{9,1},{16,24},{17,9},{24,32},{25,17},{32,40},... | collective-permute-start | bytes 786440 | tf_op jit(solution)/shard_map/ppermute | solution.py:180
  20.5 3.8 %collective-permute-start.9 = (bf16[2,512,128]{2,1,0:T(8,128)(2,1)S(1)}, bf16[2,512,128]{2,1,0:T(8,128)(2,1)S(1)}, u32[]{:S(2)}, u32[]{:S(2)}) collective-permute-start(bf16[2,512,128]{2,1,0:T(8,128)(2,1)S(1)} %collective-permute-done.8.refs_8_), channel_id=1, source_target_pairs={{0,8},{1,121},{8,16},{9,1},{16,24},{17,9},{24,32},{25,17},{32,40},... | collective-permute-start | bytes 786440 | tf_op jit(solution)/shard_map/ppermute | solution.py:181
  24.3 5.5 %collective-permute-done.2.refs_2_ = bf16[2,512,128]{2,1,0:T(8,128)(2,1)S(1)} collective-permute-done((bf16[2,512,128]{2,1,0:T(8,128)(2,1)S(1)}, bf16[2,512,128]{2,1,0:T(8,128)(2,1)S(1)}, u32[]{:S(2)}, u32[]{:S(2)}) %collective-permute-start.2) | collective-permute-done | bytes 262176 | tf_op jit(solution)/shard_map/ppermute | solution.py:180
  31.8 2.8 %collective-permute-start = (bf16[8,128,512]{2,1,0:T(8,128)(2,1)S(1)}, bf16[8,128,512]{2,1,0:T(8,128)(2,1)S(1)}, u32[]{:S(2)}, u32[]{:S(2)}) collective-permute-start(bf16[8,128,512]{2,1,0:T(8,128)(2,1)S(1)} %all-to-all-done.own_ref), channel_id=1, source_target_pairs={{0,1},{1,0},{2,3},{3,2},{4,5},{5,4},{6,7},{7,6},{8,9},{9,8},{10,11... | collective-permute-start | bytes 3145736 | tf_op jit(solution)/shard_map/ppermute | solution.py:184
  34.6 2.3 %collective-permute-start.10 = (bf16[2,512,128]{2,1,0:T(8,128)(2,1)S(1)}, bf16[2,512,128]{2,1,0:T(8,128)(2,1)S(1)}, u32[]{:S(2)}, u32[]{:S(2)}) collective-permute-start(bf16[2,512,128]{2,1,0:T(8,128)(2,1)S(1)} %collective-permute-done.9.refs_9_), channel_id=1, source_target_pairs={{0,8},{1,121},{8,16},{9,1},{16,24},{17,9},{24,32},{25,17},{32,40},... | collective-permute-start | bytes 786440 | tf_op jit(solution)/shard_map/ppermute | solution.py:181
  36.9 2.5 %collective-permute-done.3.refs_3_ = bf16[2,512,128]{2,1,0:T(8,128)(2,1)} collective-permute-done((bf16[2,512,128]{2,1,0:T(8,128)(2,1)S(1)}, bf16[2,512,128]{2,1,0:T(8,128)(2,1)}, u32[]{:S(2)}, u32[]{:S(2)}) %collective-permute-start.3) | collective-permute-done | bytes 262176 | tf_op jit(solution)/shard_map/ppermute | solution.py:180
  39.4 1.9 %collective-permute-start.4 = (bf16[2,512,128]{2,1,0:T(8,128)(2,1)}, bf16[2,512,128]{2,1,0:T(8,128)(2,1)S(1)}, u32[]{:S(2)}, u32[]{:S(2)}) collective-permute-start(bf16[2,512,128]{2,1,0:T(8,128)(2,1)} %collective-permute-done.3.refs_3_), channel_id=1, source_target_pairs={{0,8},{1,121},{8,16},{9,1},{16,24},{17,9},{24,32},{25,17},{32,40},... | collective-permute-start | bytes 786440 | tf_op jit(solution)/shard_map/ppermute | solution.py:180
  41.4 2.9 %collective-permute-done.10.refs_10_ = bf16[2,512,128]{2,1,0:T(8,128)(2,1)S(1)} collective-permute-done((bf16[2,512,128]{2,1,0:T(8,128)(2,1)S(1)}, bf16[2,512,128]{2,1,0:T(8,128)(2,1)S(1)}, u32[]{:S(2)}, u32[]{:S(2)}) %collective-permute-start.10) | collective-permute-done | bytes 262176 | tf_op jit(solution)/shard_map/ppermute | solution.py:181
  46.8 2.2 %collective-permute-done.4.refs_4_ = bf16[2,512,128]{2,1,0:T(8,128)(2,1)S(1)} collective-permute-done((bf16[2,512,128]{2,1,0:T(8,128)(2,1)}, bf16[2,512,128]{2,1,0:T(8,128)(2,1)S(1)}, u32[]{:S(2)}, u32[]{:S(2)}) %collective-permute-start.4) | collective-permute-done | bytes 262176 | tf_op jit(solution)/shard_map/ppermute | solution.py:180
  51.0 3.4 %collective-permute-done.11.refs_11_ = bf16[2,512,128]{2,1,0:T(8,128)(2,1)S(1)} collective-permute-done((bf16[2,512,128]{2,1,0:T(8,128)(2,1)S(1)}, bf16[2,512,128]{2,1,0:T(8,128)(2,1)S(1)}, u32[]{:S(2)}, u32[]{:S(2)}) %collective-permute-start.11) | collective-permute-done | bytes 262176 | tf_op jit(solution)/shard_map/ppermute | solution.py:181
  56.3 2.3 %collective-permute-done.5.refs_5_ = bf16[2,512,128]{2,1,0:T(8,128)(2,1)} collective-permute-done((bf16[2,512,128]{2,1,0:T(8,128)(2,1)S(1)}, bf16[2,512,128]{2,1,0:T(8,128)(2,1)}, u32[]{:S(2)}, u32[]{:S(2)}) %collective-permute-start.5) | collective-permute-done | bytes 262176 | tf_op jit(solution)/shard_map/ppermute | solution.py:180
  60.6 3.4 %collective-permute-done.12.refs_12_ = bf16[2,512,128]{2,1,0:T(8,128)(2,1)} collective-permute-done((bf16[2,512,128]{2,1,0:T(8,128)(2,1)S(1)}, bf16[2,512,128]{2,1,0:T(8,128)(2,1)}, u32[]{:S(2)}, u32[]{:S(2)}) %collective-permute-start.12) | collective-permute-done | bytes 262176 | tf_op jit(solution)/shard_map/ppermute | solution.py:181
  67.5 2.9 %turned.1.left_ref = bf16[2,256,1024]{2,1,0:T(8,128)(2,1)} custom-call(s32[2,32]{1,0:T(2,128)} %bnd_ref.1, s32[64]{0:T(128)} %owner_ref.1, s32[3]{0:T(128)} %pad_add_fusion.pos_ref, bf16[8,128,512]{2,1,0:T(8,128)(2,1)} %copy-done.1, bf16[8,128,512]{2,1,0:T(8,128)(2,1)} %copy-done.2), custom_call_target="tpu_custom_call" | custom-call | tf_op jit(solution)/shard_map/turned/pallas_call | solution.py:33
  70.5 3.3 %collective-permute-done.13.refs_13_ = bf16[2,512,128]{2,1,0:T(8,128)(2,1)} collective-permute-done((bf16[2,512,128]{2,1,0:T(8,128)(2,1)}, bf16[2,512,128]{2,1,0:T(8,128)(2,1)}, u32[]{:S(2)}, u32[]{:S(2)}) %collective-permute-start.13) | collective-permute-done | bytes 262176 | tf_op jit(solution)/shard_map/ppermute | solution.py:181
  73.8 4.5 %products.2.refs_0_ = bf16[7,2,256,128]{3,2,1,0:T(8,128)(2,1)} custom-call(bf16[2,256,1024]{2,1,0:T(8,128)(2,1)} %turned.1.left_ref, bf16[2,512,128]{2,1,0:T(8,128)(2,1)} %refs_0_.1, bf16[2,512,128]{2,1,0:T(8,128)(2,1)} %copy-done.7, bf16[2,512,128]{2,1,0:T(8,128)(2,1)} %copy-done.9, bf16[2,512,128]{2,1,0:T(8,128)(2,1)} %collective-permute-done.3.refs_3_, ...), custom_call_target="tpu_custom_call" | custom-call | flops 939524096 | bytes 7340032 | tf_op jit(solution)/shard_map/products/pallas_call | solution.py:60
  78.2 2.0 %collective-permute-start.18 = (bf16[7,2,256,128]{3,2,1,0:T(8,128)(2,1)}, bf16[7,2,256,128]{3,2,1,0:T(8,128)(2,1)S(1)}, u32[]{:S(2)}, u32[]{:S(2)}) collective-permute-start(bf16[7,2,256,128]{3,2,1,0:T(8,128)(2,1)} %products.2.refs_0_), channel_id=1, source_target_pairs={{0,1},{1,0},{2,3},{3,2},{4,5},{5,4},{6,7},{7,6},{8,9},{9,8},{10,11... | collective-permute-start | bytes 2752520 | tf_op jit(solution)/shard_map/ppermute | solution.py:188
  84.1 5.8 %collective-permute-done.14.refs_0_ = bf16[2,512,128]{2,1,0:T(8,128)(2,1)S(1)} collective-permute-done((bf16[2,512,128]{2,1,0:T(8,128)(2,1)}, bf16[2,512,128]{2,1,0:T(8,128)(2,1)S(1)}, u32[]{:S(2)}, u32[]{:S(2)}) %collective-permute-start.14) | collective-permute-done | bytes 262176 | tf_op jit(solution)/shard_map/ppermute | solution.py:180
  90.6 2.1 %collective-permute-done.16.refs_2_ = bf16[2,512,128]{2,1,0:T(8,128)(2,1)S(1)} collective-permute-done((bf16[2,512,128]{2,1,0:T(8,128)(2,1)}, bf16[2,512,128]{2,1,0:T(8,128)(2,1)S(1)}, u32[]{:S(2)}, u32[]{:S(2)}) %collective-permute-start.16) | collective-permute-done | bytes 262176 | tf_op jit(solution)/shard_map/ppermute | solution.py:181
  94.9 2.6 %products.3.refs_1_ = bf16[2,2,256,128]{3,2,1,0:T(8,128)(2,1)} custom-call(bf16[2,256,1024]{2,1,0:T(8,128)(2,1)} %turned.1.left_ref, bf16[2,512,128]{2,1,0:T(8,128)(2,1)} %copy-done.14, bf16[2,512,128]{2,1,0:T(8,128)(2,1)} %copy-done.16, bf16[2,512,128]{2,1,0:T(8,128)(2,1)} %copy-done.15, bf16[2,512,128]{2,1,0:T(8,128)(2,1)} %copy-done.19), custom_call_target="tpu_custom_call" | custom-call | flops 268435456 | bytes 2097152 | tf_op jit(solution)/shard_map/products/pallas_call | solution.py:60
  97.5 8.1 %collective-permute-start.19 = (bf16[2,2,256,128]{3,2,1,0:T(8,128)(2,1)}, bf16[2,2,256,128]{3,2,1,0:T(8,128)(2,1)S(1)}, u32[]{:S(2)}, u32[]{:S(2)}) collective-permute-start(bf16[2,2,256,128]{3,2,1,0:T(8,128)(2,1)} %products.3.refs_1_), channel_id=1, source_target_pairs={{0,1},{1,0},{2,3},{3,2},{4,5},{5,4},{6,7},{7,6},{8,9},{9,8},{10,11... | collective-permute-start | bytes 786440 | tf_op jit(solution)/shard_map/ppermute | solution.py:190
  108.6 2.8 %assemble.1 = bf16[8,2,256,128]{3,2,1,0:T(8,128)(2,1)} custom-call(s32[3]{0:T(128)} %pad_add_fusion.pos_ref, bf16[7,2,256,128]{3,2,1,0:T(8,128)(2,1)} %products.2.refs_0_, bf16[2,2,256,128]{3,2,1,0:T(8,128)(2,1)} %products.3.refs_1_, bf16[7,2,256,128]{3,2,1,0:T(8,128)(2,1)} %copy-done.3, bf16[2,2,256,128]{3,2,1,0:T(8,128)(2,1)} %copy-done.17), custom_call_target="tpu_custom_call" | custom-call | tf_op jit(solution)/shard_map/assemble/pallas_call | solution.py:95
  111.4 4.9 %all-to-all-start.1 = ((bf16[4,2,2,256,128]{4,3,2,1,0:T(8,128)(2,1)}), bf16[4,2,2,256,128]{4,3,2,1,0:T(8,128)(2,1)S(1)}, u32[]{:S(2)}, u32[]{:S(2)}) async-start(bf16[4,2,2,256,128]{4,3,2,1,0:T(8,128)(2,1)} %bitcast.8), calls=%async_computation.1 | async-start | bytes 2097152 | tf_op jit(solution)/shard_map/all_to_all | solution.py:193
  116.4 4.7 %collective-permute-start.21 = (bf16[2,256,128]{2,1,0:T(8,128)(2,1)S(1)}, bf16[2,256,128]{2,1,0:T(8,128)(2,1)S(1)}, u32[]{:S(2)}, u32[]{:S(2)}) collective-permute-start(bf16[2,256,128]{2,1,0:T(8,128)(2,1)S(1)} %get-tuple-element.6), channel_id=1, source_target_pairs={{0,0},{1,16},{2,34},{3,50},{4,68},{5,84},{6,102},{7,118},{8,8},{9,... | collective-permute-start | bytes 393224 | tf_op jit(solution)/shard_map/ppermute | solution.py:175
  121.1 4.8 %collective-permute-start.22 = (bf16[2,256,128]{2,1,0:T(8,128)(2,1)S(1)}, bf16[2,256,128]{2,1,0:T(8,128)(2,1)S(1)}, u32[]{:S(2)}, u32[]{:S(2)}) collective-permute-start(bf16[2,256,128]{2,1,0:T(8,128)(2,1)S(1)} %get-tuple-element.7), channel_id=1, source_target_pairs={{0,8},{1,24},{2,42},{3,58},{4,76},{5,92},{6,110},{7,126},{8,0},{9,... | collective-permute-start | bytes 393224 | tf_op jit(solution)/shard_map/ppermute | solution.py:175
  125.9 12.5 %collective-permute-done.21 = bf16[2,256,128]{2,1,0:T(8,128)(2,1)S(1)} collective-permute-done((bf16[2,256,128]{2,1,0:T(8,128)(2,1)S(1)}, bf16[2,256,128]{2,1,0:T(8,128)(2,1)S(1)}, u32[]{:S(2)}, u32[]{:S(2)}) %collective-permute-start.21) | collective-permute-done | bytes 131104 | tf_op jit(solution)/shard_map/ppermute | solution.py:175
  138.5 6.7 %collective-permute-done.22 = bf16[2,256,128]{2,1,0:T(8,128)(2,1)S(1)} collective-permute-done((bf16[2,256,128]{2,1,0:T(8,128)(2,1)S(1)}, bf16[2,256,128]{2,1,0:T(8,128)(2,1)S(1)}, u32[]{:S(2)}, u32[]{:S(2)}) %collective-permute-start.22) | collective-permute-done | bytes 131104 | tf_op jit(solution)/shard_map/ppermute | solution.py:175
  147.6 2.5 %finish.1 = (f32[2,256,256]{2,1,0:T(8,128)}, bf16[16,2,16,256]{3,2,1,0:T(8,128)(2,1)}) custom-call(s32[3]{0:T(128)} %pad_add_fusion.pos_ref, bf16[4,2,2,256,128]{4,3,2,1,0:T(8,128)(2,1)} %copy-done, bf16[2,2,256,128]{3,2,1,0:T(8,128)(2,1)} %copy-done.18), custom_call_target="tpu_custom_call" | custom-call | tf_op jit(solution)/shard_map/finish/pallas_call | solution.py:124
  150.1 38.1 %all_to_all.15 = bf16[16,2,16,256]{3,2,1,0:T(8,128)(2,1)S(1)} all-to-all(bf16[16,2,16,256]{3,2,1,0:T(8,128)(2,1)} %get-tuple-element.5), channel_id=1, replica_groups=mesh['front'=4,'wide'=16,'y'=4,'core'=2] {'wide'}, dimensions={0} | all-to-all | bytes 524288 | tf_op jit(solution)/shard_map/all_to_all | solution.py:196
  (73 shorter events, 27.7 us)
Async XLA Ops:
  0.6 31.1 %all-to-all-start = ((bf16[8,128,512]{2,1,0:T(8,128)(2,1)}), bf16[8,128,512]{2,1,0:T(8,128)(2,1)S(1)}, u32[]{:S(2)}, u32[]{:S(2)}) async-start(bf16[8,128,512]{2,1,0:T(8,128)(2,1)} %param.7), calls=%async_computation | async-start | bytes 2097152 | tf_op jit(solution)/shard_map/all_to_all | solution.py:183
  5.7 5.9 %collective-permute-start.7 = (bf16[2,512,128]{2,1,0:T(8,128)(2,1)S(1)}, bf16[2,512,128]{2,1,0:T(8,128)(2,1)S(1)}, u32[]{:S(2)}, u32[]{:S(2)}) collective-permute-start(bf16[2,512,128]{2,1,0:T(8,128)(2,1)S(1)} %copy-done.4), channel_id=1, source_target_pairs={{0,1},{1,0},{2,3},{3,2},{4,5},{5,4},{6,7},{7,6},{8,9},{9,8},{10,11... | collective-permute-start | bytes 786440 | tf_op jit(solution)/shard_map/ppermute | solution.py:169
  7.7 8.3 %collective-permute-start.1 = (bf16[2,512,128]{2,1,0:T(8,128)(2,1)S(1)}, bf16[2,512,128]{2,1,0:T(8,128)(2,1)S(1)}, u32[]{:S(2)}, u32[]{:S(2)}) collective-permute-start(bf16[2,512,128]{2,1,0:T(8,128)(2,1)S(1)} %copy-done.4), channel_id=1, source_target_pairs={{0,8},{1,121},{8,16},{9,1},{16,24},{17,9},{24,32},{25,17},{32,40},... | collective-permute-start | bytes 786440 | tf_op jit(solution)/shard_map/ppermute | solution.py:180
  11.6 58.9 %copy-start.6 = (bf16[2,512,128]{2,1,0:T(8,128)(2,1)}, bf16[2,512,128]{2,1,0:T(8,128)(2,1)S(1)}, u32[]{:S(2)}) copy-start(bf16[2,512,128]{2,1,0:T(8,128)(2,1)S(1)} %collective-permute-done.7.refs_7_) | copy-start | bytes 786436
  11.6 8.9 %collective-permute-start.8 = (bf16[2,512,128]{2,1,0:T(8,128)(2,1)S(1)}, bf16[2,512,128]{2,1,0:T(8,128)(2,1)S(1)}, u32[]{:S(2)}, u32[]{:S(2)}) collective-permute-start(bf16[2,512,128]{2,1,0:T(8,128)(2,1)S(1)} %collective-permute-done.7.refs_7_), channel_id=1, source_target_pairs={{0,8},{1,121},{8,16},{9,1},{16,24},{17,9},{24,32},{25,17},{32,40},... | collective-permute-start | bytes 786440 | tf_op jit(solution)/shard_map/ppermute | solution.py:181
  16.0 54.4 %copy-start.7 = (bf16[2,512,128]{2,1,0:T(8,128)(2,1)}, bf16[2,512,128]{2,1,0:T(8,128)(2,1)S(1)}, u32[]{:S(2)}) copy-start(bf16[2,512,128]{2,1,0:T(8,128)(2,1)S(1)} %collective-permute-done.1.refs_1_) | copy-start | bytes 786436
  16.0 13.8 %collective-permute-start.2 = (bf16[2,512,128]{2,1,0:T(8,128)(2,1)S(1)}, bf16[2,512,128]{2,1,0:T(8,128)(2,1)S(1)}, u32[]{:S(2)}, u32[]{:S(2)}) collective-permute-start(bf16[2,512,128]{2,1,0:T(8,128)(2,1)S(1)} %collective-permute-done.1.refs_1_), channel_id=1, source_target_pairs={{0,8},{1,121},{8,16},{9,1},{16,24},{17,9},{24,32},{25,17},{32,40},... | collective-permute-start | bytes 786440 | tf_op jit(solution)/shard_map/ppermute | solution.py:180
  20.5 49.9 %copy-start.8 = (bf16[2,512,128]{2,1,0:T(8,128)(2,1)}, bf16[2,512,128]{2,1,0:T(8,128)(2,1)S(1)}, u32[]{:S(2)}) copy-start(bf16[2,512,128]{2,1,0:T(8,128)(2,1)S(1)} %collective-permute-done.8.refs_8_) | copy-start | bytes 786436
  20.5 14.0 %collective-permute-start.9 = (bf16[2,512,128]{2,1,0:T(8,128)(2,1)S(1)}, bf16[2,512,128]{2,1,0:T(8,128)(2,1)S(1)}, u32[]{:S(2)}, u32[]{:S(2)}) collective-permute-start(bf16[2,512,128]{2,1,0:T(8,128)(2,1)S(1)} %collective-permute-done.8.refs_8_), channel_id=1, source_target_pairs={{0,8},{1,121},{8,16},{9,1},{16,24},{17,9},{24,32},{25,17},{32,40},... | collective-permute-start | bytes 786440 | tf_op jit(solution)/shard_map/ppermute | solution.py:181
  29.8 40.6 %copy-start.9 = (bf16[2,512,128]{2,1,0:T(8,128)(2,1)}, bf16[2,512,128]{2,1,0:T(8,128)(2,1)S(1)}, u32[]{:S(2)}) copy-start(bf16[2,512,128]{2,1,0:T(8,128)(2,1)S(1)} %collective-permute-done.2.refs_2_) | copy-start | bytes 786436
  29.8 9.6 %collective-permute-start.3 = (bf16[2,512,128]{2,1,0:T(8,128)(2,1)S(1)}, bf16[2,512,128]{2,1,0:T(8,128)(2,1)}, u32[]{:S(2)}, u32[]{:S(2)}) collective-permute-start(bf16[2,512,128]{2,1,0:T(8,128)(2,1)S(1)} %collective-permute-done.2.refs_2_), channel_id=1, source_target_pairs={{0,8},{1,121},{8,16},{9,1},{16,24},{17,9},{24,32},{25,17},{32,40},... | collective-permute-start | bytes 786440 | tf_op jit(solution)/shard_map/ppermute | solution.py:180
  31.8 34.8 %copy-start.1 = (bf16[8,128,512]{2,1,0:T(8,128)(2,1)}, bf16[8,128,512]{2,1,0:T(8,128)(2,1)S(1)}, u32[]{:S(2)}) copy-start(bf16[8,128,512]{2,1,0:T(8,128)(2,1)S(1)} %all-to-all-done.own_ref) | copy-start | bytes 3145732
  31.8 34.8 %collective-permute-start = (bf16[8,128,512]{2,1,0:T(8,128)(2,1)S(1)}, bf16[8,128,512]{2,1,0:T(8,128)(2,1)S(1)}, u32[]{:S(2)}, u32[]{:S(2)}) collective-permute-start(bf16[8,128,512]{2,1,0:T(8,128)(2,1)S(1)} %all-to-all-done.own_ref), channel_id=1, source_target_pairs={{0,1},{1,0},{2,3},{3,2},{4,5},{5,4},{6,7},{7,6},{8,9},{9,8},{10,11... | collective-permute-start | bytes 3145736 | tf_op jit(solution)/shard_map/ppermute | solution.py:184
  34.5 35.9 %copy-start.10 = (bf16[2,512,128]{2,1,0:T(8,128)(2,1)}, bf16[2,512,128]{2,1,0:T(8,128)(2,1)S(1)}, u32[]{:S(2)}) copy-start(bf16[2,512,128]{2,1,0:T(8,128)(2,1)S(1)} %collective-permute-done.9.refs_9_) | copy-start | bytes 786436
  34.6 9.6 %collective-permute-start.10 = (bf16[2,512,128]{2,1,0:T(8,128)(2,1)S(1)}, bf16[2,512,128]{2,1,0:T(8,128)(2,1)S(1)}, u32[]{:S(2)}, u32[]{:S(2)}) collective-permute-start(bf16[2,512,128]{2,1,0:T(8,128)(2,1)S(1)} %collective-permute-done.9.refs_9_), channel_id=1, source_target_pairs={{0,8},{1,121},{8,16},{9,1},{16,24},{17,9},{24,32},{25,17},{32,40},... | collective-permute-start | bytes 786440 | tf_op jit(solution)/shard_map/ppermute | solution.py:181
  39.4 9.7 %collective-permute-start.4 = (bf16[2,512,128]{2,1,0:T(8,128)(2,1)}, bf16[2,512,128]{2,1,0:T(8,128)(2,1)S(1)}, u32[]{:S(2)}, u32[]{:S(2)}) collective-permute-start(bf16[2,512,128]{2,1,0:T(8,128)(2,1)} %collective-permute-done.3.refs_3_), channel_id=1, source_target_pairs={{0,8},{1,121},{8,16},{9,1},{16,24},{17,9},{24,32},{25,17},{32,40},... | collective-permute-start | bytes 786440 | tf_op jit(solution)/shard_map/ppermute | solution.py:180
  44.9 9.5 %collective-permute-start.11 = (bf16[2,512,128]{2,1,0:T(8,128)(2,1)S(1)}, bf16[2,512,128]{2,1,0:T(8,128)(2,1)S(1)}, u32[]{:S(2)}, u32[]{:S(2)}) collective-permute-start(bf16[2,512,128]{2,1,0:T(8,128)(2,1)S(1)} %collective-permute-done.10.refs_10_), channel_id=1, source_target_pairs={{0,8},{1,121},{8,16},{9,1},{16,24},{17,9},{24,32},{25,17},{32,40},... | collective-permute-start | bytes 786440 | tf_op jit(solution)/shard_map/ppermute | solution.py:181
  49.1 9.6 %collective-permute-start.5 = (bf16[2,512,128]{2,1,0:T(8,128)(2,1)S(1)}, bf16[2,512,128]{2,1,0:T(8,128)(2,1)}, u32[]{:S(2)}, u32[]{:S(2)}) collective-permute-start(bf16[2,512,128]{2,1,0:T(8,128)(2,1)S(1)} %collective-permute-done.4.refs_4_), channel_id=1, source_target_pairs={{0,8},{1,121},{8,16},{9,1},{16,24},{17,9},{24,32},{25,17},{32,40},... | collective-permute-start | bytes 786440 | tf_op jit(solution)/shard_map/ppermute | solution.py:180
  54.4 9.6 %collective-permute-start.12 = (bf16[2,512,128]{2,1,0:T(8,128)(2,1)S(1)}, bf16[2,512,128]{2,1,0:T(8,128)(2,1)}, u32[]{:S(2)}, u32[]{:S(2)}) collective-permute-start(bf16[2,512,128]{2,1,0:T(8,128)(2,1)S(1)} %collective-permute-done.11.refs_11_), channel_id=1, source_target_pairs={{0,8},{1,121},{8,16},{9,1},{16,24},{17,9},{24,32},{25,17},{32,40},... | collective-permute-start | bytes 786440 | tf_op jit(solution)/shard_map/ppermute | solution.py:181
  58.6 11.8 %collective-permute-start.6 = (bf16[2,512,128]{2,1,0:T(8,128)(2,1)}, bf16[2,512,128]{2,1,0:T(8,128)(2,1)}, u32[]{:S(2)}, u32[]{:S(2)}) collective-permute-start(bf16[2,512,128]{2,1,0:T(8,128)(2,1)} %collective-permute-done.5.refs_5_), channel_id=1, source_target_pairs={{0,8},{1,121},{8,16},{9,1},{16,24},{17,9},{24,32},{25,17},{32,40},... | collective-permute-start | bytes 786440 | tf_op jit(solution)/shard_map/ppermute | solution.py:180
  64.0 9.8 %collective-permute-start.13 = (bf16[2,512,128]{2,1,0:T(8,128)(2,1)}, bf16[2,512,128]{2,1,0:T(8,128)(2,1)}, u32[]{:S(2)}, u32[]{:S(2)}) collective-permute-start(bf16[2,512,128]{2,1,0:T(8,128)(2,1)} %collective-permute-done.12.refs_12_), channel_id=1, source_target_pairs={{0,8},{1,121},{8,16},{9,1},{16,24},{17,9},{24,32},{25,17},{32,40},... | collective-permute-start | bytes 786440 | tf_op jit(solution)/shard_map/ppermute | solution.py:181
  78.2 28.8 %collective-permute-start.18 = (bf16[7,2,256,128]{3,2,1,0:T(8,128)(2,1)}, bf16[7,2,256,128]{3,2,1,0:T(8,128)(2,1)S(1)}, u32[]{:S(2)}, u32[]{:S(2)}) collective-permute-start(bf16[7,2,256,128]{3,2,1,0:T(8,128)(2,1)} %products.2.refs_0_), channel_id=1, source_target_pairs={{0,1},{1,0},{2,3},{3,2},{4,5},{5,4},{6,7},{7,6},{8,9},{9,8},{10,11... | collective-permute-start | bytes 2752520 | tf_op jit(solution)/shard_map/ppermute | solution.py:188
  80.3 9.7 %collective-permute-start.14 = (bf16[2,512,128]{2,1,0:T(8,128)(2,1)}, bf16[2,512,128]{2,1,0:T(8,128)(2,1)S(1)}, u32[]{:S(2)}, u32[]{:S(2)}) collective-permute-start(bf16[2,512,128]{2,1,0:T(8,128)(2,1)} %collective-permute-done.6.refs_6_), channel_id=1, source_target_pairs={{0,8},{1,121},{8,16},{9,1},{16,24},{17,9},{24,32},{25,17},{32,40},... | collective-permute-start | bytes 786440 | tf_op jit(solution)/shard_map/ppermute | solution.py:180
  82.2 10.6 %collective-permute-start.16 = (bf16[2,512,128]{2,1,0:T(8,128)(2,1)}, bf16[2,512,128]{2,1,0:T(8,128)(2,1)S(1)}, u32[]{:S(2)}, u32[]{:S(2)}) collective-permute-start(bf16[2,512,128]{2,1,0:T(8,128)(2,1)} %collective-permute-done.13.refs_13_), channel_id=1, source_target_pairs={{0,8},{1,121},{8,16},{9,1},{16,24},{17,9},{24,32},{25,17},{32,40},... | collective-permute-start | bytes 786440 | tf_op jit(solution)/shard_map/ppermute | solution.py:181
  90.0 3.5 %collective-permute-start.15 = (bf16[2,512,128]{2,1,0:T(8,128)(2,1)S(1)}, bf16[2,512,128]{2,1,0:T(8,128)(2,1)S(1)}, u32[]{:S(2)}, u32[]{:S(2)}) collective-permute-start(bf16[2,512,128]{2,1,0:T(8,128)(2,1)S(1)} %collective-permute-done.14.refs_0_), channel_id=1, source_target_pairs={{1,121},{9,1},{17,9},{25,17},{33,25},{41,33},{49,41},{57,49},{65,5... | collective-permute-start | bytes 786440 | tf_op jit(solution)/shard_map/ppermute | solution.py:180
  92.8 0.7 collective-permute-start.17
  97.5 9.5 %collective-permute-start.19 = (bf16[2,2,256,128]{3,2,1,0:T(8,128)(2,1)}, bf16[2,2,256,128]{3,2,1,0:T(8,128)(2,1)S(1)}, u32[]{:S(2)}, u32[]{:S(2)}) collective-permute-start(bf16[2,2,256,128]{3,2,1,0:T(8,128)(2,1)} %products.3.refs_1_), channel_id=1, source_target_pairs={{0,1},{1,0},{2,3},{3,2},{4,5},{5,4},{6,7},{7,6},{8,9},{9,8},{10,11... | collective-permute-start | bytes 786440 | tf_op jit(solution)/shard_map/ppermute | solution.py:190
  105.7 10.7 %collective-permute-start.20 = (bf16[2,512,128]{2,1,0:T(8,128)(2,1)S(1)}, bf16[2,512,128]{2,1,0:T(8,128)(2,1)S(1)}, u32[]{:S(2)}, u32[]{:S(2)}) collective-permute-start(bf16[2,512,128]{2,1,0:T(8,128)(2,1)S(1)} %copy-done.5), channel_id=1, source_target_pairs={{0,0},{2,2},{4,4},{6,6},{8,8},{10,10},{12,12},{14,14},{16,16},{18,... | collective-permute-start | bytes 786440 | tf_op jit(solution)/shard_map/ppermute | solution.py:171
  111.4 34.4 %all-to-all-start.1 = ((bf16[4,2,2,256,128]{4,3,2,1,0:T(8,128)(2,1)}), bf16[4,2,2,256,128]{4,3,2,1,0:T(8,128)(2,1)S(1)}, u32[]{:S(2)}, u32[]{:S(2)}) async-start(bf16[4,2,2,256,128]{4,3,2,1,0:T(8,128)(2,1)} %bitcast.8), calls=%async_computation.1 | async-start | bytes 2097152 | tf_op jit(solution)/shard_map/all_to_all | solution.py:193
  116.4 22.1 %collective-permute-start.21 = (bf16[2,256,128]{2,1,0:T(8,128)(2,1)S(1)}, bf16[2,256,128]{2,1,0:T(8,128)(2,1)S(1)}, u32[]{:S(2)}, u32[]{:S(2)}) collective-permute-start(bf16[2,256,128]{2,1,0:T(8,128)(2,1)S(1)} %get-tuple-element.6), channel_id=1, source_target_pairs={{0,0},{1,16},{2,34},{3,50},{4,68},{5,84},{6,102},{7,118},{8,8},{9,... | collective-permute-start | bytes 393224 | tf_op jit(solution)/shard_map/ppermute | solution.py:175
  121.1 24.0 %collective-permute-start.22 = (bf16[2,256,128]{2,1,0:T(8,128)(2,1)S(1)}, bf16[2,256,128]{2,1,0:T(8,128)(2,1)S(1)}, u32[]{:S(2)}, u32[]{:S(2)}) collective-permute-start(bf16[2,256,128]{2,1,0:T(8,128)(2,1)S(1)} %get-tuple-element.7), channel_id=1, source_target_pairs={{0,8},{1,24},{2,42},{3,58},{4,76},{5,92},{6,110},{7,126},{8,0},{9,... | collective-permute-start | bytes 393224 | tf_op jit(solution)/shard_map/ppermute | solution.py:175
  145.2 0.7 collective-permute-start.23
  (15 other events, 53.5 us)

commit v3 on v1

--- a/solution.py
+++ b/solution.py
@@ -8,6 +8,7 @@
 
 BLK = 128
 NARROW = ("y", "core")
+WIDE = ("block", "place")
 WHOLE = pl.BlockSpec(memory_space=pltpu.VMEM)
 
 
@@ -127,13 +128,16 @@
             def _():
                 for m in range(fronts):
                     site = jnp.dot(g_ref[m].T, low_ref[m], preferred_element_type=jnp.float32)
-                    d_ref[pl.ds(half * 8, 8), m] = site.astype(jnp.bfloat16).reshape(8, 16, halves * cols)
+                    site = site.astype(jnp.bfloat16).reshape(2, 4, 16, halves * cols)
+                    for block in range(2):
+                        for place in range(4):
+                            d_ref[place, 2 * half + block, m] = site[block, place]
 
     return pl.pallas_call(
         body,
         out_shape=(
             jax.ShapeDtypeStruct((fronts, halves * cols, rows), jnp.float32),
-            jax.ShapeDtypeStruct((16, fronts, 16, halves * cols), jnp.bfloat16),
+            jax.ShapeDtypeStruct((4, 4, fronts, 16, halves * cols), jnp.bfloat16),
         ),
         in_specs=[pl.BlockSpec(memory_space=pltpu.SMEM)] + [WHOLE] * (1 + count),
         out_specs=(WHOLE, WHOLE),
@@ -162,12 +166,12 @@
 
 
 def level(boundary, owner, ancestor_cov, gain, pivot_inverse):
-    w = lax.axis_index("wide")
+    w = lax.axis_index(WIDE)
     core = lax.axis_index("core")
     narrow = lax.axis_index("y") * 2 + core
     pos = jnp.stack([w, narrow, core]).astype(jnp.int32)
     swap = [(0, 1), (1, 0)]
-    early = 7
+    early = 8
 
     owns = [gain]
     others = [lax.ppermute(gain, "core", swap)]
@@ -176,15 +180,15 @@
     pieces = []
     for step in range(1, 9):
         pairs = ring_pairs((0, 1) if step < 8 else (1,))
-        owns.append(lax.ppermute(owns[-1], ("wide", "core"), pairs))
-        others.append(lax.ppermute(others[-1], ("wide", "core"), pairs))
+        owns.append(lax.ppermute(owns[-1], (*WIDE, "core"), pairs))
+        others.append(lax.ppermute(others[-1], (*WIDE, "core"), pairs))
         a, b = owns[step], others[step]
         if step == 8:
             a = jnp.where(core == 0, owns[0], a)
             b = jnp.where(core == 0, others[0], b)
         held = jnp.where(near, a, b)
         piece = lax.dynamic_slice_in_dim(held, (w & 1) * rows, rows, 1)
-        pieces.append(lax.ppermute(piece, ("wide", "y", "core"), piece_pairs(step)))
+        pieces.append(lax.ppermute(piece, (*WIDE, "y", "core"), piece_pairs(step)))
         if step == 1:
             arrived = lax.all_to_all(ancestor_cov, NARROW, split_axis=0, concat_axis=0, tiled=True)
             paired = lax.ppermute(arrived, "core", swap)
@@ -199,25 +203,27 @@
     parts = lax.all_to_all(ready, "y", split_axis=0, concat_axis=0, tiled=True)
 
     boundary_cov, site = finish(pos, parts, pieces)
-    sums = lax.all_to_all(site, "wide", split_axis=0, concat_axis=0, tiled=True)
+    sums = lax.all_to_all(site, "place", split_axis=0, concat_axis=0, tiled=True)
+    sums = jnp.sum(sums.astype(jnp.float32), axis=0).astype(jnp.bfloat16)
+    sums = lax.all_to_all(sums, "block", split_axis=0, concat_axis=0, tiled=True)
     reduced = jnp.sum(sums.astype(jnp.float32), axis=0)
     diag_cov = pivot_inverse - jnp.swapaxes(reduced, 1, 2)
     return boundary_cov, diag_cov
 
 
 def solution(mesh):
-    fine = Mesh(mesh.devices.reshape(4, 16, 4, 2), ("front", "wide", "y", "core"))
+    fine = Mesh(mesh.devices.reshape(4, 4, 4, 4, 2), ("front", *WIDE, "y", "core"))
     placed = (
         P("front", None),
         P(),
-        P(NARROW, None, "wide"),
-        P("front", NARROW, "wide"),
-        P("front", NARROW, "wide"),
+        P(NARROW, None, WIDE),
+        P("front", NARROW, WIDE),
+        P("front", NARROW, WIDE),
     )
     return jax.shard_map(
         level,
         mesh=fine,
         in_specs=placed,
-        out_specs=(P("front", NARROW, "wide"), P("front", NARROW, "wide")),
+        out_specs=(P("front", NARROW, WIDE), P("front", NARROW, WIDE)),
         check_vma=False,
     )

time: 177 us -> 186 us (1.051)
  the two profiles are of different devices: /device:TPU:4 before, /device:TPU:6 now
where the time goes in v3:
time: 186 us; the launch traced here: 185 us
  starting transfers between devices  73.9 us (40%)
  waiting for transfers between devices  46.1 us (25%)
  blocking collectives  36.6 us (20%)
  Pallas kernels  16.1 us (9%)
  local copies, waits for them, and re-layouts  6.57 us (4%)
  other arithmetic  4.61 us (2%)
    ppermute x8, waiting for transfers between devices, level(): owns.append(lax.ppermute(owns[-1], (*WIDE, 'core'), pairs))  27.7 us
    all_to_all x1, blocking collectives, level(): lax.all_to_all(sums, 'block', split_axis=0, concat_axis=0, tiled=True)  24.4 us
    ppermute x8, starting transfers between devices, level(): pieces.append(lax.ppermute(piece, (*WIDE, 'y', 'core'), piece_pairs(step)))  17 us
    ppermute x8, starting transfers between devices, level(): others.append(lax.ppermute(others[-1], (*WIDE, 'core'), pairs))  16 us
    ppermute x8, starting transfers between devices, level(): owns.append(lax.ppermute(owns[-1], (*WIDE, 'core'), pairs))  16 us
    all_to_all x1, blocking collectives, level(): lax.all_to_all(site, 'place', split_axis=0, concat_axis=0, tiled=True)  12.2 us
    ppermute x8, waiting for transfers between devices, level(): others.append(lax.ppermute(others[-1], (*WIDE, 'core'), pairs))  11.9 us
    ppermute x1, starting transfers between devices, level(): theirs.append(lax.ppermute(mine[1], 'core', swap))  10.5 us
  transfers between devices with their start and end apart: 30, of which 15 were waited for; matrix products, arithmetic and copies ran while one was open for 2% of the time, Pallas kernels for 4%

profile of v3, /device:TPU:6, one launch (start us, length us, event | category | flops | bytes accessed | tf_op | source)
XLA Modules:
  0.0 185.1 jit_solution(17915780245553923365)
XLA Ops:
  0.6 2.1 %collective-permute-start.8 = (bf16[2,512,128]{2,1,0:T(8,128)(2,1)}, bf16[2,512,128]{2,1,0:T(8,128)(2,1)S(1)}, u32[]{:S(2)}, u32[]{:S(2)}) collective-permute-start(bf16[2,512,128]{2,1,0:T(8,128)(2,1)} %refs_0_.1), channel_id=1, source_target_pairs={{0,1},{1,0},{2,3},{3,2},{4,5},{5,4},{6,7},{7,6},{8,9},{9,8},{10,11... | collective-permute-start | bytes 786440 | tf_op jit(solution)/shard_map/ppermute | solution.py:177
  2.7 4.6 %all-to-all-start = ((bf16[8,128,512]{2,1,0:T(8,128)(2,1)}), bf16[8,128,512]{2,1,0:T(8,128)(2,1)S(1)}, u32[]{:S(2)}, u32[]{:S(2)}) async-start(bf16[8,128,512]{2,1,0:T(8,128)(2,1)} %param.7), calls=%async_computation | async-start | bytes 2097152 | tf_op jit(solution)/shard_map/all_to_all | solution.py:193
  7.3 3.8 %collective-permute-start.1 = (bf16[2,512,128]{2,1,0:T(8,128)(2,1)S(1)}, bf16[2,512,128]{2,1,0:T(8,128)(2,1)S(1)}, u32[]{:S(2)}, u32[]{:S(2)}) collective-permute-start(bf16[2,512,128]{2,1,0:T(8,128)(2,1)S(1)} %copy-done.22), channel_id=1, source_target_pairs={{0,8},{1,121},{8,16},{9,1},{16,24},{17,9},{24,32},{25,17},{32,40},... | collective-permute-start | bytes 786440 | tf_op jit(solution)/shard_map/ppermute | solution.py:183
  11.1 3.8 %collective-permute-start.9 = (bf16[2,512,128]{2,1,0:T(8,128)(2,1)S(1)}, bf16[2,512,128]{2,1,0:T(8,128)(2,1)S(1)}, u32[]{:S(2)}, u32[]{:S(2)}) collective-permute-start(bf16[2,512,128]{2,1,0:T(8,128)(2,1)S(1)} %collective-permute-done.8.refs_8_), channel_id=1, source_target_pairs={{0,8},{1,121},{8,16},{9,1},{16,24},{17,9},{24,32},{25,17},{32,40},... | collective-permute-start | bytes 786440 | tf_op jit(solution)/shard_map/ppermute | solution.py:184
  15.0 8.1 %collective-permute-done.1.refs_1_ = bf16[2,512,128]{2,1,0:T(8,128)(2,1)S(1)} collective-permute-done((bf16[2,512,128]{2,1,0:T(8,128)(2,1)S(1)}, bf16[2,512,128]{2,1,0:T(8,128)(2,1)S(1)}, u32[]{:S(2)}, u32[]{:S(2)}) %collective-permute-start.1) | collective-permute-done | bytes 262176 | tf_op jit(solution)/shard_map/ppermute | solution.py:183
  27.8 4.7 %collective-permute-done.2.refs_2_ = bf16[2,512,128]{2,1,0:T(8,128)(2,1)S(1)} collective-permute-done((bf16[2,512,128]{2,1,0:T(8,128)(2,1)S(1)}, bf16[2,512,128]{2,1,0:T(8,128)(2,1)S(1)}, u32[]{:S(2)}, u32[]{:S(2)}) %collective-permute-start.2) | collective-permute-done | bytes 262176 | tf_op jit(solution)/shard_map/ppermute | solution.py:183
  37.4 4.6 %collective-permute-done.3.refs_3_ = bf16[2,512,128]{2,1,0:T(8,128)(2,1)S(1)} collective-permute-done((bf16[2,512,128]{2,1,0:T(8,128)(2,1)S(1)}, bf16[2,512,128]{2,1,0:T(8,128)(2,1)S(1)}, u32[]{:S(2)}, u32[]{:S(2)}) %collective-permute-start.3) | collective-permute-done | bytes 262176 | tf_op jit(solution)/shard_map/ppermute | solution.py:183
  43.9 2.2 %collective-permute-start = (bf16[8,128,512]{2,1,0:T(8,128)(2,1)S(1)}, bf16[8,128,512]{2,1,0:T(8,128)(2,1)S(1)}, u32[]{:S(2)}, u32[]{:S(2)}) collective-permute-start(bf16[8,128,512]{2,1,0:T(8,128)(2,1)S(1)} %all-to-all-done.own_ref), channel_id=1, source_target_pairs={{0,1},{1,0},{2,3},{3,2},{4,5},{5,4},{6,7},{7,6},{8,9},{9,8},{10,11... | collective-permute-start | bytes 3145736 | tf_op jit(solution)/shard_map/ppermute | solution.py:194
  46.1 1.9 %collective-permute-start.12 = (bf16[2,512,128]{2,1,0:T(8,128)(2,1)S(1)}, bf16[2,512,128]{2,1,0:T(8,128)(2,1)S(1)}, u32[]{:S(2)}, u32[]{:S(2)}) collective-permute-start(bf16[2,512,128]{2,1,0:T(8,128)(2,1)S(1)} %collective-permute-done.11.refs_11_), channel_id=1, source_target_pairs={{0,8},{1,121},{8,16},{9,1},{16,24},{17,9},{24,32},{25,17},{32,40},... | collective-permute-start | bytes 786440 | tf_op jit(solution)/shard_map/ppermute | solution.py:184
  48.1 3.4 %collective-permute-done.4.refs_4_ = bf16[2,512,128]{2,1,0:T(8,128)(2,1)S(1)} collective-permute-done((bf16[2,512,128]{2,1,0:T(8,128)(2,1)S(1)}, bf16[2,512,128]{2,1,0:T(8,128)(2,1)S(1)}, u32[]{:S(2)}, u32[]{:S(2)}) %collective-permute-start.4) | collective-permute-done | bytes 262176 | tf_op jit(solution)/shard_map/ppermute | solution.py:183
  53.4 2.2 %collective-permute-done.12.refs_12_ = bf16[2,512,128]{2,1,0:T(8,128)(2,1)S(1)} collective-permute-done((bf16[2,512,128]{2,1,0:T(8,128)(2,1)S(1)}, bf16[2,512,128]{2,1,0:T(8,128)(2,1)S(1)}, u32[]{:S(2)}, u32[]{:S(2)}) %collective-permute-start.12) | collective-permute-done | bytes 262176 | tf_op jit(solution)/shard_map/ppermute | solution.py:184
  57.5 3.4 %collective-permute-done.5.refs_5_ = bf16[2,512,128]{2,1,0:T(8,128)(2,1)S(1)} collective-permute-done((bf16[2,512,128]{2,1,0:T(8,128)(2,1)S(1)}, bf16[2,512,128]{2,1,0:T(8,128)(2,1)S(1)}, u32[]{:S(2)}, u32[]{:S(2)}) %collective-permute-start.5) | collective-permute-done | bytes 262176 | tf_op jit(solution)/shard_map/ppermute | solution.py:183
  60.9 1.9 %collective-permute-start.6 = (bf16[2,512,128]{2,1,0:T(8,128)(2,1)S(1)}, bf16[2,512,128]{2,1,0:T(8,128)(2,1)}, u32[]{:S(2)}, u32[]{:S(2)}) collective-permute-start(bf16[2,512,128]{2,1,0:T(8,128)(2,1)S(1)} %collective-permute-done.5.refs_5_), channel_id=1, source_target_pairs={{0,8},{1,121},{8,16},{9,1},{16,24},{17,9},{24,32},{25,17},{32,40},... | collective-permute-start | bytes 786440 | tf_op jit(solution)/shard_map/ppermute | solution.py:183
  62.8 2.2 %collective-permute-done.13.refs_13_ = bf16[2,512,128]{2,1,0:T(8,128)(2,1)S(1)} collective-permute-done((bf16[2,512,128]{2,1,0:T(8,128)(2,1)S(1)}, bf16[2,512,128]{2,1,0:T(8,128)(2,1)S(1)}, u32[]{:S(2)}, u32[]{:S(2)}) %collective-permute-start.13) | collective-permute-done | bytes 262176 | tf_op jit(solution)/shard_map/ppermute | solution.py:184
  65.1 1.9 %collective-permute-start.14 = (bf16[2,512,128]{2,1,0:T(8,128)(2,1)S(1)}, bf16[2,512,128]{2,1,0:T(8,128)(2,1)}, u32[]{:S(2)}, u32[]{:S(2)}) collective-permute-start(bf16[2,512,128]{2,1,0:T(8,128)(2,1)S(1)} %collective-permute-done.13.refs_13_), channel_id=1, source_target_pairs={{0,8},{1,121},{8,16},{9,1},{16,24},{17,9},{24,32},{25,17},{32,40},... | collective-permute-start | bytes 786440 | tf_op jit(solution)/shard_map/ppermute | solution.py:184
  67.0 3.5 %collective-permute-done.6.refs_6_ = bf16[2,512,128]{2,1,0:T(8,128)(2,1)} collective-permute-done((bf16[2,512,128]{2,1,0:T(8,128)(2,1)S(1)}, bf16[2,512,128]{2,1,0:T(8,128)(2,1)}, u32[]{:S(2)}, u32[]{:S(2)}) %collective-permute-start.6) | collective-permute-done | bytes 262176 | tf_op jit(solution)/shard_map/ppermute | solution.py:183
  70.5 1.9 %collective-permute-start.7 = (bf16[2,512,128]{2,1,0:T(8,128)(2,1)}, bf16[2,512,128]{2,1,0:T(8,128)(2,1)}, u32[]{:S(2)}, u32[]{:S(2)}) collective-permute-start(bf16[2,512,128]{2,1,0:T(8,128)(2,1)} %collective-permute-done.6.refs_6_), channel_id=1, source_target_pairs={{0,8},{1,121},{8,16},{9,1},{16,24},{17,9},{24,32},{25,17},{32,40},... | collective-permute-start | bytes 786440 | tf_op jit(solution)/shard_map/ppermute | solution.py:183
  72.4 2.2 %collective-permute-done.14.refs_14_ = bf16[2,512,128]{2,1,0:T(8,128)(2,1)} collective-permute-done((bf16[2,512,128]{2,1,0:T(8,128)(2,1)S(1)}, bf16[2,512,128]{2,1,0:T(8,128)(2,1)}, u32[]{:S(2)}, u32[]{:S(2)}) %collective-permute-start.14) | collective-permute-done | bytes 262176 | tf_op jit(solution)/shard_map/ppermute | solution.py:184
  78.2 2.9 %turned.1.left_ref = bf16[2,256,1024]{2,1,0:T(8,128)(2,1)} custom-call(s32[2,32]{1,0:T(2,128)} %bnd_ref.1, s32[64]{0:T(128)} %owner_ref.1, s32[3]{0:T(128)} %pad_add_fusion.pos_ref, bf16[8,128,512]{2,1,0:T(8,128)(2,1)} %copy-done.1, bf16[8,128,512]{2,1,0:T(8,128)(2,1)} %copy-done.3), custom_call_target="tpu_custom_call" | custom-call | tf_op jit(solution)/shard_map/turned/pallas_call | solution.py:34
  81.1 3.3 %collective-permute-done.15.refs_15_ = bf16[2,512,128]{2,1,0:T(8,128)(2,1)} collective-permute-done((bf16[2,512,128]{2,1,0:T(8,128)(2,1)}, bf16[2,512,128]{2,1,0:T(8,128)(2,1)}, u32[]{:S(2)}, u32[]{:S(2)}) %collective-permute-start.15) | collective-permute-done | bytes 262176 | tf_op jit(solution)/shard_map/ppermute | solution.py:184
  84.4 4.7 %products.2.refs_0_ = bf16[8,2,256,128]{3,2,1,0:T(8,128)(2,1)} custom-call(bf16[2,256,1024]{2,1,0:T(8,128)(2,1)} %turned.1.left_ref, bf16[2,512,128]{2,1,0:T(8,128)(2,1)} %refs_0_.1, bf16[2,512,128]{2,1,0:T(8,128)(2,1)} %copy-done.6, bf16[2,512,128]{2,1,0:T(8,128)(2,1)} %copy-done.14, bf16[2,512,128]{2,1,0:T(8,128)(2,1)} %copy-done.4, ...), custom_call_target="tpu_custom_call" | custom-call | flops 1073741824 | bytes 8388608 | tf_op jit(solution)/shard_map/products/pallas_call | solution.py:61
  93.9 2.4 %products.3.refs_1_ = bf16[1,2,256,128]{3,2,1,0:T(8,128)(2,1)} custom-call(bf16[2,256,1024]{2,1,0:T(8,128)(2,1)} %turned.1.left_ref, bf16[2,512,128]{2,1,0:T(8,128)(2,1)} %copy-done.26, bf16[2,512,128]{2,1,0:T(8,128)(2,1)} %copy-done.28), custom_call_target="tpu_custom_call" | custom-call | flops 134217728 | bytes 1048576 | tf_op jit(solution)/shard_map/products/pallas_call | solution.py:61
  96.3 10.5 %collective-permute-start.19 = (bf16[1,2,256,128]{3,2,1,0:T(8,128)(2,1)}, bf16[1,2,256,128]{3,2,1,0:T(8,128)(2,1)S(1)}, u32[]{:S(2)}, u32[]{:S(2)}) collective-permute-start(bf16[1,2,256,128]{3,2,1,0:T(8,128)(2,1)} %products.3.refs_1_), channel_id=1, source_target_pairs={{0,1},{1,0},{2,3},{3,2},{4,5},{5,4},{6,7},{7,6},{8,9},{9,8},{10,11... | collective-permute-start | bytes 393224 | tf_op jit(solution)/shard_map/ppermute | solution.py:200
  107.0 4.5 %collective-permute-start.20 = (bf16[2,256,128]{2,1,0:T(8,128)(2,1)S(1)}, bf16[2,256,128]{2,1,0:T(8,128)(2,1)S(1)}, u32[]{:S(2)}, u32[]{:S(2)}) collective-permute-start(bf16[2,256,128]{2,1,0:T(8,128)(2,1)S(1)} %dynamic-slice_select_fusion.8), channel_id=1, source_target_pairs={{0,7},{1,0},{8,8},{9,9},{16,16},{17,17},{24,25},{25,26},{34,33},{3... | collective-permute-start | bytes 393224 | tf_op jit(solution)/shard_map/ppermute | solution.py:191
  115.4 2.8 %assemble.1 = bf16[8,2,256,128]{3,2,1,0:T(8,128)(2,1)} custom-call(s32[3]{0:T(128)} %pad_add_fusion.pos_ref, bf16[8,2,256,128]{3,2,1,0:T(8,128)(2,1)} %products.2.refs_0_, bf16[1,2,256,128]{3,2,1,0:T(8,128)(2,1)} %products.3.refs_1_, bf16[8,2,256,128]{3,2,1,0:T(8,128)(2,1)} %copy-done.2, bf16[1,2,256,128]{3,2,1,0:T(8,128)(2,1)} %copy-done.38), custom_call_target="tpu_custom_call" | custom-call | tf_op jit(solution)/shard_map/assemble/pallas_call | solution.py:96
  118.2 3.7 %all-to-all-start.1 = ((bf16[4,2,2,256,128]{4,3,2,1,0:T(8,128)(2,1)}), bf16[4,2,2,256,128]{4,3,2,1,0:T(8,128)(2,1)S(1)}, u32[]{:S(2)}, u32[]{:S(2)}) async-start(bf16[4,2,2,256,128]{4,3,2,1,0:T(8,128)(2,1)} %bitcast.6), calls=%async_computation.1 | async-start | bytes 2097152 | tf_op jit(solution)/shard_map/all_to_all | solution.py:203
  122.0 5.2 %collective-permute-start.22 = (bf16[2,256,128]{2,1,0:T(8,128)(2,1)S(1)}, bf16[2,256,128]{2,1,0:T(8,128)(2,1)S(1)}, u32[]{:S(2)}, u32[]{:S(2)}) collective-permute-start(bf16[2,256,128]{2,1,0:T(8,128)(2,1)S(1)} %dynamic-slice_select_fusion.6), channel_id=1, source_target_pairs={{0,6},{1,1},{8,15},{9,10},{16,23},{17,18},{24,24},{25,27},{34,32},... | collective-permute-start | bytes 393224 | tf_op jit(solution)/shard_map/ppermute | solution.py:191
  137.2 2.8 %collective-permute-done.25.refs_5_ = bf16[2,256,128]{2,1,0:T(8,128)(2,1)S(1)} collective-permute-done((bf16[2,256,128]{2,1,0:T(8,128)(2,1)S(1)}, bf16[2,256,128]{2,1,0:T(8,128)(2,1)S(1)}, u32[]{:S(2)}, u32[]{:S(2)}) %collective-permute-start.25) | collective-permute-done | bytes 131104 | tf_op jit(solution)/shard_map/ppermute | solution.py:191
  140.0 2.2 %collective-permute-done.26.refs_6_ = bf16[2,256,128]{2,1,0:T(8,128)(2,1)S(1)} collective-permute-done((bf16[2,256,128]{2,1,0:T(8,128)(2,1)S(1)}, bf16[2,256,128]{2,1,0:T(8,128)(2,1)S(1)}, u32[]{:S(2)}, u32[]{:S(2)}) %collective-permute-start.26) | collective-permute-done | bytes 131104 | tf_op jit(solution)/shard_map/ppermute | solution.py:191
  144.0 3.2 %finish.1 = (f32[2,256,256]{2,1,0:T(8,128)}, bf16[4,4,2,16,256]{4,3,2,1,0:T(8,128)(2,1)}) custom-call(s32[3]{0:T(128)} %pad_add_fusion.pos_ref, bf16[4,2,2,256,128]{4,3,2,1,0:T(8,128)(2,1)} %copy-done, bf16[2,256,128]{2,1,0:T(8,128)(2,1)} %copy-done.30, bf16[2,256,128]{2,1,0:T(8,128)(2,1)} %copy-done.31, bf16[2,256,128]{2,1,0:T(8,128)(2,1)} %copy-done.32, ...), custom_call_target="tpu_custom_call" | custom-call | tf_op jit(solution)/shard_map/finish/pallas_call | solution.py:136
  147.2 12.2 %all_to_all.20 = bf16[4,4,2,16,256]{4,3,2,1,0:T(8,128)(2,1)S(1)} all-to-all(bf16[4,4,2,16,256]{4,3,2,1,0:T(8,128)(2,1)} %get-tuple-element.5), channel_id=1, replica_groups=mesh['front'=4,'block'=4,'place'=4,'y'=4,'core'=2] {'place'}, dimensions={0} | all-to-all | bytes 524288 | tf_op jit(solution)/shard_map/all_to_all | solution.py:206
  159.4 24.4 %all_to_all.21 = bf16[4,2,16,256]{3,2,1,0:T(8,128)(2,1)S(1)} all-to-all(bf16[4,2,16,256]{3,2,1,0:T(8,128)(2,1)S(1)} %reduce_sum.21), channel_id=1, replica_groups=mesh['front'=4,'block'=4,'place'=4,'y'=4,'core'=2] {'block'}, dimensions={0} | all-to-all | bytes 131072 | tf_op jit(solution)/shard_map/all_to_all | solution.py:208
  (127 shorter events, 40.3 us)
Async XLA Ops:
  0.6 10.5 %collective-permute-start.8 = (bf16[2,512,128]{2,1,0:T(8,128)(2,1)}, bf16[2,512,128]{2,1,0:T(8,128)(2,1)S(1)}, u32[]{:S(2)}, u32[]{:S(2)}) collective-permute-start(bf16[2,512,128]{2,1,0:T(8,128)(2,1)} %refs_0_.1), channel_id=1, source_target_pairs={{0,1},{1,0},{2,3},{3,2},{4,5},{5,4},{6,7},{7,6},{8,9},{9,8},{10,11... | collective-permute-start | bytes 786440 | tf_op jit(solution)/shard_map/ppermute | solution.py:177
  2.7 41.2 %all-to-all-start = ((bf16[8,128,512]{2,1,0:T(8,128)(2,1)}), bf16[8,128,512]{2,1,0:T(8,128)(2,1)S(1)}, u32[]{:S(2)}, u32[]{:S(2)}) async-start(bf16[8,128,512]{2,1,0:T(8,128)(2,1)} %param.7), calls=%async_computation | async-start | bytes 2097152 | tf_op jit(solution)/shard_map/all_to_all | solution.py:193
  7.3 15.7 %collective-permute-start.1 = (bf16[2,512,128]{2,1,0:T(8,128)(2,1)S(1)}, bf16[2,512,128]{2,1,0:T(8,128)(2,1)S(1)}, u32[]{:S(2)}, u32[]{:S(2)}) collective-permute-start(bf16[2,512,128]{2,1,0:T(8,128)(2,1)S(1)} %copy-done.22), channel_id=1, source_target_pairs={{0,8},{1,121},{8,16},{9,1},{16,24},{17,9},{24,32},{25,17},{32,40},... | collective-permute-start | bytes 786440 | tf_op jit(solution)/shard_map/ppermute | solution.py:183
  11.1 14.7 %collective-permute-start.9 = (bf16[2,512,128]{2,1,0:T(8,128)(2,1)S(1)}, bf16[2,512,128]{2,1,0:T(8,128)(2,1)S(1)}, u32[]{:S(2)}, u32[]{:S(2)}) collective-permute-start(bf16[2,512,128]{2,1,0:T(8,128)(2,1)S(1)} %collective-permute-done.8.refs_8_), channel_id=1, source_target_pairs={{0,8},{1,121},{8,16},{9,1},{16,24},{17,9},{24,32},{25,17},{32,40},... | collective-permute-start | bytes 786440 | tf_op jit(solution)/shard_map/ppermute | solution.py:184
  23.0 58.1 %copy-start.6 = (bf16[2,512,128]{2,1,0:T(8,128)(2,1)}, bf16[2,512,128]{2,1,0:T(8,128)(2,1)S(1)}, u32[]{:S(2)}) copy-start(bf16[2,512,128]{2,1,0:T(8,128)(2,1)S(1)} %collective-permute-done.1.refs_1_) | copy-start | bytes 786436
  23.0 9.5 %collective-permute-start.2 = (bf16[2,512,128]{2,1,0:T(8,128)(2,1)S(1)}, bf16[2,512,128]{2,1,0:T(8,128)(2,1)S(1)}, u32[]{:S(2)}, u32[]{:S(2)}) collective-permute-start(bf16[2,512,128]{2,1,0:T(8,128)(2,1)S(1)} %collective-permute-done.1.refs_1_), channel_id=1, source_target_pairs={{0,8},{1,121},{8,16},{9,1},{16,24},{17,9},{24,32},{25,17},{32,40},... | collective-permute-start | bytes 786440 | tf_op jit(solution)/shard_map/ppermute | solution.py:183
  25.9 55.2 %copy-start.12 = (bf16[2,512,128]{2,1,0:T(8,128)(2,1)}, bf16[2,512,128]{2,1,0:T(8,128)(2,1)S(1)}, u32[]{:S(2)}) copy-start(bf16[2,512,128]{2,1,0:T(8,128)(2,1)S(1)} %collective-permute-done.9.refs_9_) | copy-start | bytes 786436
  25.9 9.6 %collective-permute-start.10 = (bf16[2,512,128]{2,1,0:T(8,128)(2,1)S(1)}, bf16[2,512,128]{2,1,0:T(8,128)(2,1)}, u32[]{:S(2)}, u32[]{:S(2)}) collective-permute-start(bf16[2,512,128]{2,1,0:T(8,128)(2,1)S(1)} %collective-permute-done.9.refs_9_), channel_id=1, source_target_pairs={{0,8},{1,121},{8,16},{9,1},{16,24},{17,9},{24,32},{25,17},{32,40},... | collective-permute-start | bytes 786440 | tf_op jit(solution)/shard_map/ppermute | solution.py:184
  32.5 9.5 %collective-permute-start.3 = (bf16[2,512,128]{2,1,0:T(8,128)(2,1)S(1)}, bf16[2,512,128]{2,1,0:T(8,128)(2,1)S(1)}, u32[]{:S(2)}, u32[]{:S(2)}) collective-permute-start(bf16[2,512,128]{2,1,0:T(8,128)(2,1)S(1)} %collective-permute-done.2.refs_2_), channel_id=1, source_target_pairs={{0,8},{1,121},{8,16},{9,1},{16,24},{17,9},{24,32},{25,17},{32,40},... | collective-permute-start | bytes 786440 | tf_op jit(solution)/shard_map/ppermute | solution.py:183
  35.4 10.7 %collective-permute-start.11 = (bf16[2,512,128]{2,1,0:T(8,128)(2,1)}, bf16[2,512,128]{2,1,0:T(8,128)(2,1)S(1)}, u32[]{:S(2)}, u32[]{:S(2)}) collective-permute-start(bf16[2,512,128]{2,1,0:T(8,128)(2,1)} %collective-permute-done.10.refs_10_), channel_id=1, source_target_pairs={{0,8},{1,121},{8,16},{9,1},{16,24},{17,9},{24,32},{25,17},{32,40},... | collective-permute-start | bytes 786440 | tf_op jit(solution)/shard_map/ppermute | solution.py:184
  42.0 9.5 %collective-permute-start.4 = (bf16[2,512,128]{2,1,0:T(8,128)(2,1)S(1)}, bf16[2,512,128]{2,1,0:T(8,128)(2,1)S(1)}, u32[]{:S(2)}, u32[]{:S(2)}) collective-permute-start(bf16[2,512,128]{2,1,0:T(8,128)(2,1)S(1)} %collective-permute-done.3.refs_3_), channel_id=1, source_target_pairs={{0,8},{1,121},{8,16},{9,1},{16,24},{17,9},{24,32},{25,17},{32,40},... | collective-permute-start | bytes 786440 | tf_op jit(solution)/shard_map/ppermute | solution.py:183
  43.9 33.3 %collective-permute-start = (bf16[8,128,512]{2,1,0:T(8,128)(2,1)S(1)}, bf16[8,128,512]{2,1,0:T(8,128)(2,1)S(1)}, u32[]{:S(2)}, u32[]{:S(2)}) collective-permute-start(bf16[8,128,512]{2,1,0:T(8,128)(2,1)S(1)} %all-to-all-done.own_ref), channel_id=1, source_target_pairs={{0,1},{1,0},{2,3},{3,2},{4,5},{5,4},{6,7},{7,6},{8,9},{9,8},{10,11... | collective-permute-start | bytes 3145736 | tf_op jit(solution)/shard_map/ppermute | solution.py:194
  46.1 9.5 %collective-permute-start.12 = (bf16[2,512,128]{2,1,0:T(8,128)(2,1)S(1)}, bf16[2,512,128]{2,1,0:T(8,128)(2,1)S(1)}, u32[]{:S(2)}, u32[]{:S(2)}) collective-permute-start(bf16[2,512,128]{2,1,0:T(8,128)(2,1)S(1)} %collective-permute-done.11.refs_11_), channel_id=1, source_target_pairs={{0,8},{1,121},{8,16},{9,1},{16,24},{17,9},{24,32},{25,17},{32,40},... | collective-permute-start | bytes 786440 | tf_op jit(solution)/shard_map/ppermute | solution.py:184
  51.4 9.5 %collective-permute-start.5 = (bf16[2,512,128]{2,1,0:T(8,128)(2,1)S(1)}, bf16[2,512,128]{2,1,0:T(8,128)(2,1)S(1)}, u32[]{:S(2)}, u32[]{:S(2)}) collective-permute-start(bf16[2,512,128]{2,1,0:T(8,128)(2,1)S(1)} %collective-permute-done.4.refs_4_), channel_id=1, source_target_pairs={{0,8},{1,121},{8,16},{9,1},{16,24},{17,9},{24,32},{25,17},{32,40},... | collective-permute-start | bytes 786440 | tf_op jit(solution)/shard_map/ppermute | solution.py:183
  55.6 9.5 %collective-permute-start.13 = (bf16[2,512,128]{2,1,0:T(8,128)(2,1)S(1)}, bf16[2,512,128]{2,1,0:T(8,128)(2,1)S(1)}, u32[]{:S(2)}, u32[]{:S(2)}) collective-permute-start(bf16[2,512,128]{2,1,0:T(8,128)(2,1)S(1)} %collective-permute-done.12.refs_12_), channel_id=1, source_target_pairs={{0,8},{1,121},{8,16},{9,1},{16,24},{17,9},{24,32},{25,17},{32,40},... | collective-permute-start | bytes 786440 | tf_op jit(solution)/shard_map/ppermute | solution.py:184
  60.9 9.6 %collective-permute-start.6 = (bf16[2,512,128]{2,1,0:T(8,128)(2,1)S(1)}, bf16[2,512,128]{2,1,0:T(8,128)(2,1)}, u32[]{:S(2)}, u32[]{:S(2)}) collective-permute-start(bf16[2,512,128]{2,1,0:T(8,128)(2,1)S(1)} %collective-permute-done.5.refs_5_), channel_id=1, source_target_pairs={{0,8},{1,121},{8,16},{9,1},{16,24},{17,9},{24,32},{25,17},{32,40},... | collective-permute-start | bytes 786440 | tf_op jit(solution)/shard_map/ppermute | solution.py:183
  65.1 9.6 %collective-permute-start.14 = (bf16[2,512,128]{2,1,0:T(8,128)(2,1)S(1)}, bf16[2,512,128]{2,1,0:T(8,128)(2,1)}, u32[]{:S(2)}, u32[]{:S(2)}) collective-permute-start(bf16[2,512,128]{2,1,0:T(8,128)(2,1)S(1)} %collective-permute-done.13.refs_13_), channel_id=1, source_target_pairs={{0,8},{1,121},{8,16},{9,1},{16,24},{17,9},{24,32},{25,17},{32,40},... | collective-permute-start | bytes 786440 | tf_op jit(solution)/shard_map/ppermute | solution.py:184
  70.5 10.6 %collective-permute-start.7 = (bf16[2,512,128]{2,1,0:T(8,128)(2,1)}, bf16[2,512,128]{2,1,0:T(8,128)(2,1)}, u32[]{:S(2)}, u32[]{:S(2)}) collective-permute-start(bf16[2,512,128]{2,1,0:T(8,128)(2,1)} %collective-permute-done.6.refs_6_), channel_id=1, source_target_pairs={{0,8},{1,121},{8,16},{9,1},{16,24},{17,9},{24,32},{25,17},{32,40},... | collective-permute-start | bytes 786440 | tf_op jit(solution)/shard_map/ppermute | solution.py:183
  74.7 9.8 %collective-permute-start.15 = (bf16[2,512,128]{2,1,0:T(8,128)(2,1)}, bf16[2,512,128]{2,1,0:T(8,128)(2,1)}, u32[]{:S(2)}, u32[]{:S(2)}) collective-permute-start(bf16[2,512,128]{2,1,0:T(8,128)(2,1)} %collective-permute-done.14.refs_14_), channel_id=1, source_target_pairs={{0,8},{1,121},{8,16},{9,1},{16,24},{17,9},{24,32},{25,17},{32,40},... | collective-permute-start | bytes 786440 | tf_op jit(solution)/shard_map/ppermute | solution.py:184
  89.1 24.6 %collective-permute-start.18 = (bf16[8,2,256,128]{3,2,1,0:T(8,128)(2,1)}, bf16[8,2,256,128]{3,2,1,0:T(8,128)(2,1)S(1)}, u32[]{:S(2)}, u32[]{:S(2)}) collective-permute-start(bf16[8,2,256,128]{3,2,1,0:T(8,128)(2,1)} %products.2.refs_0_), channel_id=1, source_target_pairs={{0,1},{1,0},{2,3},{3,2},{4,5},{5,4},{6,7},{7,6},{8,9},{9,8},{10,11... | collective-permute-start | bytes 3145736 | tf_op jit(solution)/shard_map/ppermute | solution.py:198
  91.1 1.4 collective-permute-start.16
  91.7 0.7 collective-permute-start.17
  96.3 17.4 %collective-permute-start.19 = (bf16[1,2,256,128]{3,2,1,0:T(8,128)(2,1)}, bf16[1,2,256,128]{3,2,1,0:T(8,128)(2,1)S(1)}, u32[]{:S(2)}, u32[]{:S(2)}) collective-permute-start(bf16[1,2,256,128]{3,2,1,0:T(8,128)(2,1)} %products.3.refs_1_), channel_id=1, source_target_pairs={{0,1},{1,0},{2,3},{3,2},{4,5},{5,4},{6,7},{7,6},{8,9},{9,8},{10,11... | collective-permute-start | bytes 393224 | tf_op jit(solution)/shard_map/ppermute | solution.py:200
  107.0 25.5 %collective-permute-start.20 = (bf16[2,256,128]{2,1,0:T(8,128)(2,1)S(1)}, bf16[2,256,128]{2,1,0:T(8,128)(2,1)S(1)}, u32[]{:S(2)}, u32[]{:S(2)}) collective-permute-start(bf16[2,256,128]{2,1,0:T(8,128)(2,1)S(1)} %dynamic-slice_select_fusion.8), channel_id=1, source_target_pairs={{0,7},{1,0},{8,8},{9,9},{16,16},{17,17},{24,25},{25,26},{34,33},{3... | collective-permute-start | bytes 393224 | tf_op jit(solution)/shard_map/ppermute | solution.py:191
  112.4 21.3 %collective-permute-start.21 = (bf16[2,256,128]{2,1,0:T(8,128)(2,1)S(1)}, bf16[2,256,128]{2,1,0:T(8,128)(2,1)S(1)}, u32[]{:S(2)}, u32[]{:S(2)}) collective-permute-start(bf16[2,256,128]{2,1,0:T(8,128)(2,1)S(1)} %dynamic-slice_select_fusion.7), channel_id=1, source_target_pairs={{0,7},{1,1},{8,15},{9,9},{16,16},{17,18},{24,24},{25,26},{34,33},{... | collective-permute-start | bytes 393224 | tf_op jit(solution)/shard_map/ppermute | solution.py:191
  118.2 24.0 %all-to-all-start.1 = ((bf16[4,2,2,256,128]{4,3,2,1,0:T(8,128)(2,1)}), bf16[4,2,2,256,128]{4,3,2,1,0:T(8,128)(2,1)S(1)}, u32[]{:S(2)}, u32[]{:S(2)}) async-start(bf16[4,2,2,256,128]{4,3,2,1,0:T(8,128)(2,1)} %bitcast.6), calls=%async_computation.1 | async-start | bytes 2097152 | tf_op jit(solution)/shard_map/all_to_all | solution.py:203
  122.0 13.1 %collective-permute-start.22 = (bf16[2,256,128]{2,1,0:T(8,128)(2,1)S(1)}, bf16[2,256,128]{2,1,0:T(8,128)(2,1)S(1)}, u32[]{:S(2)}, u32[]{:S(2)}) collective-permute-start(bf16[2,256,128]{2,1,0:T(8,128)(2,1)S(1)} %dynamic-slice_select_fusion.6), channel_id=1, source_target_pairs={{0,6},{1,1},{8,15},{9,10},{16,23},{17,18},{24,24},{25,27},{34,32},... | collective-permute-start | bytes 393224 | tf_op jit(solution)/shard_map/ppermute | solution.py:191
  127.3 8.5 %collective-permute-start.23 = (bf16[2,256,128]{2,1,0:T(8,128)(2,1)S(1)}, bf16[2,256,128]{2,1,0:T(8,128)(2,1)S(1)}, u32[]{:S(2)}, u32[]{:S(2)}) collective-permute-start(bf16[2,256,128]{2,1,0:T(8,128)(2,1)S(1)} %dynamic-slice_select_fusion.5), channel_id=1, source_target_pairs={{0,6},{1,2},{8,14},{9,10},{16,23},{17,19},{24,31},{25,27},{34,32},... | collective-permute-start | bytes 393224 | tf_op jit(solution)/shard_map/ppermute | solution.py:191
  128.7 8.5 %collective-permute-start.24 = (bf16[2,256,128]{2,1,0:T(8,128)(2,1)S(1)}, bf16[2,256,128]{2,1,0:T(8,128)(2,1)S(1)}, u32[]{:S(2)}, u32[]{:S(2)}) collective-permute-start(bf16[2,256,128]{2,1,0:T(8,128)(2,1)S(1)} %dynamic-slice_select_fusion.4), channel_id=1, source_target_pairs={{0,5},{1,2},{8,14},{9,11},{16,22},{17,19},{24,31},{25,28},{34,39},... | collective-permute-start | bytes 393224 | tf_op jit(solution)/shard_map/ppermute | solution.py:191
  132.5 7.6 %collective-permute-start.25 = (bf16[2,256,128]{2,1,0:T(8,128)(2,1)S(1)}, bf16[2,256,128]{2,1,0:T(8,128)(2,1)S(1)}, u32[]{:S(2)}, u32[]{:S(2)}) collective-permute-start(bf16[2,256,128]{2,1,0:T(8,128)(2,1)S(1)} %dynamic-slice_select_fusion.3), channel_id=1, source_target_pairs={{0,5},{1,3},{8,13},{9,11},{16,22},{17,20},{24,30},{25,28},{34,39},... | collective-permute-start | bytes 393224 | tf_op jit(solution)/shard_map/ppermute | solution.py:191
  133.8 8.5 %collective-permute-start.26 = (bf16[2,256,128]{2,1,0:T(8,128)(2,1)S(1)}, bf16[2,256,128]{2,1,0:T(8,128)(2,1)S(1)}, u32[]{:S(2)}, u32[]{:S(2)}) collective-permute-start(bf16[2,256,128]{2,1,0:T(8,128)(2,1)S(1)} %dynamic-slice_select_fusion.2), channel_id=1, source_target_pairs={{0,4},{1,3},{8,13},{9,12},{16,21},{17,20},{24,30},{25,29},{34,38},... | collective-permute-start | bytes 393224 | tf_op jit(solution)/shard_map/ppermute | solution.py:191
  135.1 7.2 %collective-permute-start.27 = (bf16[2,256,128]{2,1,0:T(8,128)(2,1)S(1)}, bf16[2,256,128]{2,1,0:T(8,128)(2,1)S(1)}, u32[]{:S(2)}, u32[]{:S(2)}) collective-permute-start(bf16[2,256,128]{2,1,0:T(8,128)(2,1)S(1)} %fusion), channel_id=1, source_target_pairs={{0,0},{1,4},{8,8},{9,12},{16,17},{17,21},{24,25},{25,29},{34,34},{... | collective-permute-start | bytes 393224 | tf_op jit(solution)/shard_map/ppermute | solution.py:191
  (38 other events, 331.0 us)

commit v4 on v3

--- a/solution.py
+++ b/solution.py
@@ -70,36 +70,41 @@
     )(left, *owns, *others)
 
 
-def assemble(pos, mine, theirs):
-    shape = mine[0].shape[1:]
-
-    def body(pos_ref, *refs):
-        out = refs[-1]
+def assemble(pos, left, mine, theirs, first, second):
+    count, fronts, width, cols = mine.shape
+    rows = first.shape[1]
+
+    def body(pos_ref, left_ref, mine_ref, theirs_ref, first_ref, second_ref, out):
         w, core = pos_ref[0], pos_ref[2]
-        for from_core, parts in ((core, refs[: len(mine)]), (1 - core, refs[len(mine) : -1])):
-            step = 0
-            for ref in parts:
-                for s in range(ref.shape[0]):
-                    to = (w + (2 * from_core - 1) * step) & 15
-                    wanted = ((to >> 1) & 1) == core
-                    if step == 0:
-                        wanted = jnp.logical_and(wanted, from_core == 0)
-                    if step == 8:
-                        wanted = jnp.logical_and(wanted, from_core == 1)
-
-                    @pl.when(wanted)
-                    def _():
-                        out[2 * (to >> 2) + (to & 1)] = ref[s]
-
-                    step += 1
-
-    return pl.pallas_call(
-        body,
-        out_shape=jax.ShapeDtypeStruct((8, *shape), jnp.bfloat16),
-        in_specs=[pl.BlockSpec(memory_space=pltpu.SMEM)] + [WHOLE] * (len(mine) + len(theirs)),
+        for from_core, ref in ((core, mine_ref), (1 - core, theirs_ref)):
+            for step in range(count):
+                to = (w + (2 * from_core - 1) * step) & 15
+                wanted = ((to >> 1) & 1) == core
+                if step == 0:
+                    wanted = jnp.logical_and(wanted, from_core == 0)
+
+                @pl.when(wanted)
+                def _():
+                    out[2 * (to >> 2) + (to & 1)] = ref[step]
+
+        to = (w + 8) & 15
+
+        @pl.when(((to >> 1) & 1) == core)
+        def _():
+            near = pl.ds(pl.multiple_of((1 - core) * rows, rows), rows)
+            far = pl.ds(pl.multiple_of(core * rows, rows), rows)
+            for m in range(fronts):
+                value = jnp.dot(left_ref[m, :, near], first_ref[m], preferred_element_type=jnp.float32)
+                value += jnp.dot(left_ref[m, :, far], second_ref[m], preferred_element_type=jnp.float32)
+                out[2 * (to >> 2) + (to & 1), m] = value.astype(jnp.bfloat16)
+
+    return pl.pallas_call(
+        body,
+        out_shape=jax.ShapeDtypeStruct((8, fronts, width, cols), jnp.bfloat16),
+        in_specs=[pl.BlockSpec(memory_space=pltpu.SMEM)] + [WHOLE] * 5,
         out_specs=WHOLE,
         name="assemble",
-    )(pos, *mine, *theirs)
+    )(pos, left, mine, theirs, first, second)
 
 
 def finish(pos, arrived, pieces):
@@ -128,16 +133,13 @@
             def _():
                 for m in range(fronts):
                     site = jnp.dot(g_ref[m].T, low_ref[m], preferred_element_type=jnp.float32)
-                    site = site.astype(jnp.bfloat16).reshape(2, 4, 16, halves * cols)
-                    for block in range(2):
-                        for place in range(4):
-                            d_ref[place, 2 * half + block, m] = site[block, place]
+                    d_ref[pl.ds(half * 8, 8), m] = site.astype(jnp.bfloat16).reshape(8, 16, halves * cols)
 
     return pl.pallas_call(
         body,
         out_shape=(
             jax.ShapeDtypeStruct((fronts, halves * cols, rows), jnp.float32),
-            jax.ShapeDtypeStruct((4, 4, fronts, 16, halves * cols), jnp.bfloat16),
+            jax.ShapeDtypeStruct((16, fronts, 16, halves * cols), jnp.bfloat16),
         ),
         in_specs=[pl.BlockSpec(memory_space=pltpu.SMEM)] + [WHOLE] * (1 + count),
         out_specs=(WHOLE, WHOLE),
@@ -146,22 +148,25 @@
     )(pos, arrived, *pieces)
 
 
-def ring_pairs(cores):
+def ring_pairs():
     pairs = []
     for i in range(16):
-        if 0 in cores:
-            pairs.append((2 * i, 2 * ((i + 1) % 16)))
-        if 1 in cores:
-            pairs.append((2 * i + 1, 2 * ((i - 1) % 16) + 1))
+        pairs.append((2 * i, 2 * ((i + 1) % 16)))
+        pairs.append((2 * i + 1, 2 * ((i - 1) % 16) + 1))
     return pairs
+
+
+def last_pairs():
+    return [(2 * ((i + 1) % 16) + 1, 2 * i + (i // 2) % 2) for i in range(16)]
 
 
 def piece_pairs(step):
     pairs = []
     for i in range(16):
         down, up = (i - step % 8) % 16, (i + step) % 16
-        pairs.append((8 * i + 2 * (i // 4), 8 * i + down // 2))
-        pairs.append((8 * i + 2 * (i // 4) + 1, 8 * i + up // 2))
+        upper = 1 if step < 8 else (i // 2) % 2
+        pairs.append((8 * i + 2 * (i // 4) + 1 - upper, 8 * i + down // 2))
+        pairs.append((8 * i + 2 * (i // 4) + upper, 8 * i + up // 2))
     return pairs
 
 
@@ -171,7 +176,6 @@
     narrow = lax.axis_index("y") * 2 + core
     pos = jnp.stack([w, narrow, core]).astype(jnp.int32)
     swap = [(0, 1), (1, 0)]
-    early = 8
 
     owns = [gain]
     others = [lax.ppermute(gain, "core", swap)]
@@ -179,33 +183,31 @@
     near = (w >> 1) & 1 == core
     pieces = []
     for step in range(1, 9):
-        pairs = ring_pairs((0, 1) if step < 8 else (1,))
+        pairs = ring_pairs() if step < 8 else last_pairs()
         owns.append(lax.ppermute(owns[-1], (*WIDE, "core"), pairs))
         others.append(lax.ppermute(others[-1], (*WIDE, "core"), pairs))
         a, b = owns[step], others[step]
-        if step == 8:
-            a = jnp.where(core == 0, owns[0], a)
-            b = jnp.where(core == 0, others[0], b)
-        held = jnp.where(near, a, b)
+        if step < 8:
+            held = jnp.where(near, a, b)
+        else:
+            held = jnp.where(near, jnp.where(core == 1, a, b), others[0])
         piece = lax.dynamic_slice_in_dim(held, (w & 1) * rows, rows, 1)
         pieces.append(lax.ppermute(piece, (*WIDE, "y", "core"), piece_pairs(step)))
         if step == 1:
-            arrived = lax.all_to_all(ancestor_cov, NARROW, split_axis=0, concat_axis=0, tiled=True)
+            arrived = lax.all_to_all(
+                ancestor_cov, NARROW, split_axis=0, concat_axis=0, tiled=True
+            )
             paired = lax.ppermute(arrived, "core", swap)
             left = turned(boundary, owner, pos, arrived, paired)
 
-    mine = [products(left, owns[:early], others[:early])]
-    theirs = [lax.ppermute(mine[0], "core", swap)]
-    mine.append(products(left, owns[early:], others[early:]))
-    theirs.append(lax.ppermute(mine[1], "core", swap))
-    ready = assemble(pos, mine, theirs)
+    mine = products(left, owns[:8], others[:8])
+    theirs = lax.ppermute(mine, "core", swap)
+    ready = assemble(pos, left, mine, theirs, owns[8], others[8])
     ready = ready.reshape(4, 2, *ready.shape[1:])
     parts = lax.all_to_all(ready, "y", split_axis=0, concat_axis=0, tiled=True)
 
     boundary_cov, site = finish(pos, parts, pieces)
-    sums = lax.all_to_all(site, "place", split_axis=0, concat_axis=0, tiled=True)
-    sums = jnp.sum(sums.astype(jnp.float32), axis=0).astype(jnp.bfloat16)
-    sums = lax.all_to_all(sums, "block", split_axis=0, concat_axis=0, tiled=True)
+    sums = lax.all_to_all(site, WIDE, split_axis=0, concat_axis=0, tiled=True)
     reduced = jnp.sum(sums.astype(jnp.float32), axis=0)
     diag_cov = pivot_inverse - jnp.swapaxes(reduced, 1, 2)
     return boundary_cov, diag_cov

time: 186 us -> 168 us (0.903)
  the two profiles are of different devices: /device:TPU:6 before, /device:TPU:4 now
where the time goes in v4:
time: 168 us; the launch traced here: 167 us
  starting transfers between devices  68 us (40%)
  waiting for transfers between devices  44.9 us (27%)
  blocking collectives  28.8 us (17%)
  Pallas kernels  14.4 us (9%)
  local copies, waits for them, and re-layouts  5.19 us (3%)
  other arithmetic  4.54 us (3%)
    all_to_all x1, blocking collectives, level(): sums = lax.all_to_all(site, WIDE, split_axis=0, concat_axis=0, tiled=True)  28.8 us
    ppermute x8, waiting for transfers between devices, level(): owns.append(lax.ppermute(owns[-1], (*WIDE, 'core'), pairs))  27.7 us
    ppermute x8, starting transfers between devices, level(): pieces.append(lax.ppermute(piece, (*WIDE, 'y', 'core'), piece_pairs(step)))  19.7 us
    ppermute x8, starting transfers between devices, level(): others.append(lax.ppermute(others[-1], (*WIDE, 'core'), pairs))  16.6 us
    ppermute x8, starting transfers between devices, level(): owns.append(lax.ppermute(owns[-1], (*WIDE, 'core'), pairs))  16.6 us
    ppermute x8, waiting for transfers between devices, level(): others.append(lax.ppermute(others[-1], (*WIDE, 'core'), pairs))  12 us
    ppermute x8, waiting for transfers between devices, level(): pieces.append(lax.ppermute(piece, (*WIDE, 'y', 'core'), piece_pairs(step)))  5.25 us
    unnamed x76, local copies, waits for them, and re-layouts  5.19 us
  transfers between devices with their start and end apart: 29, of which 16 were waited for; matrix products, arithmetic and copies ran while one was open for 2% of the time, Pallas kernels for 4%

profile of v4, /device:TPU:4, one launch (start us, length us, event | category | flops | bytes accessed | tf_op | source)
XLA Modules:
  0.0 167.2 jit_solution(14206171580490343178)
XLA Ops:
  0.6 2.1 %collective-permute-start.8 = (bf16[2,512,128]{2,1,0:T(8,128)(2,1)}, bf16[2,512,128]{2,1,0:T(8,128)(2,1)S(1)}, u32[]{:S(2)}, u32[]{:S(2)}) collective-permute-start(bf16[2,512,128]{2,1,0:T(8,128)(2,1)} %refs_0_.1), channel_id=1, source_target_pairs={{0,1},{1,0},{2,3},{3,2},{4,5},{5,4},{6,7},{7,6},{8,9},{9,8},{10,11... | collective-permute-start | bytes 786440 | tf_op jit(solution)/shard_map/ppermute | solution.py:181
  2.7 4.6 %all-to-all-start = ((bf16[8,128,512]{2,1,0:T(8,128)(2,1)}), bf16[8,128,512]{2,1,0:T(8,128)(2,1)S(1)}, u32[]{:S(2)}, u32[]{:S(2)}) async-start(bf16[8,128,512]{2,1,0:T(8,128)(2,1)} %param.7), calls=%async_computation | async-start | bytes 2097152 | tf_op jit(solution)/shard_map/all_to_all | solution.py:197
  7.3 3.8 %collective-permute-start.1 = (bf16[2,512,128]{2,1,0:T(8,128)(2,1)S(1)}, bf16[2,512,128]{2,1,0:T(8,128)(2,1)S(1)}, u32[]{:S(2)}, u32[]{:S(2)}) collective-permute-start(bf16[2,512,128]{2,1,0:T(8,128)(2,1)S(1)} %copy-done.28), channel_id=1, source_target_pairs={{0,8},{1,121},{8,16},{9,1},{16,24},{17,9},{24,32},{25,17},{32,40},... | collective-permute-start | bytes 786440 | tf_op jit(solution)/shard_map/ppermute | solution.py:187
  11.1 3.8 %collective-permute-start.9 = (bf16[2,512,128]{2,1,0:T(8,128)(2,1)S(1)}, bf16[2,512,128]{2,1,0:T(8,128)(2,1)S(1)}, u32[]{:S(2)}, u32[]{:S(2)}) collective-permute-start(bf16[2,512,128]{2,1,0:T(8,128)(2,1)S(1)} %collective-permute-done.8.refs_8_), channel_id=1, source_target_pairs={{0,8},{1,121},{8,16},{9,1},{16,24},{17,9},{24,32},{25,17},{32,40},... | collective-permute-start | bytes 786440 | tf_op jit(solution)/shard_map/ppermute | solution.py:188
  15.0 8.1 %collective-permute-done.1.refs_1_ = bf16[2,512,128]{2,1,0:T(8,128)(2,1)S(1)} collective-permute-done((bf16[2,512,128]{2,1,0:T(8,128)(2,1)S(1)}, bf16[2,512,128]{2,1,0:T(8,128)(2,1)S(1)}, u32[]{:S(2)}, u32[]{:S(2)}) %collective-permute-start.1) | collective-permute-done | bytes 262176 | tf_op jit(solution)/shard_map/ppermute | solution.py:187
  25.9 1.9 %collective-permute-start.10 = (bf16[2,512,128]{2,1,0:T(8,128)(2,1)S(1)}, bf16[2,512,128]{2,1,0:T(8,128)(2,1)}, u32[]{:S(2)}, u32[]{:S(2)}) collective-permute-start(bf16[2,512,128]{2,1,0:T(8,128)(2,1)S(1)} %collective-permute-done.9.refs_9_), channel_id=1, source_target_pairs={{0,8},{1,121},{8,16},{9,1},{16,24},{17,9},{24,32},{25,17},{32,40},... | collective-permute-start | bytes 786440 | tf_op jit(solution)/shard_map/ppermute | solution.py:188
  27.8 4.7 %collective-permute-done.2.refs_2_ = bf16[2,512,128]{2,1,0:T(8,128)(2,1)S(1)} collective-permute-done((bf16[2,512,128]{2,1,0:T(8,128)(2,1)S(1)}, bf16[2,512,128]{2,1,0:T(8,128)(2,1)S(1)}, u32[]{:S(2)}, u32[]{:S(2)}) %collective-permute-start.2) | collective-permute-done | bytes 262176 | tf_op jit(solution)/shard_map/ppermute | solution.py:187
  37.3 4.6 %collective-permute-done.3.refs_3_ = bf16[2,512,128]{2,1,0:T(8,128)(2,1)S(1)} collective-permute-done((bf16[2,512,128]{2,1,0:T(8,128)(2,1)S(1)}, bf16[2,512,128]{2,1,0:T(8,128)(2,1)S(1)}, u32[]{:S(2)}, u32[]{:S(2)}) %collective-permute-start.3) | collective-permute-done | bytes 262176 | tf_op jit(solution)/shard_map/ppermute | solution.py:187
  43.9 2.2 %collective-permute-start = (bf16[8,128,512]{2,1,0:T(8,128)(2,1)S(1)}, bf16[8,128,512]{2,1,0:T(8,128)(2,1)S(1)}, u32[]{:S(2)}, u32[]{:S(2)}) collective-permute-start(bf16[8,128,512]{2,1,0:T(8,128)(2,1)S(1)} %all-to-all-done.own_ref), channel_id=1, source_target_pairs={{0,1},{1,0},{2,3},{3,2},{4,5},{5,4},{6,7},{7,6},{8,9},{9,8},{10,11... | collective-permute-start | bytes 3145736 | tf_op jit(solution)/shard_map/ppermute | solution.py:200
  46.1 1.9 %collective-permute-start.12 = (bf16[2,512,128]{2,1,0:T(8,128)(2,1)S(1)}, bf16[2,512,128]{2,1,0:T(8,128)(2,1)S(1)}, u32[]{:S(2)}, u32[]{:S(2)}) collective-permute-start(bf16[2,512,128]{2,1,0:T(8,128)(2,1)S(1)} %collective-permute-done.11.refs_11_), channel_id=1, source_target_pairs={{0,8},{1,121},{8,16},{9,1},{16,24},{17,9},{24,32},{25,17},{32,40},... | collective-permute-start | bytes 786440 | tf_op jit(solution)/shard_map/ppermute | solution.py:188
  48.1 3.4 %collective-permute-done.4.refs_4_ = bf16[2,512,128]{2,1,0:T(8,128)(2,1)S(1)} collective-permute-done((bf16[2,512,128]{2,1,0:T(8,128)(2,1)S(1)}, bf16[2,512,128]{2,1,0:T(8,128)(2,1)S(1)}, u32[]{:S(2)}, u32[]{:S(2)}) %collective-permute-start.4) | collective-permute-done | bytes 262176 | tf_op jit(solution)/shard_map/ppermute | solution.py:187
  53.4 2.3 %collective-permute-done.12.refs_12_ = bf16[2,512,128]{2,1,0:T(8,128)(2,1)S(1)} collective-permute-done((bf16[2,512,128]{2,1,0:T(8,128)(2,1)S(1)}, bf16[2,512,128]{2,1,0:T(8,128)(2,1)S(1)}, u32[]{:S(2)}, u32[]{:S(2)}) %collective-permute-start.12) | collective-permute-done | bytes 262176 | tf_op jit(solution)/shard_map/ppermute | solution.py:188
  57.5 3.4 %collective-permute-done.5.refs_5_ = bf16[2,512,128]{2,1,0:T(8,128)(2,1)S(1)} collective-permute-done((bf16[2,512,128]{2,1,0:T(8,128)(2,1)S(1)}, bf16[2,512,128]{2,1,0:T(8,128)(2,1)S(1)}, u32[]{:S(2)}, u32[]{:S(2)}) %collective-permute-start.5) | collective-permute-done | bytes 262176 | tf_op jit(solution)/shard_map/ppermute | solution.py:187
  60.9 1.9 %collective-permute-start.6 = (bf16[2,512,128]{2,1,0:T(8,128)(2,1)S(1)}, bf16[2,512,128]{2,1,0:T(8,128)(2,1)}, u32[]{:S(2)}, u32[]{:S(2)}) collective-permute-start(bf16[2,512,128]{2,1,0:T(8,128)(2,1)S(1)} %collective-permute-done.5.refs_5_), channel_id=1, source_target_pairs={{0,8},{1,121},{8,16},{9,1},{16,24},{17,9},{24,32},{25,17},{32,40},... | collective-permute-start | bytes 786440 | tf_op jit(solution)/shard_map/ppermute | solution.py:187
  62.8 2.3 %collective-permute-done.13.refs_13_ = bf16[2,512,128]{2,1,0:T(8,128)(2,1)S(1)} collective-permute-done((bf16[2,512,128]{2,1,0:T(8,128)(2,1)S(1)}, bf16[2,512,128]{2,1,0:T(8,128)(2,1)S(1)}, u32[]{:S(2)}, u32[]{:S(2)}) %collective-permute-start.13) | collective-permute-done | bytes 262176 | tf_op jit(solution)/shard_map/ppermute | solution.py:188
  65.1 1.9 %collective-permute-start.14 = (bf16[2,512,128]{2,1,0:T(8,128)(2,1)S(1)}, bf16[2,512,128]{2,1,0:T(8,128)(2,1)}, u32[]{:S(2)}, u32[]{:S(2)}) collective-permute-start(bf16[2,512,128]{2,1,0:T(8,128)(2,1)S(1)} %collective-permute-done.13.refs_13_), channel_id=1, source_target_pairs={{0,8},{1,121},{8,16},{9,1},{16,24},{17,9},{24,32},{25,17},{32,40},... | collective-permute-start | bytes 786440 | tf_op jit(solution)/shard_map/ppermute | solution.py:188
  67.0 3.5 %collective-permute-done.6.refs_6_ = bf16[2,512,128]{2,1,0:T(8,128)(2,1)} collective-permute-done((bf16[2,512,128]{2,1,0:T(8,128)(2,1)S(1)}, bf16[2,512,128]{2,1,0:T(8,128)(2,1)}, u32[]{:S(2)}, u32[]{:S(2)}) %collective-permute-start.6) | collective-permute-done | bytes 262176 | tf_op jit(solution)/shard_map/ppermute | solution.py:187
  70.5 1.9 %collective-permute-start.7 = (bf16[2,512,128]{2,1,0:T(8,128)(2,1)}, bf16[2,512,128]{2,1,0:T(8,128)(2,1)}, u32[]{:S(2)}, u32[]{:S(2)}) collective-permute-start(bf16[2,512,128]{2,1,0:T(8,128)(2,1)} %collective-permute-done.6.refs_6_), channel_id=1, source_target_pairs={{0,8},{1,121},{8,16},{9,1},{16,24},{17,9},{24,32},{25,17},{32,40},... | collective-permute-start | bytes 786440 | tf_op jit(solution)/shard_map/ppermute | solution.py:187
  72.4 2.3 %collective-permute-done.14.refs_14_ = bf16[2,512,128]{2,1,0:T(8,128)(2,1)} collective-permute-done((bf16[2,512,128]{2,1,0:T(8,128)(2,1)S(1)}, bf16[2,512,128]{2,1,0:T(8,128)(2,1)}, u32[]{:S(2)}, u32[]{:S(2)}) %collective-permute-start.14) | collective-permute-done | bytes 262176 | tf_op jit(solution)/shard_map/ppermute | solution.py:188
  74.7 1.9 %collective-permute-start.15 = (bf16[2,512,128]{2,1,0:T(8,128)(2,1)}, bf16[2,512,128]{2,1,0:T(8,128)(2,1)}, u32[]{:S(2)}, u32[]{:S(2)}) collective-permute-start(bf16[2,512,128]{2,1,0:T(8,128)(2,1)} %collective-permute-done.14.refs_14_), channel_id=1, source_target_pairs={{0,8},{1,121},{8,16},{9,1},{16,24},{17,9},{24,32},{25,17},{32,40},... | collective-permute-start | bytes 786440 | tf_op jit(solution)/shard_map/ppermute | solution.py:188
  78.1 2.9 %turned.1.left_ref = bf16[2,256,1024]{2,1,0:T(8,128)(2,1)} custom-call(s32[2,32]{1,0:T(2,128)} %bnd_ref.1, s32[64]{0:T(128)} %owner_ref.1, s32[3]{0:T(128)} %pad_add_fusion.pos_ref, bf16[8,128,512]{2,1,0:T(8,128)(2,1)} %copy-done.1, bf16[8,128,512]{2,1,0:T(8,128)(2,1)} %copy-done.3), custom_call_target="tpu_custom_call" | custom-call | tf_op jit(solution)/shard_map/turned/pallas_call | solution.py:34
  81.1 3.3 %collective-permute-done.15.refs_15_ = bf16[2,512,128]{2,1,0:T(8,128)(2,1)} collective-permute-done((bf16[2,512,128]{2,1,0:T(8,128)(2,1)}, bf16[2,512,128]{2,1,0:T(8,128)(2,1)}, u32[]{:S(2)}, u32[]{:S(2)}) %collective-permute-start.15) | collective-permute-done | bytes 262176 | tf_op jit(solution)/shard_map/ppermute | solution.py:188
  84.4 4.7 %products.1.mine_ref = bf16[8,2,256,128]{3,2,1,0:T(8,128)(2,1)} custom-call(bf16[2,256,1024]{2,1,0:T(8,128)(2,1)} %turned.1.left_ref, bf16[2,512,128]{2,1,0:T(8,128)(2,1)} %refs_0_.1, bf16[2,512,128]{2,1,0:T(8,128)(2,1)} %copy-done.8, bf16[2,512,128]{2,1,0:T(8,128)(2,1)} %copy-done.16, bf16[2,512,128]{2,1,0:T(8,128)(2,1)} %copy-done.6, ...), custom_call_target="tpu_custom_call" | custom-call | flops 1073741824 | bytes 8388608 | tf_op jit(solution)/shard_map/products/pallas_call | solution.py:61
  89.1 2.0 %collective-permute-start.16 = (bf16[8,2,256,128]{3,2,1,0:T(8,128)(2,1)}, bf16[8,2,256,128]{3,2,1,0:T(8,128)(2,1)S(1)}, u32[]{:S(2)}, u32[]{:S(2)}) collective-permute-start(bf16[8,2,256,128]{3,2,1,0:T(8,128)(2,1)} %products.1.mine_ref), channel_id=1, source_target_pairs={{0,1},{1,0},{2,3},{3,2},{4,5},{5,4},{6,7},{7,6},{8,9},{9,8},{10,11... | collective-permute-start | bytes 3145736 | tf_op jit(solution)/shard_map/ppermute | solution.py:204
  93.9 6.0 %collective-permute-start.19 = (bf16[2,256,128]{2,1,0:T(8,128)(2,1)S(1)}, bf16[2,256,128]{2,1,0:T(8,128)(2,1)S(1)}, u32[]{:S(2)}, u32[]{:S(2)}) collective-permute-start(bf16[2,256,128]{2,1,0:T(8,128)(2,1)S(1)} %dynamic-slice_select_fusion.8), channel_id=1, source_target_pairs={{0,7},{1,0},{8,8},{9,9},{16,16},{17,17},{24,25},{25,26},{34,33},{3... | collective-permute-start | bytes 393224 | tf_op jit(solution)/shard_map/ppermute | solution.py:195
  104.0 3.6 %assemble.1 = bf16[8,2,256,128]{3,2,1,0:T(8,128)(2,1)} custom-call(s32[3]{0:T(128)} %pad_add_fusion.pos_ref, bf16[2,256,1024]{2,1,0:T(8,128)(2,1)} %turned.1.left_ref, bf16[8,2,256,128]{3,2,1,0:T(8,128)(2,1)} %products.1.mine_ref, bf16[8,2,256,128]{3,2,1,0:T(8,128)(2,1)} %copy-done.2, bf16[2,512,128]{2,1,0:T(8,128)(2,1)} %copy-done.24, ...), custom_call_target="tpu_custom_call" | custom-call | tf_op jit(solution)/shard_map/assemble/pallas_call | solution.py:101
  107.6 4.3 %all-to-all-start.1 = ((bf16[4,2,2,256,128]{4,3,2,1,0:T(8,128)(2,1)}), bf16[4,2,2,256,128]{4,3,2,1,0:T(8,128)(2,1)S(1)}, u32[]{:S(2)}, u32[]{:S(2)}) async-start(bf16[4,2,2,256,128]{4,3,2,1,0:T(8,128)(2,1)} %bitcast.6), calls=%async_computation.1 | async-start | bytes 2097152 | tf_op jit(solution)/shard_map/all_to_all | solution.py:207
  112.0 5.3 %collective-permute-start.21 = (bf16[2,256,128]{2,1,0:T(8,128)(2,1)S(1)}, bf16[2,256,128]{2,1,0:T(8,128)(2,1)S(1)}, u32[]{:S(2)}, u32[]{:S(2)}) collective-permute-start(bf16[2,256,128]{2,1,0:T(8,128)(2,1)S(1)} %dynamic-slice_select_fusion.6), channel_id=1, source_target_pairs={{0,6},{1,1},{8,15},{9,10},{16,23},{17,18},{24,24},{25,27},{34,32},... | collective-permute-start | bytes 393224 | tf_op jit(solution)/shard_map/ppermute | solution.py:195
  125.0 1.9 %collective-permute-start.26 = (bf16[2,256,128]{2,1,0:T(8,128)(2,1)S(1)}, bf16[2,256,128]{2,1,0:T(8,128)(2,1)S(1)}, u32[]{:S(2)}, u32[]{:S(2)}) collective-permute-start(bf16[2,256,128]{2,1,0:T(8,128)(2,1)S(1)} %dynamic-slice_select_fusion), channel_id=1, source_target_pairs={{1,0},{0,4},{9,8},{8,12},{16,17},{17,21},{24,25},{25,29},{35,34},{... | collective-permute-start | bytes 393224 | tf_op jit(solution)/shard_map/ppermute | solution.py:195
  127.2 2.1 %collective-permute-done.24.refs_5_ = bf16[2,256,128]{2,1,0:T(8,128)(2,1)S(1)} collective-permute-done((bf16[2,256,128]{2,1,0:T(8,128)(2,1)S(1)}, bf16[2,256,128]{2,1,0:T(8,128)(2,1)S(1)}, u32[]{:S(2)}, u32[]{:S(2)}) %collective-permute-start.24) | collective-permute-done | bytes 131104 | tf_op jit(solution)/shard_map/ppermute | solution.py:195
  133.8 3.2 %finish.1 = (f32[2,256,256]{2,1,0:T(8,128)}, bf16[16,2,16,256]{3,2,1,0:T(8,128)(2,1)}) custom-call(s32[3]{0:T(128)} %pad_add_fusion.pos_ref, bf16[4,2,2,256,128]{4,3,2,1,0:T(8,128)(2,1)} %copy-done, bf16[2,256,128]{2,1,0:T(8,128)(2,1)} %copy-done.29, bf16[2,256,128]{2,1,0:T(8,128)(2,1)} %copy-done.30, bf16[2,256,128]{2,1,0:T(8,128)(2,1)} %copy-done.31, ...), custom_call_target="tpu_custom_call" | custom-call | tf_op jit(solution)/shard_map/finish/pallas_call | solution.py:138
  137.0 28.8 %all_to_all.15 = bf16[16,2,16,256]{3,2,1,0:T(8,128)(2,1)S(1)} all-to-all(bf16[16,2,16,256]{3,2,1,0:T(8,128)(2,1)} %get-tuple-element.5), channel_id=1, replica_groups=mesh['front'=4,'block'=4,'place'=4,'y'=4,'core'=2] {'block','place'}, dimensions={0} | all-to-all | bytes 524288 | tf_op jit(solution)/shard_map/all_to_all | solution.py:210
  (118 shorter events, 35.3 us)
Async XLA Ops:
  0.6 10.5 %collective-permute-start.8 = (bf16[2,512,128]{2,1,0:T(8,128)(2,1)}, bf16[2,512,128]{2,1,0:T(8,128)(2,1)S(1)}, u32[]{:S(2)}, u32[]{:S(2)}) collective-permute-start(bf16[2,512,128]{2,1,0:T(8,128)(2,1)} %refs_0_.1), channel_id=1, source_target_pairs={{0,1},{1,0},{2,3},{3,2},{4,5},{5,4},{6,7},{7,6},{8,9},{9,8},{10,11... | collective-permute-start | bytes 786440 | tf_op jit(solution)/shard_map/ppermute | solution.py:181
  2.7 41.2 %all-to-all-start = ((bf16[8,128,512]{2,1,0:T(8,128)(2,1)}), bf16[8,128,512]{2,1,0:T(8,128)(2,1)S(1)}, u32[]{:S(2)}, u32[]{:S(2)}) async-start(bf16[8,128,512]{2,1,0:T(8,128)(2,1)} %param.7), calls=%async_computation | async-start | bytes 2097152 | tf_op jit(solution)/shard_map/all_to_all | solution.py:197
  7.3 15.7 %collective-permute-start.1 = (bf16[2,512,128]{2,1,0:T(8,128)(2,1)S(1)}, bf16[2,512,128]{2,1,0:T(8,128)(2,1)S(1)}, u32[]{:S(2)}, u32[]{:S(2)}) collective-permute-start(bf16[2,512,128]{2,1,0:T(8,128)(2,1)S(1)} %copy-done.28), channel_id=1, source_target_pairs={{0,8},{1,121},{8,16},{9,1},{16,24},{17,9},{24,32},{25,17},{32,40},... | collective-permute-start | bytes 786440 | tf_op jit(solution)/shard_map/ppermute | solution.py:187
  11.1 69.9 %copy-start.4 = (bf16[2,512,128]{2,1,0:T(8,128)(2,1)}, bf16[2,512,128]{2,1,0:T(8,128)(2,1)S(1)}, u32[]{:S(2)}) copy-start(bf16[2,512,128]{2,1,0:T(8,128)(2,1)S(1)} %collective-permute-done.8.refs_8_) | copy-start | bytes 786436
  11.1 14.7 %collective-permute-start.9 = (bf16[2,512,128]{2,1,0:T(8,128)(2,1)S(1)}, bf16[2,512,128]{2,1,0:T(8,128)(2,1)S(1)}, u32[]{:S(2)}, u32[]{:S(2)}) collective-permute-start(bf16[2,512,128]{2,1,0:T(8,128)(2,1)S(1)} %collective-permute-done.8.refs_8_), channel_id=1, source_target_pairs={{0,8},{1,121},{8,16},{9,1},{16,24},{17,9},{24,32},{25,17},{32,40},... | collective-permute-start | bytes 786440 | tf_op jit(solution)/shard_map/ppermute | solution.py:188
  23.0 58.0 %copy-start.8 = (bf16[2,512,128]{2,1,0:T(8,128)(2,1)}, bf16[2,512,128]{2,1,0:T(8,128)(2,1)S(1)}, u32[]{:S(2)}) copy-start(bf16[2,512,128]{2,1,0:T(8,128)(2,1)S(1)} %collective-permute-done.1.refs_1_) | copy-start | bytes 786436
  23.0 9.5 %collective-permute-start.2 = (bf16[2,512,128]{2,1,0:T(8,128)(2,1)S(1)}, bf16[2,512,128]{2,1,0:T(8,128)(2,1)S(1)}, u32[]{:S(2)}, u32[]{:S(2)}) collective-permute-start(bf16[2,512,128]{2,1,0:T(8,128)(2,1)S(1)} %collective-permute-done.1.refs_1_), channel_id=1, source_target_pairs={{0,8},{1,121},{8,16},{9,1},{16,24},{17,9},{24,32},{25,17},{32,40},... | collective-permute-start | bytes 786440 | tf_op jit(solution)/shard_map/ppermute | solution.py:187
  25.9 9.6 %collective-permute-start.10 = (bf16[2,512,128]{2,1,0:T(8,128)(2,1)S(1)}, bf16[2,512,128]{2,1,0:T(8,128)(2,1)}, u32[]{:S(2)}, u32[]{:S(2)}) collective-permute-start(bf16[2,512,128]{2,1,0:T(8,128)(2,1)S(1)} %collective-permute-done.9.refs_9_), channel_id=1, source_target_pairs={{0,8},{1,121},{8,16},{9,1},{16,24},{17,9},{24,32},{25,17},{32,40},... | collective-permute-start | bytes 786440 | tf_op jit(solution)/shard_map/ppermute | solution.py:188
  32.5 9.5 %collective-permute-start.3 = (bf16[2,512,128]{2,1,0:T(8,128)(2,1)S(1)}, bf16[2,512,128]{2,1,0:T(8,128)(2,1)S(1)}, u32[]{:S(2)}, u32[]{:S(2)}) collective-permute-start(bf16[2,512,128]{2,1,0:T(8,128)(2,1)S(1)} %collective-permute-done.2.refs_2_), channel_id=1, source_target_pairs={{0,8},{1,121},{8,16},{9,1},{16,24},{17,9},{24,32},{25,17},{32,40},... | collective-permute-start | bytes 786440 | tf_op jit(solution)/shard_map/ppermute | solution.py:187
  35.4 10.7 %collective-permute-start.11 = (bf16[2,512,128]{2,1,0:T(8,128)(2,1)}, bf16[2,512,128]{2,1,0:T(8,128)(2,1)S(1)}, u32[]{:S(2)}, u32[]{:S(2)}) collective-permute-start(bf16[2,512,128]{2,1,0:T(8,128)(2,1)} %collective-permute-done.10.refs_10_), channel_id=1, source_target_pairs={{0,8},{1,121},{8,16},{9,1},{16,24},{17,9},{24,32},{25,17},{32,40},... | collective-permute-start | bytes 786440 | tf_op jit(solution)/shard_map/ppermute | solution.py:188
  42.0 39.1 %copy-start.6 = (bf16[2,512,128]{2,1,0:T(8,128)(2,1)}, bf16[2,512,128]{2,1,0:T(8,128)(2,1)S(1)}, u32[]{:S(2)}) copy-start(bf16[2,512,128]{2,1,0:T(8,128)(2,1)S(1)} %collective-permute-done.3.refs_3_) | copy-start | bytes 786436
  42.0 9.5 %collective-permute-start.4 = (bf16[2,512,128]{2,1,0:T(8,128)(2,1)S(1)}, bf16[2,512,128]{2,1,0:T(8,128)(2,1)S(1)}, u32[]{:S(2)}, u32[]{:S(2)}) collective-permute-start(bf16[2,512,128]{2,1,0:T(8,128)(2,1)S(1)} %collective-permute-done.3.refs_3_), channel_id=1, source_target_pairs={{0,8},{1,121},{8,16},{9,1},{16,24},{17,9},{24,32},{25,17},{32,40},... | collective-permute-start | bytes 786440 | tf_op jit(solution)/shard_map/ppermute | solution.py:187
  43.9 33.2 %collective-permute-start = (bf16[8,128,512]{2,1,0:T(8,128)(2,1)S(1)}, bf16[8,128,512]{2,1,0:T(8,128)(2,1)S(1)}, u32[]{:S(2)}, u32[]{:S(2)}) collective-permute-start(bf16[8,128,512]{2,1,0:T(8,128)(2,1)S(1)} %all-to-all-done.own_ref), channel_id=1, source_target_pairs={{0,1},{1,0},{2,3},{3,2},{4,5},{5,4},{6,7},{7,6},{8,9},{9,8},{10,11... | collective-permute-start | bytes 3145736 | tf_op jit(solution)/shard_map/ppermute | solution.py:200
  46.1 9.5 %collective-permute-start.12 = (bf16[2,512,128]{2,1,0:T(8,128)(2,1)S(1)}, bf16[2,512,128]{2,1,0:T(8,128)(2,1)S(1)}, u32[]{:S(2)}, u32[]{:S(2)}) collective-permute-start(bf16[2,512,128]{2,1,0:T(8,128)(2,1)S(1)} %collective-permute-done.11.refs_11_), channel_id=1, source_target_pairs={{0,8},{1,121},{8,16},{9,1},{16,24},{17,9},{24,32},{25,17},{32,40},... | collective-permute-start | bytes 786440 | tf_op jit(solution)/shard_map/ppermute | solution.py:188
  51.4 9.5 %collective-permute-start.5 = (bf16[2,512,128]{2,1,0:T(8,128)(2,1)S(1)}, bf16[2,512,128]{2,1,0:T(8,128)(2,1)S(1)}, u32[]{:S(2)}, u32[]{:S(2)}) collective-permute-start(bf16[2,512,128]{2,1,0:T(8,128)(2,1)S(1)} %collective-permute-done.4.refs_4_), channel_id=1, source_target_pairs={{0,8},{1,121},{8,16},{9,1},{16,24},{17,9},{24,32},{25,17},{32,40},... | collective-permute-start | bytes 786440 | tf_op jit(solution)/shard_map/ppermute | solution.py:187
  55.6 9.5 %collective-permute-start.13 = (bf16[2,512,128]{2,1,0:T(8,128)(2,1)S(1)}, bf16[2,512,128]{2,1,0:T(8,128)(2,1)S(1)}, u32[]{:S(2)}, u32[]{:S(2)}) collective-permute-start(bf16[2,512,128]{2,1,0:T(8,128)(2,1)S(1)} %collective-permute-done.12.refs_12_), channel_id=1, source_target_pairs={{0,8},{1,121},{8,16},{9,1},{16,24},{17,9},{24,32},{25,17},{32,40},... | collective-permute-start | bytes 786440 | tf_op jit(solution)/shard_map/ppermute | solution.py:188
  60.9 9.6 %collective-permute-start.6 = (bf16[2,512,128]{2,1,0:T(8,128)(2,1)S(1)}, bf16[2,512,128]{2,1,0:T(8,128)(2,1)}, u32[]{:S(2)}, u32[]{:S(2)}) collective-permute-start(bf16[2,512,128]{2,1,0:T(8,128)(2,1)S(1)} %collective-permute-done.5.refs_5_), channel_id=1, source_target_pairs={{0,8},{1,121},{8,16},{9,1},{16,24},{17,9},{24,32},{25,17},{32,40},... | collective-permute-start | bytes 786440 | tf_op jit(solution)/shard_map/ppermute | solution.py:187
  65.1 9.6 %collective-permute-start.14 = (bf16[2,512,128]{2,1,0:T(8,128)(2,1)S(1)}, bf16[2,512,128]{2,1,0:T(8,128)(2,1)}, u32[]{:S(2)}, u32[]{:S(2)}) collective-permute-start(bf16[2,512,128]{2,1,0:T(8,128)(2,1)S(1)} %collective-permute-done.13.refs_13_), channel_id=1, source_target_pairs={{0,8},{1,121},{8,16},{9,1},{16,24},{17,9},{24,32},{25,17},{32,40},... | collective-permute-start | bytes 786440 | tf_op jit(solution)/shard_map/ppermute | solution.py:188
  70.5 10.6 %collective-permute-start.7 = (bf16[2,512,128]{2,1,0:T(8,128)(2,1)}, bf16[2,512,128]{2,1,0:T(8,128)(2,1)}, u32[]{:S(2)}, u32[]{:S(2)}) collective-permute-start(bf16[2,512,128]{2,1,0:T(8,128)(2,1)} %collective-permute-done.6.refs_6_), channel_id=1, source_target_pairs={{0,8},{1,121},{8,16},{9,1},{16,24},{17,9},{24,32},{25,17},{32,40},... | collective-permute-start | bytes 786440 | tf_op jit(solution)/shard_map/ppermute | solution.py:187
  74.7 9.8 %collective-permute-start.15 = (bf16[2,512,128]{2,1,0:T(8,128)(2,1)}, bf16[2,512,128]{2,1,0:T(8,128)(2,1)}, u32[]{:S(2)}, u32[]{:S(2)}) collective-permute-start(bf16[2,512,128]{2,1,0:T(8,128)(2,1)} %collective-permute-done.14.refs_14_), channel_id=1, source_target_pairs={{0,8},{1,121},{8,16},{9,1},{16,24},{17,9},{24,32},{25,17},{32,40},... | collective-permute-start | bytes 786440 | tf_op jit(solution)/shard_map/ppermute | solution.py:188
  89.1 13.0 %collective-permute-start.16 = (bf16[8,2,256,128]{3,2,1,0:T(8,128)(2,1)}, bf16[8,2,256,128]{3,2,1,0:T(8,128)(2,1)S(1)}, u32[]{:S(2)}, u32[]{:S(2)}) collective-permute-start(bf16[8,2,256,128]{3,2,1,0:T(8,128)(2,1)} %products.1.mine_ref), channel_id=1, source_target_pairs={{0,1},{1,0},{2,3},{3,2},{4,5},{5,4},{6,7},{7,6},{8,9},{9,8},{10,11... | collective-permute-start | bytes 3145736 | tf_op jit(solution)/shard_map/ppermute | solution.py:204
  91.2 11.0 %collective-permute-start.17 = (bf16[2,512,128]{2,1,0:T(8,128)(2,1)}, bf16[2,512,128]{2,1,0:T(8,128)(2,1)S(1)}, u32[]{:S(2)}, u32[]{:S(2)}) collective-permute-start(bf16[2,512,128]{2,1,0:T(8,128)(2,1)} %collective-permute-done.7.refs_7_), channel_id=1, source_target_pairs={{9,0},{17,8},{25,17},{33,25},{41,32},{49,40},{57,49},{65,57},{73,6... | collective-permute-start | bytes 786440 | tf_op jit(solution)/shard_map/ppermute | solution.py:187
  92.5 9.7 %collective-permute-start.18 = (bf16[2,512,128]{2,1,0:T(8,128)(2,1)}, bf16[2,512,128]{2,1,0:T(8,128)(2,1)S(1)}, u32[]{:S(2)}, u32[]{:S(2)}) collective-permute-start(bf16[2,512,128]{2,1,0:T(8,128)(2,1)} %collective-permute-done.15.refs_15_), channel_id=1, source_target_pairs={{9,0},{17,8},{25,17},{33,25},{41,32},{49,40},{57,49},{65,57},{73,6... | collective-permute-start | bytes 786440 | tf_op jit(solution)/shard_map/ppermute | solution.py:188
  93.9 28.4 %collective-permute-start.19 = (bf16[2,256,128]{2,1,0:T(8,128)(2,1)S(1)}, bf16[2,256,128]{2,1,0:T(8,128)(2,1)S(1)}, u32[]{:S(2)}, u32[]{:S(2)}) collective-permute-start(bf16[2,256,128]{2,1,0:T(8,128)(2,1)S(1)} %dynamic-slice_select_fusion.8), channel_id=1, source_target_pairs={{0,7},{1,0},{8,8},{9,9},{16,16},{17,17},{24,25},{25,26},{34,33},{3... | collective-permute-start | bytes 393224 | tf_op jit(solution)/shard_map/ppermute | solution.py:195
  100.8 22.8 %collective-permute-start.20 = (bf16[2,256,128]{2,1,0:T(8,128)(2,1)S(1)}, bf16[2,256,128]{2,1,0:T(8,128)(2,1)S(1)}, u32[]{:S(2)}, u32[]{:S(2)}) collective-permute-start(bf16[2,256,128]{2,1,0:T(8,128)(2,1)S(1)} %dynamic-slice_select_fusion.7), channel_id=1, source_target_pairs={{0,7},{1,1},{8,15},{9,9},{16,16},{17,18},{24,24},{25,26},{34,33},{... | collective-permute-start | bytes 393224 | tf_op jit(solution)/shard_map/ppermute | solution.py:195
  107.6 24.6 %all-to-all-start.1 = ((bf16[4,2,2,256,128]{4,3,2,1,0:T(8,128)(2,1)}), bf16[4,2,2,256,128]{4,3,2,1,0:T(8,128)(2,1)S(1)}, u32[]{:S(2)}, u32[]{:S(2)}) async-start(bf16[4,2,2,256,128]{4,3,2,1,0:T(8,128)(2,1)} %bitcast.6), calls=%async_computation.1 | async-start | bytes 2097152 | tf_op jit(solution)/shard_map/all_to_all | solution.py:207
  112.0 13.0 %collective-permute-start.21 = (bf16[2,256,128]{2,1,0:T(8,128)(2,1)S(1)}, bf16[2,256,128]{2,1,0:T(8,128)(2,1)S(1)}, u32[]{:S(2)}, u32[]{:S(2)}) collective-permute-start(bf16[2,256,128]{2,1,0:T(8,128)(2,1)S(1)} %dynamic-slice_select_fusion.6), channel_id=1, source_target_pairs={{0,6},{1,1},{8,15},{9,10},{16,23},{17,18},{24,24},{25,27},{34,32},... | collective-permute-start | bytes 393224 | tf_op jit(solution)/shard_map/ppermute | solution.py:195
  117.3 9.6 %collective-permute-start.22 = (bf16[2,256,128]{2,1,0:T(8,128)(2,1)S(1)}, bf16[2,256,128]{2,1,0:T(8,128)(2,1)S(1)}, u32[]{:S(2)}, u32[]{:S(2)}) collective-permute-start(bf16[2,256,128]{2,1,0:T(8,128)(2,1)S(1)} %dynamic-slice_select_fusion.5), channel_id=1, source_target_pairs={{0,6},{1,2},{8,14},{9,10},{16,23},{17,19},{24,31},{25,27},{34,32},... | collective-permute-start | bytes 393224 | tf_op jit(solution)/shard_map/ppermute | solution.py:195
  118.7 8.5 %collective-permute-start.23 = (bf16[2,256,128]{2,1,0:T(8,128)(2,1)S(1)}, bf16[2,256,128]{2,1,0:T(8,128)(2,1)S(1)}, u32[]{:S(2)}, u32[]{:S(2)}) collective-permute-start(bf16[2,256,128]{2,1,0:T(8,128)(2,1)S(1)} %dynamic-slice_select_fusion.4), channel_id=1, source_target_pairs={{0,5},{1,2},{8,14},{9,11},{16,22},{17,19},{24,31},{25,28},{34,39},... | collective-permute-start | bytes 393224 | tf_op jit(solution)/shard_map/ppermute | solution.py:195
  122.3 7.0 %collective-permute-start.24 = (bf16[2,256,128]{2,1,0:T(8,128)(2,1)S(1)}, bf16[2,256,128]{2,1,0:T(8,128)(2,1)S(1)}, u32[]{:S(2)}, u32[]{:S(2)}) collective-permute-start(bf16[2,256,128]{2,1,0:T(8,128)(2,1)S(1)} %dynamic-slice_select_fusion.3), channel_id=1, source_target_pairs={{0,5},{1,3},{8,13},{9,11},{16,22},{17,20},{24,30},{25,28},{34,39},... | collective-permute-start | bytes 393224 | tf_op jit(solution)/shard_map/ppermute | solution.py:195
  123.6 7.1 %collective-permute-start.25 = (bf16[2,256,128]{2,1,0:T(8,128)(2,1)S(1)}, bf16[2,256,128]{2,1,0:T(8,128)(2,1)S(1)}, u32[]{:S(2)}, u32[]{:S(2)}) collective-permute-start(bf16[2,256,128]{2,1,0:T(8,128)(2,1)S(1)} %dynamic-slice_select_fusion.2), channel_id=1, source_target_pairs={{0,4},{1,3},{8,13},{9,12},{16,21},{17,20},{24,30},{25,29},{34,38},... | collective-permute-start | bytes 393224 | tf_op jit(solution)/shard_map/ppermute | solution.py:195
  125.0 7.2 %collective-permute-start.26 = (bf16[2,256,128]{2,1,0:T(8,128)(2,1)S(1)}, bf16[2,256,128]{2,1,0:T(8,128)(2,1)S(1)}, u32[]{:S(2)}, u32[]{:S(2)}) collective-permute-start(bf16[2,256,128]{2,1,0:T(8,128)(2,1)S(1)} %dynamic-slice_select_fusion), channel_id=1, source_target_pairs={{1,0},{0,4},{9,8},{8,12},{16,17},{17,21},{24,25},{25,29},{35,34},{... | collective-permute-start | bytes 393224 | tf_op jit(solution)/shard_map/ppermute | solution.py:195
  (35 other events, 273.6 us)
